TPU v7x, 32 devices: a whole 2x2x4 slice. The times are simulated.
32 devices in a mesh: shard: 4 (over z), ctx: 2 (over x), tp: 4 (over y, core).
Axes of the slice: x: 2, y: 2, z: 4, core: 2. Of those that a mesh axis runs over, the one named last changes fastest.
Arguments:
- noised: bfloat16 [4, 4, 64, 64], P('shard', None, ('ctx', 'tp')), may hold values from -6 to 6
- velocity: bfloat16 [4, 4, 64, 64], P('shard', None, ('ctx', 'tp')), may hold values from -6 to 6
- labels: int32 [4], P('shard'), may hold values from 0 to 999
- time_ids: int32 [4], P('shard'), may hold values from 0 to 999
- stem: float32 [3592, 768], P(None, ('shard', 'tp')), may hold values from -0.21875 to 0.21875
- stem_mean: float32 [3592, 768], P(None, ('shard', 'tp')), may hold values from -0.00036621094 to 0.00036621094
- stem_square: float32 [3592, 768], P(None, ('shard', 'tp')), may hold values from 1e-10 to 1e-08
- modulation: float32 [4, 768, 4608], P(None, ('shard', 'tp')), may hold values from -0.875 to 0.875
- modulation_mean: float32 [4, 768, 4608], P(None, ('shard', 'tp')), may hold values from -0.00036621094 to 0.00036621094
- modulation_square: float32 [4, 768, 4608], P(None, ('shard', 'tp')), may hold values from 1e-10 to 1e-08
- attention_in: float32 [4, 3, 768, 768], P(None, None, 'shard', 'tp'), may hold values from -0.21875 to 0.21875
- attention_in_mean: float32 [4, 3, 768, 768], P(None, None, 'shard', 'tp'), may hold values from -0.00036621094 to 0.00036621094
- attention_in_square: float32 [4, 3, 768, 768], P(None, None, 'shard', 'tp'), may hold values from 1e-10 to 1e-08
- attention_out: float32 [4, 768, 768], P(None, 'shard', 'tp'), may hold values from -0.875 to 0.875
- attention_out_mean: float32 [4, 768, 768], P(None, 'shard', 'tp'), may hold values from -0.00036621094 to 0.00036621094
- attention_out_square: float32 [4, 768, 768], P(None, 'shard', 'tp'), may hold values from 1e-10 to 1e-08
- feedforward: float32 [4, 2, 768, 3072], P(None, None, 'shard', 'tp'), may hold values from -0.21875 to 0.21875
- feedforward_mean: float32 [4, 2, 768, 3072], P(None, None, 'shard', 'tp'), may hold values from -0.00036621094 to 0.00036621094
- feedforward_square: float32 [4, 2, 768, 3072], P(None, None, 'shard', 'tp'), may hold values from 1e-10 to 1e-08
Outputs:
- train_loss: float32 [], replicated
- total_norm: float32 [], replicated
- stem_new: float32 [3592, 768], P(None, ('shard', 'tp'))
- stem_mean_new: float32 [3592, 768], P(None, ('shard', 'tp'))
- stem_square_new: float32 [3592, 768], P(None, ('shard', 'tp'))
- stem_copy: bfloat16 [3592, 768], P(None, ('shard', 'tp'))
- modulation_new: float32 [4, 768, 4608], P(None, ('shard', 'tp'))
- modulation_mean_new: float32 [4, 768, 4608], P(None, ('shard', 'tp'))
- modulation_square_new: float32 [4, 768, 4608], P(None, ('shard', 'tp'))
- modulation_copy: bfloat16 [4, 768, 4608], P(None, ('shard', 'tp'))
- attention_in_new: float32 [4, 3, 768, 768], P(None, None, 'shard', 'tp')
- attention_in_mean_new: float32 [4, 3, 768, 768], P(None, None, 'shard', 'tp')
- attention_in_square_new: float32 [4, 3, 768, 768], P(None, None, 'shard', 'tp')
- attention_in_copy: bfloat16 [4, 3, 768, 768], P(None, None, 'shard', 'tp')
- attention_out_new: float32 [4, 768, 768], P(None, 'shard', 'tp')
- attention_out_mean_new: float32 [4, 768, 768], P(None, 'shard', 'tp')
- attention_out_square_new: float32 [4, 768, 768], P(None, 'shard', 'tp')
- attention_out_copy: bfloat16 [4, 768, 768], P(None, 'shard', 'tp')
- feedforward_new: float32 [4, 2, 768, 3072], P(None, None, 'shard', 'tp')
- feedforward_mean_new: float32 [4, 2, 768, 3072], P(None, None, 'shard', 'tp')
- feedforward_square_new: float32 [4, 2, 768, 3072], P(None, None, 'shard', 'tp')
- feedforward_copy: bfloat16 [4, 2, 768, 3072], P(None, None, 'shard', 'tp')
All inputs are finite; a program needn't handle non-finite values.
Results may differ from a plain program's by a relative error of at most 0.019.
The roundings to bfloat16 on the way count: a program that leaves them out, or rounds other values in their place, can miss the bound.
Values may be sent and summed in bfloat16 or wider, within the bound.
A program may use at most 320 MiB of HBM per device.

v0:
```python
import math

import jax
import jax.numpy as jnp
from jax import lax
from jax.sharding import PartitionSpec as P

D = 768
HEAD_DIM = 64
CLASSES = 1000
FREQ = 256
PATCH = 2
STEPS = 1000
LAYERS = 4
PATCHES = 1024
PDIM = 16


norm_eps = 1e-06
clip_level = 0.5
learn_rate = 0.01
beta_first = 0.5
beta_second = 0.5
adam_eps = 1e-08
weight_decay = 0.1
bias_fix = 0.875
highest = lax.Precision.HIGHEST


def layer_norm(values):
    centre = values - jnp.mean(values, -1, keepdims=True)
    spread = jnp.mean(centre * centre, -1, keepdims=True)
    return centre * lax.rsqrt(spread + norm_eps)


def modulate(values, shift_rows, scale_rows):
    return layer_norm(values) * (1.0 + scale_rows) + shift_rows


def gelu_tanh(values):
    return jax.nn.gelu(values, approximate=True)


def patchify(image_in):
    latent_count, channels, height, columns = image_in.shape
    shaped = image_in.reshape(
        latent_count, channels, height // PATCH, PATCH, columns // PATCH, PATCH
    )
    shaped = shaped.transpose(0, 2, 4, 3, 5, 1)
    return shaped.reshape(
        latent_count, height // PATCH * (columns // PATCH), PATCH * PATCH * channels
    )


def positions(first_row, height, columns, model_width):
    quarter = model_width // 4
    omegas = jnp.exp(-math.log(10000.0) * jnp.arange(quarter).astype(jnp.float32) / quarter)
    row_angle = (first_row + jnp.arange(height)).astype(jnp.float32)[:, None] * omegas[None, :]
    col_angle = jnp.arange(columns).astype(jnp.float32)[:, None] * omegas[None, :]
    row_part = jnp.concatenate([jnp.sin(row_angle), jnp.cos(row_angle)], -1)
    col_part = jnp.concatenate([jnp.sin(col_angle), jnp.cos(col_angle)], -1)
    grid_table = jnp.concatenate(
        [
            jnp.broadcast_to(col_part[None], (height, columns, 2 * quarter)),
            jnp.broadcast_to(row_part[:, None], (height, columns, 2 * quarter)),
        ],
        -1,
    )
    return grid_table.reshape(height * columns, model_width)


def time_features(step_ids):
    half_width = FREQ // 2
    frequencies = jnp.exp(
        -math.log(10000.0) * jnp.arange(half_width).astype(jnp.float32) / half_width
    )
    angles = step_ids.astype(jnp.float32)[:, None] * frequencies[None, :]
    return jnp.concatenate([jnp.cos(angles), jnp.sin(angles)], -1)


def split_stem(stem_rows):
    bounds = [CLASSES, FREQ, D, D, D, PDIM, PDIM]
    pieces_out = []
    offset = 0
    for extent in bounds:
        pieces_out.append(stem_rows[offset : offset + extent])
        offset = offset + extent
    return pieces_out


def adam_update(master, first_moment, second_moment, gradient, factor):
    clipped = gradient * factor
    first_new = beta_first * first_moment + (1.0 - beta_first) * clipped
    second_new = beta_second * second_moment + (1.0 - beta_second) * clipped * clipped
    direction = first_new / bias_fix / (jnp.sqrt(second_new / bias_fix) + adam_eps)
    master_new = master - learn_rate * (direction + weight_decay * master)
    return (master_new, first_new, second_new, master_new.astype(jnp.bfloat16))


def spread_rows(values):
    return lax.all_gather(values, "tp", axis=1, tiled=True)


def collect_rows(part_sum):
    return lax.psum_scatter(
        part_sum.astype(jnp.bfloat16), "tp", scatter_dimension=1, tiled=True
    ).astype(jnp.float32)


def spread_grads(values):
    return lax.all_gather(values, "tp", axis=1, tiled=True)


def collect_grads(part_sum):
    return lax.psum_scatter(
        part_sum.astype(jnp.bfloat16), "tp", scatter_dimension=1, tiled=True
    ).astype(jnp.float32)


def global_sums(values):
    return lax.psum(values, ("shard", "ctx", "tp"))


def local(
    noised,
    velocity,
    labels,
    time_ids,
    stem,
    stem_mean,
    stem_square,
    modulation,
    modulation_mean,
    modulation_square,
    attention_in,
    attention_in_mean,
    attention_in_square,
    attention_out,
    attention_out_mean,
    attention_out_square,
    feedforward,
    feedforward_mean,
    feedforward_square,
):
    tensor_ways = lax.axis_size("tp")
    shard_ways = lax.axis_size("shard")
    latent_count = noised.shape[0]
    score_scale = HEAD_DIM ** (-0.5)
    stem_full, modulation_full = (
        lax.all_gather(stem.astype(jnp.bfloat16), ("shard", "tp"), axis=1, tiled=True),
        lax.all_gather(modulation.astype(jnp.bfloat16), ("shard", "tp"), axis=1, tiled=True),
    )
    class_table, time_in, time_out, final_shift, final_scale, patch_in, head_rows = split_stem(
        stem_full
    )
    features = time_features(time_ids).astype(jnp.bfloat16)
    time_pre = jnp.dot(features, time_in, preferred_element_type=jnp.float32)
    time_hidden = jax.nn.silu(time_pre).astype(jnp.bfloat16)
    time_embed = jnp.dot(time_hidden, time_out, preferred_element_type=jnp.float32)
    onehot = (labels[:, None] == jnp.arange(CLASSES)[None, :]).astype(jnp.bfloat16)
    condition = time_embed + jnp.dot(onehot, class_table, preferred_element_type=jnp.float32)
    gated_condition = jax.nn.silu(condition).astype(jnp.bfloat16)
    gated_wide = gated_condition.astype(jnp.float32)
    all_modulation = jnp.einsum(
        "bd,lde->lbe", gated_condition, modulation_full, preferred_element_type=jnp.float32
    )
    pieces = patchify(noised)
    rows_here = noised.shape[2] // PATCH
    first_row = (lax.axis_index("ctx") * tensor_ways + lax.axis_index("tp")) * rows_here
    embedded = jnp.einsum("bpf,fd->bpd", pieces, patch_in, preferred_element_type=jnp.float32)
    hidden = embedded + positions(first_row, rows_here, noised.shape[3] // PATCH, D)[None]
    stored = []
    for layer_at in range(LAYERS):
        weights_in, weights_out, weights_hidden = (
            lax.all_gather(
                attention_in[layer_at].astype(jnp.bfloat16), "shard", axis=1, tiled=True
            ),
            lax.all_gather(
                attention_out[layer_at].astype(jnp.bfloat16), "shard", axis=0, tiled=True
            ),
            lax.all_gather(feedforward[layer_at].astype(jnp.bfloat16), "shard", axis=1, tiled=True),
        )
        layer_modulation = all_modulation[layer_at].reshape(latent_count, 6, 1, D)
        shift_one, scale_one, gate_one, shift_two, scale_two, gate_two = [
            layer_modulation[:, number] for number in range(6)
        ]
        attention_input = hidden
        normed_one = spread_rows(modulate(hidden, shift_one, scale_one).astype(jnp.bfloat16))
        block_rows = normed_one.shape[1]
        heads_here = weights_in.shape[2] // HEAD_DIM
        projected = jnp.einsum(
            "bpd,jde->jbpe", normed_one, weights_in, preferred_element_type=jnp.float32
        )
        query_rows = (projected[0] * score_scale).astype(jnp.bfloat16)
        key_local = projected[1].astype(jnp.bfloat16)
        value_local = projected[2].astype(jnp.bfloat16)
        key_rows, value_rows = (
            lax.all_gather(key_local, "ctx", axis=1, tiled=True),
            lax.all_gather(value_local, "ctx", axis=1, tiled=True),
        )
        query_heads = query_rows.reshape(latent_count, block_rows, heads_here, HEAD_DIM)
        key_heads = key_rows.reshape(latent_count, key_rows.shape[1], heads_here, HEAD_DIM)
        value_heads = value_rows.reshape(latent_count, value_rows.shape[1], heads_here, HEAD_DIM)
        scores = jnp.einsum(
            "bqhe,bkhe->bhqk", query_heads, key_heads, preferred_element_type=jnp.float32
        )
        row_top = jnp.max(scores, -1, keepdims=True)
        exponent = jnp.exp(scores - row_top)
        row_total = jnp.sum(exponent, -1, keepdims=True)
        log_total = row_top + jnp.log(row_total)
        weights_low = (exponent / row_total).astype(jnp.bfloat16)
        mixed_heads = (
            jnp.einsum(
                "bhqk,bkhe->bqhe", weights_low, value_heads, preferred_element_type=jnp.float32
            )
            .astype(jnp.bfloat16)
            .reshape(latent_count, block_rows, -1)
        )
        branch_one = collect_rows(
            jnp.einsum("bpe,de->bpd", mixed_heads, weights_out, preferred_element_type=jnp.float32)
        )
        hidden = hidden + gate_one * branch_one
        feed_input = hidden
        normed_two = spread_rows(modulate(hidden, shift_two, scale_two).astype(jnp.bfloat16))
        hidden_pre = jnp.einsum(
            "bpd,df->bpf", normed_two, weights_hidden[0], preferred_element_type=jnp.float32
        )
        activated = gelu_tanh(hidden_pre).astype(jnp.bfloat16)
        branch_two = collect_rows(
            jnp.einsum(
                "bpf,df->bpd", activated, weights_hidden[1], preferred_element_type=jnp.float32
            )
        )
        hidden = hidden + gate_two * branch_two
        stored.append(
            (
                attention_input,
                normed_one,
                query_heads,
                key_heads,
                value_heads,
                log_total,
                mixed_heads,
                branch_one,
                feed_input,
                normed_two,
                hidden_pre,
                activated,
                branch_two,
                (weights_in, weights_out, weights_hidden),
            )
        )
    end_shift = jnp.dot(gated_condition, final_shift, preferred_element_type=jnp.float32)[
        :, None, :
    ]
    end_scale = jnp.dot(gated_condition, final_scale, preferred_element_type=jnp.float32)[
        :, None, :
    ]
    final_normed = modulate(hidden, end_shift, end_scale).astype(jnp.bfloat16)
    predicted = jnp.einsum(
        "bpd,cd->bpc", final_normed, head_rows, preferred_element_type=jnp.float32
    )
    target_rows = patchify(velocity).astype(jnp.float32)
    weighting = (0.5 + time_ids.astype(jnp.float32) / STEPS)[:, None, None]
    misfit = predicted - target_rows
    loss_scale = 1.0 / (latent_count * shard_ways * PATCHES * PDIM)
    loss_local = jnp.sum(weighting * misfit * misfit) * loss_scale
    train_loss = global_sums(loss_local)
    grad_pred = (2.0 * loss_scale * weighting * misfit).astype(jnp.bfloat16)
    grad_head = jnp.einsum(
        "bpc,bpd->cd", grad_pred, final_normed, preferred_element_type=jnp.float32
    )
    grad_normed = jnp.einsum(
        "bpc,cd->bpd", grad_pred, head_rows, preferred_element_type=jnp.float32
    )
    final_pull = jax.vjp(modulate, hidden, end_shift, end_scale)[1]
    grad_hidden, grad_end_shift, grad_end_scale = final_pull(grad_normed)
    grad_gated = jnp.dot(grad_end_shift[:, 0], final_shift.astype(jnp.float32).T, precision=highest)
    grad_gated = grad_gated + jnp.dot(
        grad_end_scale[:, 0], final_scale.astype(jnp.float32).T, precision=highest
    )
    factors = jnp.array([score_scale, 1.0, 1.0], jnp.float32)
    grads_in = []
    grads_out = []
    grads_hidden = []
    grads_mod = []
    for layer_at in reversed(range(LAYERS)):
        (
            attention_input,
            normed_one,
            query_heads,
            key_heads,
            value_heads,
            log_total,
            mixed_heads,
            branch_one,
            feed_input,
            normed_two,
            hidden_pre,
            activated,
            branch_two,
            weights_saved,
        ) = stored[layer_at]
        weights_in, weights_out, weights_hidden = (
            lax.all_gather(
                attention_in[layer_at].astype(jnp.bfloat16), "shard", axis=1, tiled=True
            ),
            lax.all_gather(
                attention_out[layer_at].astype(jnp.bfloat16), "shard", axis=0, tiled=True
            ),
            lax.all_gather(feedforward[layer_at].astype(jnp.bfloat16), "shard", axis=1, tiled=True),
        )
        layer_modulation = all_modulation[layer_at].reshape(latent_count, 6, 1, D)
        shift_one, scale_one, gate_one, shift_two, scale_two, gate_two = [
            layer_modulation[:, number] for number in range(6)
        ]
        block_rows = normed_one.shape[1]
        heads_here = weights_in.shape[2] // HEAD_DIM
        grad_gate_two = jnp.sum(grad_hidden * branch_two, 1)
        grad_branch_two = spread_grads((gate_two * grad_hidden).astype(jnp.bfloat16))
        grad_down = jnp.einsum(
            "bpd,bpf->df", grad_branch_two, activated, preferred_element_type=jnp.float32
        )
        grad_act = jnp.einsum(
            "bpd,df->bpf", grad_branch_two, weights_hidden[1], preferred_element_type=jnp.float32
        )
        gelu_pull = jax.vjp(gelu_tanh, hidden_pre)[1]
        grad_pre = gelu_pull(grad_act)[0].astype(jnp.bfloat16)
        grad_up = jnp.einsum(
            "bpd,bpf->df", normed_two, grad_pre, preferred_element_type=jnp.float32
        )
        grad_normed_two = collect_grads(
            jnp.einsum(
                "bpf,df->bpd", grad_pre, weights_hidden[0], preferred_element_type=jnp.float32
            )
        )
        modulate_pull = jax.vjp(modulate, feed_input, shift_two, scale_two)[1]
        step_hidden, grad_shift_two, grad_scale_two = modulate_pull(grad_normed_two)
        grad_hidden = grad_hidden + step_hidden
        grad_gate_one = jnp.sum(grad_hidden * branch_one, 1)
        grad_branch_one = spread_grads((gate_one * grad_hidden).astype(jnp.bfloat16))
        grad_out_w = jnp.einsum(
            "bpd,bpe->de", grad_branch_one, mixed_heads, preferred_element_type=jnp.float32
        )
        grad_mixed = (
            jnp.einsum(
                "bpd,de->bpe", grad_branch_one, weights_out, preferred_element_type=jnp.float32
            )
            .astype(jnp.bfloat16)
            .reshape(latent_count, block_rows, heads_here, HEAD_DIM)
        )
        scores = jnp.einsum(
            "bqhe,bkhe->bhqk", query_heads, key_heads, preferred_element_type=jnp.float32
        )
        attention_weights = jnp.exp(scores - log_total)
        weights_low = attention_weights.astype(jnp.bfloat16)
        grad_values_part = jnp.einsum(
            "bhqk,bqhe->bkhe", weights_low, grad_mixed, preferred_element_type=jnp.float32
        )
        grad_probs = jnp.einsum(
            "bqhe,bkhe->bhqk", grad_mixed, value_heads, preferred_element_type=jnp.float32
        )
        inner_sum = jnp.sum(attention_weights * grad_probs, -1, keepdims=True)
        grad_scores = (attention_weights * (grad_probs - inner_sum)).astype(jnp.bfloat16)
        grad_queries = jnp.einsum(
            "bhqk,bkhe->bqhe", grad_scores, key_heads, preferred_element_type=jnp.float32
        ).astype(jnp.bfloat16)
        grad_keys_part = jnp.einsum(
            "bhqk,bqhe->bkhe", grad_scores, query_heads, preferred_element_type=jnp.float32
        )
        grad_keys, grad_values = (
            lax.psum_scatter(
                grad_keys_part.astype(jnp.bfloat16), "ctx", scatter_dimension=1, tiled=True
            ).astype(jnp.float32),
            lax.psum_scatter(
                grad_values_part.astype(jnp.bfloat16), "ctx", scatter_dimension=1, tiled=True
            ).astype(jnp.float32),
        )
        stacked = jnp.stack(
            [
                grad_queries.reshape(latent_count, block_rows, -1),
                grad_keys.astype(jnp.bfloat16).reshape(latent_count, block_rows, -1),
                grad_values.astype(jnp.bfloat16).reshape(latent_count, block_rows, -1),
            ]
        )
        grad_in_w = (
            jnp.einsum("bpd,jbpe->jde", normed_one, stacked, preferred_element_type=jnp.float32)
            * factors[:, None, None]
        )
        grad_rows_part = jnp.einsum(
            "jbpe,jde->jbpd", stacked, weights_in, preferred_element_type=jnp.float32
        )
        grad_normed_one = collect_grads(jnp.sum(grad_rows_part * factors[:, None, None, None], 0))
        modulate_pull = jax.vjp(modulate, attention_input, shift_one, scale_one)[1]
        step_hidden, grad_shift_one, grad_scale_one = modulate_pull(grad_normed_one)
        grad_hidden = grad_hidden + step_hidden
        grad_mod = jnp.concatenate(
            [
                grad_shift_one,
                grad_scale_one,
                grad_gate_one[:, None, :],
                grad_shift_two,
                grad_scale_two,
                grad_gate_two[:, None, :],
            ],
            1,
        ).reshape(latent_count, 6 * D)
        grad_gated = grad_gated + jnp.dot(
            grad_mod, modulation_full[layer_at].astype(jnp.float32).T, precision=highest
        )
        grads_in.insert(0, grad_in_w)
        grads_out.insert(0, grad_out_w)
        grads_hidden.insert(0, jnp.stack([grad_up, grad_down]))
        grads_mod.insert(0, grad_mod)
    grad_embed = grad_hidden.astype(jnp.bfloat16)
    grad_patch = jnp.einsum("bpf,bpd->fd", pieces, grad_embed, preferred_element_type=jnp.float32)
    grad_condition = jax.vjp(jax.nn.silu, condition)[1](grad_gated)[0]
    grad_time_hidden = jnp.dot(grad_condition, time_out.astype(jnp.float32).T, precision=highest)
    grad_time_pre = jax.vjp(jax.nn.silu, time_pre)[1](grad_time_hidden)[0]
    shard_in, shard_out, shard_hidden = (
        lax.psum_scatter(
            jnp.stack(grads_in).astype(jnp.bfloat16), "shard", scatter_dimension=2, tiled=True
        ).astype(jnp.float32),
        lax.psum_scatter(
            jnp.stack(grads_out).astype(jnp.bfloat16), "shard", scatter_dimension=1, tiled=True
        ).astype(jnp.float32),
        lax.psum_scatter(
            jnp.stack(grads_hidden).astype(jnp.bfloat16), "shard", scatter_dimension=2, tiled=True
        ).astype(jnp.float32),
    )
    grad_final_shift = jnp.einsum("bd,be->de", gated_wide, grad_end_shift[:, 0], precision=highest)
    grad_final_scale = jnp.einsum("bd,be->de", gated_wide, grad_end_scale[:, 0], precision=highest)
    grad_modulation = jnp.einsum("bd,lbe->lde", gated_wide, jnp.stack(grads_mod), precision=highest)
    grad_table = jnp.dot(onehot.astype(jnp.float32).T, grad_condition, precision=highest)
    grad_time_out = jnp.dot(time_hidden.astype(jnp.float32).T, grad_condition, precision=highest)
    grad_time_in = jnp.dot(features.astype(jnp.float32).T, grad_time_pre, precision=highest)
    grad_stem = jnp.concatenate(
        [
            grad_table,
            grad_time_in,
            grad_time_out,
            grad_final_shift,
            grad_final_scale,
            grad_patch,
            grad_head,
        ],
        0,
    )
    shard_stem, shard_modulation = (
        lax.psum_scatter(grad_stem, ("shard", "tp"), scatter_dimension=1, tiled=True),
        lax.psum_scatter(grad_modulation, ("shard", "tp"), scatter_dimension=1, tiled=True),
    )
    shard_stem, shard_modulation, shard_in, shard_out, shard_hidden = (
        lax.psum(shard_stem.astype(jnp.bfloat16), "ctx").astype(jnp.float32),
        lax.psum(shard_modulation.astype(jnp.bfloat16), "ctx").astype(jnp.float32),
        lax.psum(shard_in.astype(jnp.bfloat16), "ctx").astype(jnp.float32),
        lax.psum(shard_out.astype(jnp.bfloat16), "ctx").astype(jnp.float32),
        lax.psum(shard_hidden.astype(jnp.bfloat16), "ctx").astype(jnp.float32),
    )
    squares = (
        jnp.sum(shard_stem * shard_stem)
        + jnp.sum(shard_modulation * shard_modulation)
        + jnp.sum(shard_in * shard_in)
        + jnp.sum(shard_out * shard_out)
        + jnp.sum(shard_hidden * shard_hidden)
    )
    squares = jnp.where(lax.axis_index("ctx") == 0, squares, jnp.zeros((), jnp.float32))
    square_total = global_sums(squares)
    total_norm = jnp.sqrt(square_total)
    factor = clip_level / jnp.maximum(total_norm, clip_level)
    stem_out = adam_update(stem, stem_mean, stem_square, shard_stem, factor)
    mod_out = adam_update(modulation, modulation_mean, modulation_square, shard_modulation, factor)
    in_out = adam_update(attention_in, attention_in_mean, attention_in_square, shard_in, factor)
    proj_out = adam_update(
        attention_out, attention_out_mean, attention_out_square, shard_out, factor
    )
    feed_out = adam_update(feedforward, feedforward_mean, feedforward_square, shard_hidden, factor)
    return (
        train_loss,
        total_norm,
        stem_out[0],
        stem_out[1],
        stem_out[2],
        stem_out[3],
        mod_out[0],
        mod_out[1],
        mod_out[2],
        mod_out[3],
        in_out[0],
        in_out[1],
        in_out[2],
        in_out[3],
        proj_out[0],
        proj_out[1],
        proj_out[2],
        proj_out[3],
        feed_out[0],
        feed_out[1],
        feed_out[2],
        feed_out[3],
    )


def solution(mesh):
    placed = (
        P("shard", None, ("ctx", "tp"), None),
        P("shard", None, ("ctx", "tp"), None),
        P("shard"),
        P("shard"),
        P(None, ("shard", "tp")),
        P(None, ("shard", "tp")),
        P(None, ("shard", "tp")),
        P(None, ("shard", "tp"), None),
        P(None, ("shard", "tp"), None),
        P(None, ("shard", "tp"), None),
        P(None, None, "shard", "tp"),
        P(None, None, "shard", "tp"),
        P(None, None, "shard", "tp"),
        P(None, "shard", "tp"),
        P(None, "shard", "tp"),
        P(None, "shard", "tp"),
        P(None, None, "shard", "tp"),
        P(None, None, "shard", "tp"),
        P(None, None, "shard", "tp"),
    )
    return jax.shard_map(
        local,
        mesh=mesh,
        in_specs=placed,
        out_specs=(
            P(),
            P(),
            P(None, ("shard", "tp")),
            P(None, ("shard", "tp")),
            P(None, ("shard", "tp")),
            P(None, ("shard", "tp")),
            P(None, ("shard", "tp"), None),
            P(None, ("shard", "tp"), None),
            P(None, ("shard", "tp"), None),
            P(None, ("shard", "tp"), None),
            P(None, None, "shard", "tp"),
            P(None, None, "shard", "tp"),
            P(None, None, "shard", "tp"),
            P(None, None, "shard", "tp"),
            P(None, "shard", "tp"),
            P(None, "shard", "tp"),
            P(None, "shard", "tp"),
            P(None, "shard", "tp"),
            P(None, None, "shard", "tp"),
            P(None, None, "shard", "tp"),
            P(None, None, "shard", "tp"),
            P(None, None, "shard", "tp"),
        ),
        check_vma=False,
    )
```

profile of v0, /device:TPU:0, one launch (start us, length us, event | category | flops | bytes accessed | tf_op | source)
XLA Modules:
  0.0 2447.8 jit_solution(12812554578233640514)
XLA Ops:
  19.2 47.9 %all-gather.1 = bf16[1,3,768,192]{3,1,0,2:T(4,128)(2,1)S(1)} all-gather(bf16[1,3,192,192]{3,1,0,2:T(4,128)(2,1)S(1)} %get-tuple-element.215), channel_id=3, replica_groups=mesh['shard'=4,'ctx'=2,'tp'=4] {'shard'}, dimensions={2}, use_global_device_ids=true | all-gather | bytes 1105920 | tf_op jit(solution)/shard_map/all_gather | solution.py:175
  68.9 19.7 all-gather.4
  101.7 136.7 %all-gather.30.cloned.1.call-done = bf16[4,768,4608]{2,1,0:T(8,128)(2,1)} async-done(((bf16[4,48,4608]{2,1,0:T(8,128)(2,1)}), bf16[4,768,4608]{2,1,0:T(8,128)(2,1)}) %all-gather.30.cloned.1.call-update) | async-done | bytes 28311568 | tf_op jit(solution)/shard_map/all_gather | solution.py:151
  288.6 19.2 reduce-scatter.34.cloned.1.call-done
  317.3 21.2 all-gather.32.cloned.1.call-done
  343.9 29.4 %all-gather.6 = bf16[1,3,768,192]{3,1,0,2:T(4,128)(2,1)S(1)} all-gather(bf16[1,3,192,192]{3,1,0,2:T(4,128)(2,1)S(1)} %copy-done.94), channel_id=8, replica_groups=mesh['shard'=4,'ctx'=2,'tp'=4] {'shard'}, dimensions={2}, use_global_device_ids=true | all-gather | bytes 1105920 | tf_op jit(solution)/shard_map/all_gather | solution.py:175
  423.6 21.9 reduce-scatter.38.cloned.1.call-done
  455.5 19.1 all-gather.34.cloned.1.call-done
  480.1 29.4 %all-gather.11 = bf16[1,3,768,192]{3,1,0,2:T(4,128)(2,1)S(1)} all-gather(bf16[1,3,192,192]{3,1,0,2:T(4,128)(2,1)S(1)} %copy-done.93), channel_id=13, replica_groups=mesh['shard'=4,'ctx'=2,'tp'=4] {'shard'}, dimensions={2}, use_global_device_ids=true | all-gather | bytes 1105920 | tf_op jit(solution)/shard_map/all_gather | solution.py:175
  560.8 22.1 reduce-scatter.42.cloned.1.call-done
  592.9 19.0 all-gather.36.cloned.1.call-done
  617.4 29.4 %all-gather.16 = bf16[1,3,768,192]{3,1,0,2:T(4,128)(2,1)S(1)} all-gather(bf16[1,3,192,192]{3,1,0,2:T(4,128)(2,1)S(1)} %copy-done.92), channel_id=18, replica_groups=mesh['shard'=4,'ctx'=2,'tp'=4] {'shard'}, dimensions={2}, use_global_device_ids=true | all-gather | bytes 1105920 | tf_op jit(solution)/shard_map/all_gather | solution.py:175
  697.5 22.1 reduce-scatter.46.cloned.1.call-done
  729.1 20.0 all-gather.38.cloned.1.call-done
  758.7 17.8 reduce-scatter.48.cloned.1.call-done
  795.3 23.8 reduce-scatter.50.cloned.1.call-done
  854.6 16.0 reduce-scatter.54.cloned.1.call-done
  874.2 23.3 reduce-scatter.56.cloned.1.call-done
  915.6 23.8 reduce-scatter.58.cloned.1.call-done
  974.5 15.8 reduce-scatter.62.cloned.1.call-done
  993.9 23.3 reduce-scatter.64.cloned.1.call-done
  1035.2 23.8 reduce-scatter.66.cloned.1.call-done
  1094.1 16.0 reduce-scatter.70.cloned.1.call-done
  1113.7 23.3 reduce-scatter.72.cloned.1.call-done
  1155.7 23.8 reduce-scatter.74.cloned.1.call-done
  1215.3 16.0 reduce-scatter.78.cloned.1.call-done
  1332.4 18.3 multiply_bitcast_fusion
  1380.4 108.7 %reduce-scatter.82.cloned.1.call-done = f32[3592,48]{0,1:T(8,128)} async-done(((f32[3592,768]{0,1:T(8,128)}), f32[3592,48]{0,1:T(8,128)}) %reduce-scatter.82.cloned.1.call-update) | async-done | bytes 689680 | tf_op jit(solution)/shard_map/reduce_scatter | solution.py:450
  1490.9 525.8 %reduce-scatter.84.cloned.1.call-done = f32[4,48,4608]{2,1,0:T(8,128)} async-done(((f32[4,768,4608]{2,1,0:T(8,128)}), f32[4,48,4608]{2,1,0:T(8,128)}) %reduce-scatter.84.cloned.1.call-update) | async-done | bytes 3538960 | tf_op jit(solution)/shard_map/reduce_scatter | solution.py:451
  2020.1 159.3 %reduce-scatter.86.cloned.1.call-done = bf16[4,2,192,768]{3,2,1,0:T(8,128)(2,1)} async-done(((bf16[4,2,768,768]{3,2,1,0:T(8,128)(2,1)}), bf16[4,2,192,768]{3,2,1,0:T(8,128)(2,1)}) %reduce-scatter.86.cloned.1.call-update) | async-done | bytes 2359312 | tf_op jit(solution)/shard_map/reduce_scatter | solution.py:427
  2190.3 138.3 %all-reduce.4.cloned.1.call-done = (bf16[3592,48]{0,1:T(8,128)(2,1)}, bf16[4,48,4608]{2,1,0:T(8,128)(2,1)}, bf16[4,3,192,192]{2,3,1,0:T(8,128)(2,1)}, bf16[4,192...) async-done(((bf16[3592,48]{0,1:T(8,128)(2,1)}, bf16[4,48,4608]{2,1,0:T(8,128)(2,1)}, bf16[4,3,192,192]{2,3,1,0:T(8,128)(2,1)}, bf16[4,192,192]{1,2,0:T(8,128)(2,1)}, ...) | async-done | bytes 5653264 | tf_op jit(solution)/shard_map/psum | solution.py:454
  2345.2 39.5 %all-reduce = (f32[]{:T(128)}, f32[]{:T(128)}) all-reduce(f32[]{:T(128)S(6)} %mul.1488, f32[]{:T(128)S(6)} %select_n.4), channel_id=1, replica_groups=mesh['shard'=4,'ctx'=2,'tp'=4] {'shard','ctx','tp'}, use_global_device_ids=true, to_apply=%region_35.36 | all-reduce | flops 2 | bytes 16 | tf_op jit(solution)/shard_map/psum | solution.py:121
  (1079 shorter events, 726.9 us)
Async XLA Ops:
  8.0 85.6 %all-gather.28.cloned.1.call-start = ((), (), s32[]{:S(2)}) async-start(), calls=%async_computation.29 | async-start | bytes 6057984 | tf_op jit(solution)/shard_map/all_gather | solution.py:150
  10.0 228.4 %all-gather.30.cloned.1.call-start = ((), (), s32[]{:S(2)}) async-start(), calls=%async_computation.30 | async-start | bytes 30081024 | tf_op jit(solution)/shard_map/all_gather | solution.py:151
  13.6 294.2 %reduce-scatter.34.cloned.1.call-start = ((), (), s32[]{:S(2)}) async-start(), calls=%async_computation.31 | async-start | bytes 983040 | tf_op jit(solution)/shard_map/reduce_scatter | solution.py:105
  284.5 54.1 %all-gather.32.cloned.1.call-start = ((), (), s32[]{:S(2)}) async-start(), calls=%async_computation.58 | async-start | bytes 2949120 | tf_op jit(solution)/shard_map/all_gather | solution.py:181
  288.6 101.3 %reduce-scatter.36.cloned.1.call-start = ((), (), s32[]{:S(2)}) async-start(), calls=%async_computation.32 | async-start | bytes 983040 | tf_op jit(solution)/shard_map/reduce_scatter | solution.py:105
  343.9 101.6 %reduce-scatter.38.cloned.1.call-start = ((), (), s32[]{:S(2)}) async-start(), calls=%async_computation.33 | async-start | bytes 983040 | tf_op jit(solution)/shard_map/reduce_scatter | solution.py:105
  422.8 51.8 %all-gather.34.cloned.1.call-start = ((), (), s32[]{:S(2)}) async-start(), calls=%async_computation.59 | async-start | bytes 2949120 | tf_op jit(solution)/shard_map/all_gather | solution.py:181
  423.4 103.9 %reduce-scatter.40.cloned.1.call-start = ((), (), s32[]{:S(2)}) async-start(), calls=%async_computation.34 | async-start | bytes 983040 | tf_op jit(solution)/shard_map/reduce_scatter | solution.py:105
  480.0 102.9 %reduce-scatter.42.cloned.1.call-start = ((), (), s32[]{:S(2)}) async-start(), calls=%async_computation.35 | async-start | bytes 983040 | tf_op jit(solution)/shard_map/reduce_scatter | solution.py:105
  560.1 51.8 %all-gather.36.cloned.1.call-start = ((), (), s32[]{:S(2)}) async-start(), calls=%async_computation.60 | async-start | bytes 2949120 | tf_op jit(solution)/shard_map/all_gather | solution.py:181
  560.7 103.8 %reduce-scatter.44.cloned.1.call-start = ((), (), s32[]{:S(2)}) async-start(), calls=%async_computation.36 | async-start | bytes 983040 | tf_op jit(solution)/shard_map/reduce_scatter | solution.py:105
  617.3 102.3 %reduce-scatter.46.cloned.1.call-start = ((), (), s32[]{:S(2)}) async-start(), calls=%async_computation.37 | async-start | bytes 983040 | tf_op jit(solution)/shard_map/reduce_scatter | solution.py:105
  696.7 52.3 %all-gather.38.cloned.1.call-start = ((), (), s32[]{:S(2)}) async-start(), calls=%async_computation.61 | async-start | bytes 2949120 | tf_op jit(solution)/shard_map/all_gather | solution.py:181
  697.5 79.0 %reduce-scatter.48.cloned.1.call-start = ((), (), s32[]{:S(2)}) async-start(), calls=%async_computation.38 | async-start | bytes 983040 | tf_op jit(solution)/shard_map/reduce_scatter | solution.py:105
  754.4 64.8 %reduce-scatter.50.cloned.1.call-start = ((), (), s32[]{:S(2)}) async-start(), calls=%async_computation.39 | async-start | bytes 983040 | tf_op jit(solution)/shard_map/reduce_scatter | solution.py:115
  795.3 59.3 %reduce-scatter.52.cloned.1.call-start = ((), (), s32[]{:S(2)}) async-start(), calls=%async_computation.40 | async-start | bytes 589824 | tf_op jit(solution)/shard_map/reduce_scatter | solution.py:372
  845.7 51.8 %reduce-scatter.56.cloned.1.call-start = ((), (), s32[]{:S(2)}) async-start(), calls=%async_computation.42 | async-start | bytes 983040 | tf_op jit(solution)/shard_map/reduce_scatter | solution.py:115
  874.2 65.2 %reduce-scatter.58.cloned.1.call-start = ((), (), s32[]{:S(2)}) async-start(), calls=%async_computation.43 | async-start | bytes 983040 | tf_op jit(solution)/shard_map/reduce_scatter | solution.py:115
  915.5 59.0 %reduce-scatter.60.cloned.1.call-start = ((), (), s32[]{:S(2)}) async-start(), calls=%async_computation.44 | async-start | bytes 589824 | tf_op jit(solution)/shard_map/reduce_scatter | solution.py:372
  965.7 51.5 %reduce-scatter.64.cloned.1.call-start = ((), (), s32[]{:S(2)}) async-start(), calls=%async_computation.46 | async-start | bytes 983040 | tf_op jit(solution)/shard_map/reduce_scatter | solution.py:115
  993.8 65.2 %reduce-scatter.66.cloned.1.call-start = ((), (), s32[]{:S(2)}) async-start(), calls=%async_computation.47 | async-start | bytes 983040 | tf_op jit(solution)/shard_map/reduce_scatter | solution.py:115
  1035.2 59.0 %reduce-scatter.68.cloned.1.call-start = ((), (), s32[]{:S(2)}) async-start(), calls=%async_computation.48 | async-start | bytes 589824 | tf_op jit(solution)/shard_map/reduce_scatter | solution.py:372
  1085.2 51.8 %reduce-scatter.72.cloned.1.call-start = ((), (), s32[]{:S(2)}) async-start(), calls=%async_computation.50 | async-start | bytes 983040 | tf_op jit(solution)/shard_map/reduce_scatter | solution.py:115
  1113.7 65.8 %reduce-scatter.74.cloned.1.call-start = ((), (), s32[]{:S(2)}) async-start(), calls=%async_computation.51 | async-start | bytes 983040 | tf_op jit(solution)/shard_map/reduce_scatter | solution.py:115
  1155.6 59.7 %reduce-scatter.76.cloned.1.call-start = ((), (), s32[]{:S(2)}) async-start(), calls=%async_computation.52 | async-start | bytes 589824 | tf_op jit(solution)/shard_map/reduce_scatter | solution.py:372
  1206.5 94.7 %reduce-scatter.80.cloned.1.call-start = ((), (), s32[]{:S(2)}) async-start(), calls=%async_computation.54 | async-start | bytes 983040 | tf_op jit(solution)/shard_map/reduce_scatter | solution.py:115
  1234.9 137.0 %reduce-scatter.90.cloned.1.call-start = ((), (), s32[]{:S(2)}) async-start(), calls=%async_computation.63 | async-start | bytes 1474560
  1242.0 132.3 %reduce-scatter.88.cloned.1.call-start = ((), (), s32[]{:S(2)}) async-start(), calls=%async_computation.62 | async-start | bytes 4423680
  1267.3 221.8 %reduce-scatter.82.cloned.1.call-start = ((), (), s32[]{:S(2)}) async-start(), calls=%async_computation.55 | async-start | bytes 12115968 | tf_op jit(solution)/shard_map/reduce_scatter | solution.py:450
  1331.4 685.3 %reduce-scatter.84.cloned.1.call-start = ((), (), s32[]{:S(2)}) async-start(), calls=%async_computation.56 | async-start | bytes 60162048 | tf_op jit(solution)/shard_map/reduce_scatter | solution.py:451
  1350.7 828.7 %reduce-scatter.86.cloned.1.call-start = ((), (), s32[]{:S(2)}) async-start(), calls=%async_computation.57 | async-start | bytes 11796480 | tf_op jit(solution)/shard_map/reduce_scatter | solution.py:427
  1371.8 956.8 %all-reduce.4.cloned.1.call-start = ((), (), s32[]{:S(2)}) async-start(), calls=%async_computation.64 | async-start | bytes 12115968 | tf_op jit(solution)/shard_map/psum | solution.py:454
  (312 other events, 5717.9 us)
Sparse Core Ops, SparseCore 0:
  11.6 82.0 all-gather.27
  95.7 142.6 all-gather.29
  284.6 23.1 reduce-scatter.33
  344.0 21.9 reduce-scatter.35
  422.9 22.5 reduce-scatter.37
  480.1 21.9 reduce-scatter.39
  560.3 22.5 reduce-scatter.41
  617.4 21.9 reduce-scatter.43
  696.8 22.7 reduce-scatter.45
  754.5 21.9 reduce-scatter.47
  795.4 23.7 reduce-scatter.49
  874.3 23.2 reduce-scatter.55
  915.6 23.7 reduce-scatter.57
  994.0 23.2 reduce-scatter.63
  1035.3 23.7 reduce-scatter.65
  1113.8 23.2 reduce-scatter.71
  1155.7 23.7 reduce-scatter.73
  1235.0 23.1 reduce-scatter.79
  1261.1 29.3 reduce-scatter.89
  1293.2 65.0 reduce-scatter.87
  1362.5 126.4 reduce-scatter.81
  1493.3 523.3 reduce-scatter.83
  2019.1 160.2 reduce-scatter.85
Sparse Core Ops, SparseCore 1:
  288.7 49.8 all-gather.31
  425.4 49.2 all-gather.33
  562.8 49.1 all-gather.35
  699.7 49.3 all-gather.37
  840.9 13.6 reduce-scatter.51
  857.4 13.1 reduce-scatter.53
  960.8 13.6 reduce-scatter.59
  977.1 13.1 reduce-scatter.61
  1080.4 13.6 reduce-scatter.67
  1097.0 13.1 reduce-scatter.69
  1201.6 13.6 reduce-scatter.75
  1218.2 13.1 reduce-scatter.77
  2179.5 149.0 all-reduce.3
where the time goes:
time: 2460 us; the launch traced here: 2450 us
  waiting for transfers between devices  1510 us (61%)
  blocking collectives  430 us (17%)
  matrix products  200 us (8%)
  other arithmetic  151 us (6%)
  local copies, waits for them, and re-layouts  125 us (5%)
  between operations  26.9 us (1%)
    reduce_scatter x1, waiting for transfers between devices, local(): lax.psum_scatter(grad_modulation, ('shard', 'tp'), scatter_dimension=1, t...  526 us
    reduce_scatter x8, waiting for transfers between devices, collect_grads(): lax.psum_scatter(part_sum.astype(jnp.bfloat16), 'tp', scatter_dimension=1...  165 us
    reduce_scatter x1, waiting for transfers between devices, local(): lax.psum_scatter(jnp.stack(grads_hidden).astype(jnp.bfloat16), 'shard', s...  159 us
    psum x1, waiting for transfers between devices, local(): lax.psum(shard_stem.astype(jnp.bfloat16), 'ctx').astype(jnp.float32)  138 us
    all_gather x1, waiting for transfers between devices, local(): lax.all_gather(modulation.astype(jnp.bfloat16), ('shard', 'tp'), axis=1,...  137 us
    all_gather x4, blocking collectives, local(): lax.all_gather(attention_in[layer_at].astype(jnp.bfloat16), 'shard', axis...  136 us
    reduce_scatter x1, waiting for transfers between devices, local(): lax.psum_scatter(grad_stem, ('shard', 'tp'), scatter_dimension=1, tiled=T...  109 us
    reduce_scatter x8, waiting for transfers between devices, collect_rows(): lax.psum_scatter(part_sum.astype(jnp.bfloat16), 'tp', scatter_dimension=1...  103 us
  transfers between devices with their start and end apart: 36, of which 30 were waited for; matrix products, arithmetic and copies ran while one was open for 9% of the time, Pallas kernels for 0%

commit v1 on v0

v1 whole, which is shorter than its diff:
```python
import math

import jax
import jax.numpy as jnp
from jax import lax
from jax.sharding import PartitionSpec as P

D = 768
HEAD_DIM = 64
CLASSES = 1000
FREQ = 256
PATCH = 2
STEPS = 1000
LAYERS = 4
PATCHES = 1024
PDIM = 16


norm_eps = 1e-06
clip_level = 0.5
learn_rate = 0.01
beta_first = 0.5
beta_second = 0.5
adam_eps = 1e-08
weight_decay = 0.1
bias_fix = 0.875
highest = lax.Precision.HIGHEST


def layer_norm(values):
    centre = values - jnp.mean(values, -1, keepdims=True)
    spread = jnp.mean(centre * centre, -1, keepdims=True)
    return centre * lax.rsqrt(spread + norm_eps)


def modulate(values, shift_rows, scale_rows):
    return layer_norm(values) * (1.0 + scale_rows) + shift_rows


def gelu_tanh(values):
    return jax.nn.gelu(values, approximate=True)


def patchify(image_in):
    latent_count, channels, height, columns = image_in.shape
    shaped = image_in.reshape(
        latent_count, channels, height // PATCH, PATCH, columns // PATCH, PATCH
    )
    shaped = shaped.transpose(0, 2, 4, 3, 5, 1)
    return shaped.reshape(
        latent_count, height // PATCH * (columns // PATCH), PATCH * PATCH * channels
    )


def positions(first_row, height, columns, model_width):
    quarter = model_width // 4
    omegas = jnp.exp(-math.log(10000.0) * jnp.arange(quarter).astype(jnp.float32) / quarter)
    row_angle = (first_row + jnp.arange(height)).astype(jnp.float32)[:, None] * omegas[None, :]
    col_angle = jnp.arange(columns).astype(jnp.float32)[:, None] * omegas[None, :]
    row_part = jnp.concatenate([jnp.sin(row_angle), jnp.cos(row_angle)], -1)
    col_part = jnp.concatenate([jnp.sin(col_angle), jnp.cos(col_angle)], -1)
    grid_table = jnp.concatenate(
        [
            jnp.broadcast_to(col_part[None], (height, columns, 2 * quarter)),
            jnp.broadcast_to(row_part[:, None], (height, columns, 2 * quarter)),
        ],
        -1,
    )
    return grid_table.reshape(height * columns, model_width)


def time_features(step_ids):
    half_width = FREQ // 2
    frequencies = jnp.exp(
        -math.log(10000.0) * jnp.arange(half_width).astype(jnp.float32) / half_width
    )
    angles = step_ids.astype(jnp.float32)[:, None] * frequencies[None, :]
    return jnp.concatenate([jnp.cos(angles), jnp.sin(angles)], -1)


def split_stem(stem_rows):
    bounds = [CLASSES, FREQ, D, D, D, PDIM, PDIM]
    pieces_out = []
    offset = 0
    for extent in bounds:
        pieces_out.append(stem_rows[offset : offset + extent])
        offset = offset + extent
    return pieces_out


def adam_update(master, first_moment, second_moment, gradient, factor):
    clipped = gradient * factor
    first_new = beta_first * first_moment + (1.0 - beta_first) * clipped
    second_new = beta_second * second_moment + (1.0 - beta_second) * clipped * clipped
    direction = first_new / bias_fix / (jnp.sqrt(second_new / bias_fix) + adam_eps)
    master_new = master - learn_rate * (direction + weight_decay * master)
    return (master_new, first_new, second_new, master_new.astype(jnp.bfloat16))


GROUP = ("ctx", "tp")
OWNERS = ("shard", "tp")
EVERY = ("shard", "ctx", "tp")


def gather_group(values):
    return lax.all_gather(values, GROUP, axis=0, tiled=True)


def scatter_group(part_sum):
    return lax.psum_scatter(
        part_sum.astype(jnp.bfloat16), GROUP, scatter_dimension=0, tiled=True
    ).astype(jnp.float32)


def scatter_tp(part_sum):
    return lax.psum_scatter(
        part_sum.astype(jnp.bfloat16), "tp", scatter_dimension=0, tiled=True
    ).astype(jnp.float32)


def own_half(values):
    half = values.shape[0] // lax.axis_size("ctx")
    return lax.dynamic_slice_in_dim(values, lax.axis_index("ctx") * half, half, 0)


def into_heads(values):
    return values.reshape(values.shape[0], -1, HEAD_DIM)


def attention_forward(hidden, mods, weights):
    width = weights.shape[1] // 4
    shift, scale, gate = mods[0:1], mods[1:2], mods[2:3]
    normed = gather_group(modulate(hidden, shift, scale).astype(jnp.bfloat16))
    query = jnp.dot(own_half(normed), weights[:, :width], preferred_element_type=jnp.float32)
    query = into_heads((query * HEAD_DIM**-0.5).astype(jnp.bfloat16))
    key_value = jnp.dot(
        normed, weights[:, width : 3 * width], preferred_element_type=jnp.float32
    ).astype(jnp.bfloat16)
    key, value = into_heads(key_value[:, :width]), into_heads(key_value[:, width:])
    scores = jnp.einsum("qhe,khe->hqk", query, key, preferred_element_type=jnp.float32)
    row_top = jnp.max(scores, -1, keepdims=True)
    exponent = jnp.exp(scores - row_top)
    row_total = jnp.sum(exponent, -1, keepdims=True)
    log_total = row_top + jnp.log(row_total)
    weights_low = (exponent / row_total).astype(jnp.bfloat16)
    mixed = jnp.einsum("hqk,khe->qhe", weights_low, value, preferred_element_type=jnp.float32)
    mixed = mixed.astype(jnp.bfloat16).reshape(mixed.shape[0], -1)
    branch = scatter_tp(
        jnp.einsum(
            "pe,de->pd", mixed, weights[:, 3 * width :], preferred_element_type=jnp.float32
        )
    )
    kept = (hidden, normed, query, key, value, log_total, mixed, branch)
    return hidden + gate * branch, kept


def feed_forward(hidden, mods, weights):
    width = weights.shape[1] // 2
    shift, scale, gate = mods[3:4], mods[4:5], mods[5:6]
    normed = gather_group(modulate(hidden, shift, scale).astype(jnp.bfloat16))
    hidden_pre = jnp.dot(normed, weights[:, :width], preferred_element_type=jnp.float32)
    activated = gelu_tanh(hidden_pre).astype(jnp.bfloat16)
    branch = scatter_group(
        jnp.einsum("pf,df->pd", activated, weights[:, width:], preferred_element_type=jnp.float32)
    )
    return hidden + gate * branch, (hidden, normed, hidden_pre, branch)


def feed_backward(grad_hidden, mods, weights, kept):
    hidden, normed, hidden_pre, branch = kept
    width = weights.shape[1] // 2
    shift, scale, gate = mods[3:4], mods[4:5], mods[5:6]
    grad_gate = jnp.sum(grad_hidden * branch, 0, keepdims=True)
    grad_branch = gather_group((gate * grad_hidden).astype(jnp.bfloat16))
    activated, gelu_pull = jax.vjp(gelu_tanh, hidden_pre)
    grad_down = jnp.einsum(
        "pd,pf->df",
        grad_branch,
        activated.astype(jnp.bfloat16),
        preferred_element_type=jnp.float32,
    )
    grad_act = jnp.dot(grad_branch, weights[:, width:], preferred_element_type=jnp.float32)
    grad_pre = gelu_pull(grad_act)[0].astype(jnp.bfloat16)
    grad_up = jnp.einsum("pd,pf->df", normed, grad_pre, preferred_element_type=jnp.float32)
    grad_normed = scatter_group(
        jnp.einsum("pf,df->pd", grad_pre, weights[:, :width], preferred_element_type=jnp.float32)
    )
    step, grad_shift, grad_scale = jax.vjp(modulate, hidden, shift, scale)[1](grad_normed)
    grads = jnp.concatenate([grad_up, grad_down], 1).astype(jnp.bfloat16)
    return grad_hidden + step, grads, jnp.concatenate([grad_shift, grad_scale, grad_gate], 0)


def attention_backward(grad_hidden, mods, weights, kept):
    hidden, normed, query, key, value, log_total, mixed, branch = kept
    width = weights.shape[1] // 4
    shift, scale, gate = mods[0:1], mods[1:2], mods[2:3]
    grad_gate = jnp.sum(grad_hidden * branch, 0, keepdims=True)
    grad_branch = lax.all_gather(
        (gate * grad_hidden).astype(jnp.bfloat16), "tp", axis=0, tiled=True
    )
    grad_out = jnp.einsum("pd,pe->de", grad_branch, mixed, preferred_element_type=jnp.float32)
    grad_mixed = into_heads(
        jnp.dot(grad_branch, weights[:, 3 * width :], preferred_element_type=jnp.float32).astype(
            jnp.bfloat16
        )
    )
    scores = jnp.einsum("qhe,khe->hqk", query, key, preferred_element_type=jnp.float32)
    attention_weights = jnp.exp(scores - log_total)
    weights_low = attention_weights.astype(jnp.bfloat16)
    grad_value = jnp.einsum(
        "hqk,qhe->khe", weights_low, grad_mixed, preferred_element_type=jnp.float32
    ).astype(jnp.bfloat16)
    grad_probs = jnp.einsum(
        "qhe,khe->hqk", grad_mixed, value, preferred_element_type=jnp.float32
    )
    inner_sum = jnp.sum(attention_weights * grad_probs, -1, keepdims=True)
    grad_scores = (attention_weights * (grad_probs - inner_sum)).astype(jnp.bfloat16)
    grad_query = jnp.einsum(
        "hqk,khe->qhe", grad_scores, key, preferred_element_type=jnp.float32
    ).astype(jnp.bfloat16)
    grad_key = jnp.einsum(
        "hqk,qhe->khe", grad_scores, query, preferred_element_type=jnp.float32
    ).astype(jnp.bfloat16)
    rows = normed.shape[0]
    grad_query = (grad_query * HEAD_DIM**-0.5).astype(jnp.bfloat16).reshape(query.shape[0], -1)
    pair = jnp.concatenate([grad_key.reshape(rows, -1), grad_value.reshape(rows, -1)], 1)
    grad_wq = jnp.einsum(
        "pd,pe->de", own_half(normed), grad_query, preferred_element_type=jnp.float32
    )
    grad_kv = jnp.einsum("pd,pe->de", normed, pair, preferred_element_type=jnp.float32)
    from_pair = jnp.einsum(
        "pe,de->pd", pair, weights[:, width : 3 * width], preferred_element_type=jnp.float32
    )
    from_query = jnp.einsum(
        "pe,de->pd", grad_query, weights[:, :width], preferred_element_type=jnp.float32
    )
    first = lax.axis_index("ctx") * query.shape[0]
    mine = lax.dynamic_slice_in_dim(from_pair, first, query.shape[0], 0) + from_query
    grad_normed = scatter_group(lax.dynamic_update_slice_in_dim(from_pair, mine, first, 0))
    step, grad_shift, grad_scale = jax.vjp(modulate, hidden, shift, scale)[1](grad_normed)
    grads = jnp.concatenate([grad_wq, grad_kv, grad_out], 1).astype(jnp.bfloat16)
    return grad_hidden + step, grads, jnp.concatenate([grad_shift, grad_scale, grad_gate], 0)


def silu_grad(values):
    gate = jax.nn.sigmoid(values)
    return gate * (1.0 + values * (1.0 - gate))


def local(
    noised,
    velocity,
    labels,
    time_ids,
    stem,
    stem_mean,
    stem_square,
    modulation,
    modulation_mean,
    modulation_square,
    attention_in,
    attention_in_mean,
    attention_in_square,
    attention_out,
    attention_out_mean,
    attention_out_square,
    feedforward,
    feedforward_mean,
    feedforward_square,
):
    tensor_ways = lax.axis_size("tp")
    shard_ways = lax.axis_size("shard")
    own_latent = lax.axis_index("shard")
    own_ctx = lax.axis_index("ctx")
    owned = stem.shape[1]
    first_owned = (own_latent * tensor_ways + lax.axis_index("tp")) * owned

    def own_columns(values):
        return lax.dynamic_slice_in_dim(values, first_owned, owned, values.ndim - 1)

    stem_low = stem.astype(jnp.bfloat16)
    class_own, time_in_own, time_out_own, shift_own, scale_own, patch_own, head_own = split_stem(
        stem_low
    )
    modulation_low = modulation.astype(jnp.bfloat16)
    packed_ids = lax.all_gather(
        jnp.stack([labels, time_ids], 1), "shard", axis=0, tiled=True
    )
    all_labels, all_times = packed_ids[:, 0], packed_ids[:, 1]
    latents = all_labels.shape[0]
    features = time_features(all_times).astype(jnp.bfloat16)
    time_pre = jnp.dot(features, time_in_own, preferred_element_type=jnp.float32)
    time_hidden_own = jax.nn.silu(time_pre).astype(jnp.bfloat16)
    packed = lax.all_gather(
        jnp.concatenate([time_hidden_own, patch_own, head_own], 0), OWNERS, axis=1, tiled=True
    )
    time_hidden = packed[:latents]
    patch_in, head_rows = packed[latents : latents + PDIM], packed[latents + PDIM :]
    onehot = (all_labels[:, None] == jnp.arange(CLASSES)[None, :]).astype(jnp.bfloat16)
    condition = jnp.dot(time_hidden, time_out_own, preferred_element_type=jnp.float32) + jnp.dot(
        onehot, class_own, preferred_element_type=jnp.float32
    )
    gated_own = jax.nn.silu(condition).astype(jnp.bfloat16)
    mod_part = jnp.einsum(
        "bd,lde->ble", gated_own, modulation_low, preferred_element_type=jnp.float32
    )
    layer_mods = lax.psum(
        lax.psum_scatter(mod_part, "shard", scatter_dimension=0, tiled=True), "tp"
    )[0].reshape(LAYERS, 6, D)
    gated = lax.all_gather(gated_own, OWNERS, axis=1, tiled=True)
    end_own = jnp.stack(
        [
            jnp.dot(gated, shift_own, preferred_element_type=jnp.float32),
            jnp.dot(gated, scale_own, preferred_element_type=jnp.float32),
        ],
        1,
    )
    end_all = lax.all_gather(end_own, OWNERS, axis=2, tiled=True)
    end_mods = lax.dynamic_index_in_dim(end_all, own_latent, 0, keepdims=False)
    end_shift, end_scale = end_mods[0:1], end_mods[1:2]

    hidden_half = feedforward.shape[3] // lax.axis_size("ctx")
    feed_low = lax.dynamic_slice_in_dim(feedforward, own_ctx * hidden_half, hidden_half, 3).astype(
        jnp.bfloat16
    )
    in_low, out_low = attention_in.astype(jnp.bfloat16), attention_out.astype(jnp.bfloat16)
    attention_blocks, feed_blocks = [], []
    for layer_at in range(LAYERS):
        block = jnp.concatenate([in_low[layer_at, number] for number in range(3)] + [out_low[layer_at]], 1)
        attention_blocks.append(lax.all_gather(block, "shard", axis=0, tiled=True))
        block = jnp.concatenate([feed_low[layer_at, 0], feed_low[layer_at, 1]], 1)
        feed_blocks.append(lax.all_gather(block, "shard", axis=0, tiled=True))

    pieces = patchify(noised)[0]
    rows_here = noised.shape[2] // PATCH
    first_row = (own_ctx * tensor_ways + lax.axis_index("tp")) * rows_here
    embedded = jnp.dot(pieces, patch_in, preferred_element_type=jnp.float32)
    hidden = embedded + positions(first_row, rows_here, noised.shape[3] // PATCH, D)
    kept_attention, kept_feed = [], []
    for layer_at in range(LAYERS):
        hidden, kept = attention_forward(hidden, layer_mods[layer_at], attention_blocks[layer_at])
        kept_attention.append(kept)
        hidden, kept = feed_forward(hidden, layer_mods[layer_at], feed_blocks[layer_at])
        kept_feed.append(kept)

    final_normed = modulate(hidden, end_shift, end_scale).astype(jnp.bfloat16)
    predicted = jnp.einsum(
        "pd,cd->pc", final_normed, head_rows, preferred_element_type=jnp.float32
    )
    target_rows = patchify(velocity)[0].astype(jnp.float32)
    weighting = 0.5 + time_ids.astype(jnp.float32)[0] / STEPS
    misfit = predicted - target_rows
    loss_scale = 1.0 / (shard_ways * PATCHES * PDIM)
    loss_local = jnp.sum(weighting * misfit * misfit) * loss_scale
    grad_pred = (2.0 * loss_scale * weighting * misfit).astype(jnp.bfloat16)
    grad_head = jnp.einsum("pc,pd->cd", grad_pred, final_normed, preferred_element_type=jnp.float32)
    grad_normed = jnp.dot(grad_pred, head_rows, preferred_element_type=jnp.float32)
    grad_hidden, grad_end_shift, grad_end_scale = jax.vjp(modulate, hidden, end_shift, end_scale)[
        1
    ](grad_normed)

    small = []
    shard_attention, shard_feed = [None] * LAYERS, [None] * LAYERS
    for layer_at in reversed(range(LAYERS)):
        grad_hidden, grads, small_two = feed_backward(
            grad_hidden, layer_mods[layer_at], feed_blocks[layer_at], kept_feed[layer_at]
        )
        shard_feed[layer_at] = lax.psum_scatter(grads, "shard", scatter_dimension=0, tiled=True)
        grad_hidden, grads, small_one = attention_backward(
            grad_hidden, layer_mods[layer_at], attention_blocks[layer_at], kept_attention[layer_at]
        )
        shard_attention[layer_at] = lax.psum_scatter(
            grads, "shard", scatter_dimension=0, tiled=True
        )
        small.append(jnp.concatenate([small_one, small_two], 0))
    grad_embed = grad_hidden.astype(jnp.bfloat16)
    grad_patch = jnp.einsum("pf,pd->fd", pieces, grad_embed, preferred_element_type=jnp.float32)

    small = jnp.concatenate(small[::-1] + [grad_end_shift, grad_end_scale], 0)
    small = lax.all_gather(lax.psum(small, GROUP), "shard", axis=0, tiled=False)
    grad_mod = small[:, : 6 * LAYERS].reshape(latents, LAYERS, 6 * D)
    grad_ends = small[:, 6 * LAYERS :]
    ends_here = own_columns(grad_ends)
    gated_part = jnp.dot(
        ends_here[:, 0], shift_own.astype(jnp.float32).T, precision=highest
    ) + jnp.dot(ends_here[:, 1], scale_own.astype(jnp.float32).T, precision=highest)
    grad_gated = lax.psum_scatter(
        gated_part, OWNERS, scatter_dimension=1, tiled=True
    ) + jnp.einsum(
        "ble,lde->bd", grad_mod, modulation_low.astype(jnp.float32), precision=highest
    )
    grad_condition = grad_gated * silu_grad(condition)
    grad_time_hidden = lax.psum_scatter(
        jnp.dot(grad_condition, time_out_own.astype(jnp.float32).T, precision=highest),
        OWNERS,
        scatter_dimension=1,
        tiled=True,
    )
    grad_time_pre = grad_time_hidden * silu_grad(time_pre)
    gated_wide = gated.astype(jnp.float32)
    grad_ends_own = lax.psum(
        lax.psum_scatter(
            jnp.concatenate([grad_patch, grad_head], 0), OWNERS, scatter_dimension=1, tiled=True
        ),
        "ctx",
    )
    shard_stem = jnp.concatenate(
        [
            jnp.dot(onehot.astype(jnp.float32).T, grad_condition, precision=highest),
            jnp.dot(features.astype(jnp.float32).T, grad_time_pre, precision=highest),
            jnp.dot(time_hidden.astype(jnp.float32).T, grad_condition, precision=highest),
            jnp.dot(gated_wide.T, ends_here[:, 0], precision=highest),
            jnp.dot(gated_wide.T, ends_here[:, 1], precision=highest),
            grad_ends_own,
        ],
        0,
    )
    shard_modulation = jnp.einsum(
        "bd,ble->lde", gated_own.astype(jnp.float32), grad_mod, precision=highest
    )
    shard_attention = lax.psum(jnp.stack(shard_attention), "ctx").astype(jnp.float32)
    cut = attention_in.shape[3]
    shard_in = jnp.stack(
        [shard_attention[:, :, number * cut : (number + 1) * cut] for number in range(3)], 1
    )
    shard_out = shard_attention[:, :, 3 * cut :]
    shard_hidden = jnp.stack(shard_feed).reshape(LAYERS, -1, 2, hidden_half).transpose(0, 2, 1, 3)
    shard_hidden = lax.all_gather(shard_hidden, "ctx", axis=3, tiled=True).astype(jnp.float32)
    squares = (
        jnp.sum(shard_stem * shard_stem)
        + jnp.sum(shard_modulation * shard_modulation)
        + jnp.sum(shard_in * shard_in)
        + jnp.sum(shard_out * shard_out)
        + jnp.sum(shard_hidden * shard_hidden)
    )
    squares = jnp.where(own_ctx == 0, squares, jnp.zeros((), jnp.float32))
    sums = lax.psum(jnp.stack([squares, loss_local]), EVERY)
    square_total, train_loss = sums[0], sums[1]
    total_norm = jnp.sqrt(square_total)
    factor = clip_level / jnp.maximum(total_norm, clip_level)
    stem_out = adam_update(stem, stem_mean, stem_square, shard_stem, factor)
    mod_out = adam_update(modulation, modulation_mean, modulation_square, shard_modulation, factor)
    in_out = adam_update(attention_in, attention_in_mean, attention_in_square, shard_in, factor)
    proj_out = adam_update(
        attention_out, attention_out_mean, attention_out_square, shard_out, factor
    )
    feed_out = adam_update(feedforward, feedforward_mean, feedforward_square, shard_hidden, factor)
    return (
        train_loss,
        total_norm,
        stem_out[0],
        stem_out[1],
        stem_out[2],
        stem_out[3],
        mod_out[0],
        mod_out[1],
        mod_out[2],
        mod_out[3],
        in_out[0],
        in_out[1],
        in_out[2],
        in_out[3],
        proj_out[0],
        proj_out[1],
        proj_out[2],
        proj_out[3],
        feed_out[0],
        feed_out[1],
        feed_out[2],
        feed_out[3],
    )


def solution(mesh):
    placed = (
        P("shard", None, ("ctx", "tp"), None),
        P("shard", None, ("ctx", "tp"), None),
        P("shard"),
        P("shard"),
        P(None, ("shard", "tp")),
        P(None, ("shard", "tp")),
        P(None, ("shard", "tp")),
        P(None, ("shard", "tp"), None),
        P(None, ("shard", "tp"), None),
        P(None, ("shard", "tp"), None),
        P(None, None, "shard", "tp"),
        P(None, None, "shard", "tp"),
        P(None, None, "shard", "tp"),
        P(None, "shard", "tp"),
        P(None, "shard", "tp"),
        P(None, "shard", "tp"),
        P(None, None, "shard", "tp"),
        P(None, None, "shard", "tp"),
        P(None, None, "shard", "tp"),
    )
    return jax.shard_map(
        local,
        mesh=mesh,
        in_specs=placed,
        out_specs=(
            P(),
            P(),
            P(None, ("shard", "tp")),
            P(None, ("shard", "tp")),
            P(None, ("shard", "tp")),
            P(None, ("shard", "tp")),
            P(None, ("shard", "tp"), None),
            P(None, ("shard", "tp"), None),
            P(None, ("shard", "tp"), None),
            P(None, ("shard", "tp"), None),
            P(None, None, "shard", "tp"),
            P(None, None, "shard", "tp"),
            P(None, None, "shard", "tp"),
            P(None, None, "shard", "tp"),
            P(None, "shard", "tp"),
            P(None, "shard", "tp"),
            P(None, "shard", "tp"),
            P(None, "shard", "tp"),
            P(None, None, "shard", "tp"),
            P(None, None, "shard", "tp"),
            P(None, None, "shard", "tp"),
            P(None, None, "shard", "tp"),
        ),
        check_vma=False,
    )
```

time: 2460 us -> 2190 us (0.89)
  blocking collectives: 430 us -> 174 us
  waiting for transfers between devices: 1510 us -> 1550 us
  other arithmetic: 151 us -> 112 us
  matrix products: 200 us -> 170 us
    reduce_scatter x27 -> x1, waiting for transfers between devices: 1150 us -> 56.6 us  [local(): lax.psum_scatter(jnp.concatenate([grad_patch, grad_head], 0), OWNERS, sca...]
    unnamed x38 -> x79, waiting for transfers between devices: 2.3 us -> 823 us
    all_gather x6 -> x21, waiting for transfers between devices: 220 us -> 594 us  [the longest x12 322 us: gather_group(): return lax.all_gather(values, GROUP, axis=0, tiled=True)]
    all_gather x32 -> x9, blocking collectives: 391 us -> 125 us  [the longest x4 35.7 us: attention_backward(): lax.all_gather((gate * grad_hidden).astype(jnp.bfloat16), 'tp', axis=0, t...]
    psum x1 -> x3, waiting for transfers between devices: 138 us -> 80.4 us  [the longest x1 38.6 us: local(): lax.psum(jnp.stack(shard_attention), 'ctx').astype(jnp.float32)]
    dot_general x86 -> x104, matrix products: 198 us -> 168 us  [the longest x4 15.7 us: attention_backward(): jnp.einsum('qhe,khe->hqk', grad_mixed, value, preferred_element_type=jnp....]
    unnamed x645 -> x656, local copies, waits for them, and re-layouts: 100 us -> 116 us
  transfers between devices with their start and end apart: 36 -> 52, of which waited for: 30 -> 51; matrix products, arithmetic and copies ran while one was open for 9% -> 7% of each run, Pallas kernels for 0% -> 0%
where the time goes in v1:
time: 2190 us; the launch traced here: 2180 us
  waiting for transfers between devices  1550 us (71%)
  blocking collectives  174 us (8%)
  matrix products  170 us (8%)
  local copies, waits for them, and re-layouts  137 us (6%)
  other arithmetic  112 us (5%)
  between operations  26.2 us (1%)
    unnamed x79, waiting for transfers between devices  823 us
    all_gather x12, waiting for transfers between devices, gather_group(): return lax.all_gather(values, GROUP, axis=0, tiled=True)  322 us
    all_gather x4, waiting for transfers between devices, local(): attention_blocks.append(lax.all_gather(block, 'shard', axis=0, tiled=True))  122 us
    all_gather x4, waiting for transfers between devices, local(): feed_blocks.append(lax.all_gather(block, 'shard', axis=0, tiled=True))  119 us
    unnamed x656, local copies, waits for them, and re-layouts  116 us
    reduce_scatter x1, waiting for transfers between devices, local(): lax.psum_scatter(jnp.concatenate([grad_patch, grad_head], 0), OWNERS, sca...  56.6 us
  transfers between devices with their start and end apart: 52, of which 51 were waited for; matrix products, arithmetic and copies ran while one was open for 7% of the time, Pallas kernels for 0%

profile of v1, /device:TPU:0, one launch (start us, length us, event | category | flops | bytes accessed | tf_op | source)
XLA Modules:
  0.0 2177.1 jit_solution(16799899683098616177)
XLA Ops:
  50.3 30.4 %all-reduce.12.cloned.1.call-done = f32[4,4,4608]{2,1,0:T(4,128)} async-done(((f32[4,4,4608]{2,1,0:T(4,128)}), f32[4,4,4608]{2,1,0:T(4,128)}) %all-reduce.12.cloned.1.call-update) | async-done | bytes 294928
  115.0 32.4 %all-gather.27.cloned.1.call-done = bf16[768,768]{1,0:T(8,128)(2,1)} async-done(((bf16[192,768]{1,0:T(8,128)(2,1)}), bf16[768,768]{1,0:T(8,128)(2,1)}) %all-gather.27.cloned.1.call-update) | async-done | bytes 1179664 | tf_op jit(solution)/shard_map/all_gather | solution.py:330
  211.4 29.8 %all-gather.31.cloned.1.call-done = bf16[768,768]{1,0:T(8,128)(2,1)} async-done(((bf16[192,768]{1,0:T(8,128)(2,1)}), bf16[768,768]{1,0:T(8,128)(2,1)}) %all-gather.31.cloned.1.call-update) | async-done | bytes 1179664 | tf_op jit(solution)/shard_map/all_gather | solution.py:332
  277.1 36.4 %reduce-scatter.84.cloned.1.call-done = bf16[128,768]{1,0:T(8,128)(2,1)} async-done(((bf16[1024,768]{1,0:T(8,128)(2,1)}), bf16[128,768]{1,0:T(8,128)(2,1)}) %reduce-scatter.84.cloned.1.call-update) | async-done | bytes 196624
  315.9 30.0 %all-gather.35.cloned.1.call-done = bf16[768,768]{1,0:T(8,128)(2,1)} async-done(((bf16[192,768]{1,0:T(8,128)(2,1)}), bf16[768,768]{1,0:T(8,128)(2,1)}) %all-gather.35.cloned.1.call-update) | async-done | bytes 1179664 | tf_op jit(solution)/shard_map/all_gather | solution.py:330
  411.2 29.8 %all-gather.39.cloned.1.call-done = bf16[768,768]{1,0:T(8,128)(2,1)} async-done(((bf16[192,768]{1,0:T(8,128)(2,1)}), bf16[768,768]{1,0:T(8,128)(2,1)}) %all-gather.39.cloned.1.call-update) | async-done | bytes 1179664 | tf_op jit(solution)/shard_map/all_gather | solution.py:332
  476.5 36.7 %reduce-scatter.88.cloned.1.call-done = bf16[128,768]{1,0:T(8,128)(2,1)} async-done(((bf16[1024,768]{1,0:T(8,128)(2,1)}), bf16[128,768]{1,0:T(8,128)(2,1)}) %reduce-scatter.88.cloned.1.call-update) | async-done | bytes 196624
  516.1 29.4 %all-gather.43.cloned.1.call-done = bf16[768,768]{1,0:T(8,128)(2,1)} async-done(((bf16[192,768]{1,0:T(8,128)(2,1)}), bf16[768,768]{1,0:T(8,128)(2,1)}) %all-gather.43.cloned.1.call-update) | async-done | bytes 1179664 | tf_op jit(solution)/shard_map/all_gather | solution.py:330
  610.6 29.8 %all-gather.47.cloned.1.call-done = bf16[768,768]{1,0:T(8,128)(2,1)} async-done(((bf16[192,768]{1,0:T(8,128)(2,1)}), bf16[768,768]{1,0:T(8,128)(2,1)}) %all-gather.47.cloned.1.call-update) | async-done | bytes 1179664 | tf_op jit(solution)/shard_map/all_gather | solution.py:332
  640.4 27.5 %all-gather.45.cloned.1.call-done = bf16[1024,768]{0,1:T(8,128)(2,1)} async-done(((bf16[128,768]{0,1:T(8,128)(2,1)}), bf16[1024,768]{0,1:T(8,128)(2,1)}) %all-gather.45.cloned.1.call-update) | async-done | bytes 1572880 | tf_op jit(solution)/shard_map/all_gather | solution.py:106
  676.1 36.6 %reduce-scatter.92.cloned.1.call-done = bf16[128,768]{1,0:T(8,128)(2,1)} async-done(((bf16[1024,768]{1,0:T(8,128)(2,1)}), bf16[128,768]{1,0:T(8,128)(2,1)}) %reduce-scatter.92.cloned.1.call-update) | async-done | bytes 196624
  715.3 29.8 %all-gather.51.cloned.1.call-done = bf16[768,768]{1,0:T(8,128)(2,1)} async-done(((bf16[192,768]{1,0:T(8,128)(2,1)}), bf16[768,768]{1,0:T(8,128)(2,1)}) %all-gather.51.cloned.1.call-update) | async-done | bytes 1179664 | tf_op jit(solution)/shard_map/all_gather | solution.py:330
  811.2 29.1 %all-gather.55.cloned.1.call-done = bf16[768,768]{1,0:T(8,128)(2,1)} async-done(((bf16[192,768]{1,0:T(8,128)(2,1)}), bf16[768,768]{1,0:T(8,128)(2,1)}) %all-gather.55.cloned.1.call-update) | async-done | bytes 1179664 | tf_op jit(solution)/shard_map/all_gather | solution.py:332
  964.8 38.4 %reduce-scatter.98.cloned.1.call-done = bf16[128,768]{1,0:T(8,128)(2,1)} async-done(((bf16[1024,768]{1,0:T(8,128)(2,1)}), bf16[128,768]{1,0:T(8,128)(2,1)}) %reduce-scatter.98.cloned.1.call-update) | async-done | bytes 196624
  1030.5 38.5 %reduce-scatter.100.cloned.1.call-done = bf16[128,768]{1,0:T(8,128)(2,1)} async-done(((bf16[1024,768]{1,0:T(8,128)(2,1)}), bf16[128,768]{1,0:T(8,128)(2,1)}) %reduce-scatter.100.cloned.1.call-update) | async-done | bytes 196624
  1107.0 38.3 %reduce-scatter.102.cloned.1.call-done = bf16[128,768]{1,0:T(8,128)(2,1)} async-done(((bf16[1024,768]{1,0:T(8,128)(2,1)}), bf16[128,768]{1,0:T(8,128)(2,1)}) %reduce-scatter.102.cloned.1.call-update) | async-done | bytes 196624
  1170.3 38.4 %reduce-scatter.104.cloned.1.call-done = bf16[128,768]{1,0:T(8,128)(2,1)} async-done(((bf16[1024,768]{1,0:T(8,128)(2,1)}), bf16[128,768]{1,0:T(8,128)(2,1)}) %reduce-scatter.104.cloned.1.call-update) | async-done | bytes 196624
  1246.8 38.4 %reduce-scatter.106.cloned.1.call-done = bf16[128,768]{1,0:T(8,128)(2,1)} async-done(((bf16[1024,768]{1,0:T(8,128)(2,1)}), bf16[128,768]{1,0:T(8,128)(2,1)}) %reduce-scatter.106.cloned.1.call-update) | async-done | bytes 196624
  1310.2 38.4 %reduce-scatter.108.cloned.1.call-done = bf16[128,768]{1,0:T(8,128)(2,1)} async-done(((bf16[1024,768]{1,0:T(8,128)(2,1)}), bf16[128,768]{1,0:T(8,128)(2,1)}) %reduce-scatter.108.cloned.1.call-update) | async-done | bytes 196624
  1386.6 38.3 %reduce-scatter.110.cloned.1.call-done = bf16[128,768]{1,0:T(8,128)(2,1)} async-done(((bf16[1024,768]{1,0:T(8,128)(2,1)}), bf16[128,768]{1,0:T(8,128)(2,1)}) %reduce-scatter.110.cloned.1.call-update) | async-done | bytes 196624
  1457.1 31.7 %reduce-scatter.112.cloned.1.call-done = bf16[128,768]{1,0:T(8,128)(2,1)} async-done(((bf16[1024,768]{1,0:T(8,128)(2,1)}), bf16[128,768]{1,0:T(8,128)(2,1)}) %reduce-scatter.112.cloned.1.call-update) | async-done | bytes 196624
  1581.3 29.3 %reduce-scatter.130.cloned.1.call-done = bf16[192,768]{1,0:T(8,128)(2,1)} async-done(((bf16[768,768]{1,0:T(8,128)(2,1)}), bf16[192,768]{1,0:T(8,128)(2,1)}) %reduce-scatter.130.cloned.1.call-update) | async-done | bytes 294928
  1611.9 29.5 %reduce-scatter.128.cloned.1.call-done = bf16[192,768]{1,0:T(8,128)(2,1)} async-done(((bf16[768,768]{1,0:T(8,128)(2,1)}), bf16[192,768]{1,0:T(8,128)(2,1)}) %reduce-scatter.128.cloned.1.call-update) | async-done | bytes 294928
  1642.8 29.4 %reduce-scatter.126.cloned.1.call-done = bf16[192,768]{1,0:T(8,128)(2,1)} async-done(((bf16[768,768]{1,0:T(8,128)(2,1)}), bf16[192,768]{1,0:T(8,128)(2,1)}) %reduce-scatter.126.cloned.1.call-update) | async-done | bytes 294928
  1704.8 28.8 %reduce-scatter.122.cloned.1.call-done = bf16[192,768]{1,0:T(8,128)(2,1)} async-done(((bf16[768,768]{1,0:T(8,128)(2,1)}), bf16[192,768]{1,0:T(8,128)(2,1)}) %reduce-scatter.122.cloned.1.call-update) | async-done | bytes 294928
  1735.7 28.7 %reduce-scatter.120.cloned.1.call-done = bf16[192,768]{1,0:T(8,128)(2,1)} async-done(((bf16[768,768]{1,0:T(8,128)(2,1)}), bf16[192,768]{1,0:T(8,128)(2,1)}) %reduce-scatter.120.cloned.1.call-update) | async-done | bytes 294928
  1772.5 50.4 %reduce-scatter.114.cloned.1.call-done = f32[48,4]{1,0:T(8,128)} async-done(((f32[768,4]{1,0:T(8,128)}), f32[48,4]{1,0:T(8,128)}) %reduce-scatter.114.cloned.1.call-update) | async-done | bytes 784
  1858.9 31.8 %all-gather.65.cloned.1.call-done = bf16[4,2,192,768]{3,2,1,0:T(8,128)(2,1)} async-done(((bf16[4,2,192,384]{3,2,1,0:T(8,128)(2,1)}), bf16[4,2,192,768]{3,2,1,0:T(8,128)(2,1)}) %all-gather.65.cloned.1.call-update) | async-done | bytes 2359312 | tf_op jit(solution)/shard_map/all_gather | solution.py:428
  1903.5 47.3 %reduce-scatter.116.cloned.1.call-done = f32[48,4]{1,0:T(8,128)} async-done(((f32[768,4]{1,0:T(8,128)}), f32[48,4]{1,0:T(8,128)}) %reduce-scatter.116.cloned.1.call-update) | async-done | bytes 784
  1953.2 56.6 %reduce-scatter.80.cloned.1.call-done = f32[32,48]{0,1:T(8,128)} async-done(((f32[32,768]{0,1:T(8,128)}), f32[32,48]{0,1:T(8,128)}) %reduce-scatter.80.cloned.1.call-update) | async-done | bytes 6160 | tf_op jit(solution)/shard_map/reduce_scatter | solution.py:402
  2024.7 38.6 %all-reduce.10.cloned.1.call-done = bf16[4,192,768]{1,2,0:T(8,128)(2,1)} async-done(((bf16[4,192,768]{1,2,0:T(8,128)(2,1)}), bf16[4,192,768]{1,2,0:T(8,128)(2,1)}) %all-reduce.10.cloned.1.call-update) | async-done | bytes 1179664 | tf_op jit(solution)/shard_map/psum | solution.py:421
  2074.5 39.5 %psum.39 = f32[2]{0:T(128)S(1)} all-reduce(f32[2]{0:T(128)S(1)} %pad_maximum_fusion.38), channel_id=1, replica_groups=mesh['shard'=4,'ctx'=2,'tp'=4] {'shard','ctx','tp'}, use_global_device_ids=true, to_apply=%region_112.113 | all-reduce | flops 2 | bytes 16 | tf_op jit(solution)/shard_map/psum | solution.py:437
  (1125 shorter events, 1033.0 us)
Async XLA Ops:
  83.8 90.9 %all-gather.25.cloned.1.call-start = ((), (), s32[]{:S(2)}) async-start(), calls=%async_computation.28 | async-start | bytes 1769472 | tf_op jit(solution)/shard_map/all_gather | solution.py:106
  114.9 94.0 %reduce-scatter.82.cloned.1.call-start = ((), (), s32[]{:S(2)}) async-start(), calls=%async_computation.52 | async-start | bytes 983040
  211.3 102.1 %reduce-scatter.84.cloned.1.call-start = ((), (), s32[]{:S(2)}) async-start(), calls=%async_computation.53 | async-start | bytes 1769472
  276.8 96.4 %all-gather.33.cloned.1.call-start = ((), (), s32[]{:S(2)}) async-start(), calls=%async_computation.32 | async-start | bytes 1769472 | tf_op jit(solution)/shard_map/all_gather | solution.py:106
  315.9 92.8 %reduce-scatter.86.cloned.1.call-start = ((), (), s32[]{:S(2)}) async-start(), calls=%async_computation.54 | async-start | bytes 983040
  411.1 102.1 %reduce-scatter.88.cloned.1.call-start = ((), (), s32[]{:S(2)}) async-start(), calls=%async_computation.55 | async-start | bytes 1769472
  476.5 96.3 %all-gather.41.cloned.1.call-start = ((), (), s32[]{:S(2)}) async-start(), calls=%async_computation.36 | async-start | bytes 1769472 | tf_op jit(solution)/shard_map/all_gather | solution.py:106
  515.6 92.5 %reduce-scatter.90.cloned.1.call-start = ((), (), s32[]{:S(2)}) async-start(), calls=%async_computation.56 | async-start | bytes 983040
  585.6 82.4 %all-gather.45.cloned.1.call-start = ((), (), s32[]{:S(2)}) async-start(), calls=%async_computation.38 | async-start | bytes 1769472 | tf_op jit(solution)/shard_map/all_gather | solution.py:106
  610.6 102.1 %reduce-scatter.92.cloned.1.call-start = ((), (), s32[]{:S(2)}) async-start(), calls=%async_computation.57 | async-start | bytes 1769472
  676.1 96.6 %all-gather.49.cloned.1.call-start = ((), (), s32[]{:S(2)}) async-start(), calls=%async_computation.40 | async-start | bytes 1769472 | tf_op jit(solution)/shard_map/all_gather | solution.py:106
  715.1 92.9 %reduce-scatter.94.cloned.1.call-start = ((), (), s32[]{:S(2)}) async-start(), calls=%async_computation.58 | async-start | bytes 983040
  811.2 110.2 %reduce-scatter.96.cloned.1.call-start = ((), (), s32[]{:S(2)}) async-start(), calls=%async_computation.59 | async-start | bytes 1769472
  874.1 83.6 %all-gather.57.cloned.1.call-start = ((), (), s32[]{:S(2)}) async-start(), calls=%async_computation.44 | async-start | bytes 1769472 | tf_op jit(solution)/shard_map/all_gather | solution.py:106
  964.7 104.3 %reduce-scatter.100.cloned.1.call-start = ((), (), s32[]{:S(2)}) async-start(), calls=%async_computation.61 | async-start | bytes 1769472
  1106.9 101.8 %reduce-scatter.104.cloned.1.call-start = ((), (), s32[]{:S(2)}) async-start(), calls=%async_computation.63 | async-start | bytes 1769472
  1246.7 101.9 %reduce-scatter.108.cloned.1.call-start = ((), (), s32[]{:S(2)}) async-start(), calls=%async_computation.65 | async-start | bytes 1769472
  1386.5 102.2 %reduce-scatter.112.cloned.1.call-start = ((), (), s32[]{:S(2)}) async-start(), calls=%async_computation.67 | async-start | bytes 1769472
  1450.3 95.4 %all-reduce.8.cloned.1.call-start = ((), (), s32[]{:S(2)}) async-start(), calls=%async_computation.48 | async-start | bytes 196608 | tf_op jit(solution)/shard_map/psum | solution.py:380
  1493.5 86.5 %reduce-scatter.132.cloned.1.call-start = ((), (), s32[]{:S(2)}) async-start(), calls=%async_computation.77 | async-start | bytes 1474560
  1496.3 114.3 %reduce-scatter.130.cloned.1.call-start = ((), (), s32[]{:S(2)}) async-start(), calls=%async_computation.76 | async-start | bytes 1474560
  1501.6 139.8 %reduce-scatter.128.cloned.1.call-start = ((), (), s32[]{:S(2)}) async-start(), calls=%async_computation.75 | async-start | bytes 1474560
  1507.1 165.0 %reduce-scatter.126.cloned.1.call-start = ((), (), s32[]{:S(2)}) async-start(), calls=%async_computation.74 | async-start | bytes 1474560
  1512.4 190.5 %reduce-scatter.124.cloned.1.call-start = ((), (), s32[]{:S(2)}) async-start(), calls=%async_computation.73 | async-start | bytes 1474560
  1517.1 216.6 %reduce-scatter.122.cloned.1.call-start = ((), (), s32[]{:S(2)}) async-start(), calls=%async_computation.72 | async-start | bytes 1474560
  1521.8 242.6 %reduce-scatter.120.cloned.1.call-start = ((), (), s32[]{:S(2)}) async-start(), calls=%async_computation.71 | async-start | bytes 1474560
  1526.4 296.5 %reduce-scatter.114.cloned.1.call-start = ((), (), s32[]{:S(2)}) async-start(), calls=%async_computation.68 | async-start | bytes 417792
  1566.7 287.4 %reduce-scatter.118.cloned.1.call-start = ((), (), s32[]{:S(2)}) async-start(), calls=%async_computation.70 | async-start | bytes 1474560
  1568.3 322.4 %all-gather.65.cloned.1.call-start = ((), (), s32[]{:S(2)}) async-start(), calls=%async_computation.51 | async-start | bytes 3538944 | tf_op jit(solution)/shard_map/all_gather | solution.py:428
  1674.7 276.1 %reduce-scatter.116.cloned.1.call-start = ((), (), s32[]{:S(2)}) async-start(), calls=%async_computation.69 | async-start | bytes 417792
  1828.3 181.5 %reduce-scatter.80.cloned.1.call-start = ((), (), s32[]{:S(2)}) async-start(), calls=%async_computation.49 | async-start | bytes 417792 | tf_op jit(solution)/shard_map/reduce_scatter | solution.py:402
  1831.7 231.6 %all-reduce.10.cloned.1.call-start = ((), (), s32[]{:S(2)}) async-start(), calls=%async_computation.50 | async-start | bytes 3145728 | tf_op jit(solution)/shard_map/psum | solution.py:421
  (320 other events, 10219.2 us)
Sparse Core Ops, SparseCore 0:
  47.4 33.1 all-reduce.11
  83.6 29.4 all-reduce.5
  115.2 32.1 all-gather.26
  210.9 30.2 all-gather.30
  275.0 38.3 reduce-scatter.83
  315.6 30.2 all-gather.34
  410.7 30.2 all-gather.38
  474.8 38.3 reduce-scatter.87
  515.2 30.2 all-gather.42
  610.1 30.2 all-gather.46
  674.3 38.3 reduce-scatter.91
  714.8 30.2 all-gather.50
  810.0 30.2 all-gather.54
  874.2 42.9 reduce-scatter.95
  964.8 38.3 reduce-scatter.97
  1030.6 38.3 reduce-scatter.99
  1107.0 38.2 reduce-scatter.101
  1170.4 38.3 reduce-scatter.103
  1246.8 38.3 reduce-scatter.105
  1310.2 38.3 reduce-scatter.107
  1386.7 38.2 reduce-scatter.109
  1450.4 38.3 reduce-scatter.111
  1493.6 52.0 all-reduce.7
  1548.6 31.3 reduce-scatter.131
  1705.7 27.9 reduce-scatter.121
  1736.4 27.9 reduce-scatter.119
  1768.3 54.6 reduce-scatter.113
  1825.7 28.3 reduce-scatter.117
  1856.0 34.6 all-gather.64
  1894.8 56.0 reduce-scatter.115
  1954.8 55.0 reduce-scatter.79
  2012.7 50.5 all-reduce.9
  (20 shorter events, 505.7 us)

commit v2 on v1

v2 whole, which is shorter than its diff:
```python
import functools
import math

import jax
import jax.numpy as jnp
from jax import lax
from jax.experimental import pallas as pl
from jax.experimental.pallas import tpu as pltpu
from jax.sharding import PartitionSpec as P

D = 768
HEAD_DIM = 64
CLASSES = 1000
FREQ = 256
PATCH = 2
STEPS = 1000
LAYERS = 4
PATCHES = 1024
PDIM = 16


norm_eps = 1e-06
clip_level = 0.5
learn_rate = 0.01
beta_first = 0.5
beta_second = 0.5
adam_eps = 1e-08
weight_decay = 0.1
bias_fix = 0.875
highest = lax.Precision.HIGHEST


def layer_norm(values):
    centre = values - jnp.mean(values, -1, keepdims=True)
    spread = jnp.mean(centre * centre, -1, keepdims=True)
    return centre * lax.rsqrt(spread + norm_eps)


def modulate(values, shift_rows, scale_rows):
    return layer_norm(values) * (1.0 + scale_rows) + shift_rows


def gelu_tanh(values):
    return jax.nn.gelu(values, approximate=True)


def patchify(image_in):
    latent_count, channels, height, columns = image_in.shape
    shaped = image_in.reshape(
        latent_count, channels, height // PATCH, PATCH, columns // PATCH, PATCH
    )
    shaped = shaped.transpose(0, 2, 4, 3, 5, 1)
    return shaped.reshape(
        latent_count, height // PATCH * (columns // PATCH), PATCH * PATCH * channels
    )


def positions(first_row, height, columns, model_width):
    quarter = model_width // 4
    omegas = jnp.exp(-math.log(10000.0) * jnp.arange(quarter).astype(jnp.float32) / quarter)
    row_angle = (first_row + jnp.arange(height)).astype(jnp.float32)[:, None] * omegas[None, :]
    col_angle = jnp.arange(columns).astype(jnp.float32)[:, None] * omegas[None, :]
    row_part = jnp.concatenate([jnp.sin(row_angle), jnp.cos(row_angle)], -1)
    col_part = jnp.concatenate([jnp.sin(col_angle), jnp.cos(col_angle)], -1)
    grid_table = jnp.concatenate(
        [
            jnp.broadcast_to(col_part[None], (height, columns, 2 * quarter)),
            jnp.broadcast_to(row_part[:, None], (height, columns, 2 * quarter)),
        ],
        -1,
    )
    return grid_table.reshape(height * columns, model_width)


def time_features(step_ids):
    half_width = FREQ // 2
    frequencies = jnp.exp(
        -math.log(10000.0) * jnp.arange(half_width).astype(jnp.float32) / half_width
    )
    angles = step_ids.astype(jnp.float32)[:, None] * frequencies[None, :]
    return jnp.concatenate([jnp.cos(angles), jnp.sin(angles)], -1)


def split_stem(stem_rows):
    bounds = [CLASSES, FREQ, D, D, D, PDIM, PDIM]
    pieces_out = []
    offset = 0
    for extent in bounds:
        pieces_out.append(stem_rows[offset : offset + extent])
        offset = offset + extent
    return pieces_out


def adam_update(master, first_moment, second_moment, gradient, factor):
    clipped = gradient * factor
    first_new = beta_first * first_moment + (1.0 - beta_first) * clipped
    second_new = beta_second * second_moment + (1.0 - beta_second) * clipped * clipped
    direction = first_new / bias_fix / (jnp.sqrt(second_new / bias_fix) + adam_eps)
    master_new = master - learn_rate * (direction + weight_decay * master)
    return (master_new, first_new, second_new, master_new.astype(jnp.bfloat16))


GROUP = ("ctx", "tp")
OWNERS = ("shard", "tp")
EVERY = ("shard", "ctx", "tp")
HOP_WAYS = 8


MESH = pl.DeviceIdType.MESH
BF = jnp.bfloat16
F32 = jnp.float32
SCORE_SCALE = HEAD_DIM**-0.5


def place():
    ctx, tp = lax.axis_index("ctx"), lax.axis_index("tp")
    core = tp % 2
    row = tp // 2
    return ctx, row, core


def square(ctx, row, core):
    return ctx * 4 + row * 2 + core


def remote(index, src, dst, send, recv, **where):
    return pltpu.make_async_remote_copy(
        src_ref=src,
        dst_ref=dst,
        send_sem=send.at[index],
        recv_sem=recv.at[index],
        device_id=where,
        device_id_type=MESH,
    )


def greet_signal(shard_ways):
    ctx, row, core = place()
    barrier = pltpu.get_barrier_semaphore()
    tp = row * 2 + core
    pl.semaphore_signal(barrier, inc=1, device_id={"ctx": 1 - ctx}, device_id_type=MESH)
    pl.semaphore_signal(barrier, inc=1, device_id={"tp": (tp + 2) % 4}, device_id_type=MESH)
    pl.semaphore_signal(
        barrier, inc=1, device_id={"tp": row * 2 + 1 - core}, device_id_type=MESH
    )
    if shard_ways == 1:
        return
    at = lax.axis_index("shard")

    @pl.when(at > 0)
    def _():
        pl.semaphore_signal(barrier, inc=1, device_id={"shard": at - 1}, device_id_type=MESH)

    @pl.when(at < shard_ways - 1)
    def _():
        pl.semaphore_signal(barrier, inc=1, device_id={"shard": at + 1}, device_id_type=MESH)


def greet_wait(shard_ways):
    barrier = pltpu.get_barrier_semaphore()
    if shard_ways == 1:
        pl.semaphore_wait(barrier, 3)
        return
    at = lax.axis_index("shard")

    @pl.when((at > 0) & (at < shard_ways - 1))
    def _():
        pl.semaphore_wait(barrier, 5)

    @pl.when((at == 0) | (at == shard_ways - 1))
    def _():
        pl.semaphore_wait(barrier, 4)


GATHER_COPIES = 13


class GroupGather:
    def __init__(self, buf, send, recv):
        ctx, row, core = place()
        half = buf.shape[1] // 2
        tp = row * 2 + core
        across, along = {"ctx": 1 - ctx}, {"tp": (tp + 2) % 4}
        beside = {"tp": row * 2 + 1 - core}
        own = square(ctx, row, core)
        self.by_x, self.by_y = square(1 - ctx, row, core), square(ctx, 1 - row, core)
        self.far = square(1 - ctx, 1 - row, core)

        def piece(block, which):
            if which is None:
                return buf.at[block]
            return buf.at[block, pl.ds(which * half, half)]

        def make(index, block, which, where):
            return remote(index, piece(block, which), piece(block, which), send, recv, **where)

        self.first = [
            make(0, own, 0, across),
            make(1, own, 1, along),
            make(2, own, None, beside),
            make(3, own, 1, across),
            make(4, own, 0, along),
        ]
        self.second = [
            (0, make(5, self.by_x, 0, along)),
            (0, make(6, self.by_x, 0, beside)),
            (1, make(7, self.by_y, 1, across)),
            (1, make(8, self.by_y, 1, beside)),
            (3, make(9, self.by_x, 1, beside)),
            (4, make(10, self.by_y, 0, beside)),
        ]
        self.third = [
            (5, make(11, self.far, 0, beside)),
            (7, make(12, self.far, 1, beside)),
        ]
        self.all = self.first + [c for _, c in self.second] + [c for _, c in self.third]

    def start(self):
        for copy in self.first:
            copy.start()

    def relay(self):
        waited = set()
        for needs, copy in self.second:
            if needs not in waited:
                self.all[needs].wait_recv()
                waited.add(needs)
            copy.start()

    def relay_far(self):
        for needs, copy in self.third:
            self.all[needs].wait_recv()
            copy.start()

    def wait_chip(self, which):
        for index in {"own": (2,), "x": (6, 9), "y": (8, 10), "far": (11, 12)}[which]:
            self.all[index].wait_recv()

    def finish(self):
        for copy in self.all:
            copy.wait_send()


SCATTER_COPIES = 10


class GroupScatter:
    def __init__(self, part, beside_in, summed, turn_in, send, recv, base):
        ctx, row, core = place()
        half = part.shape[1] // 2
        tp = row * 2 + core
        across, along = {"ctx": 1 - ctx}, {"tp": (tp + 2) % 4}
        beside = {"tp": row * 2 + 1 - core}
        self.part, self.beside_in, self.summed, self.turn_in = part, beside_in, summed, turn_in
        self.core, self.half = core, half
        self.chips = {
            "far": (1 - ctx, 1 - row),
            "x": (1 - ctx, row),
            "y": (ctx, 1 - row),
            "own": (ctx, row),
        }
        self.slot = {name: a * 2 + b for name, (a, b) in self.chips.items()}
        self.order = ["far", "x", "y", "own"]
        self.pair = {}
        for number, name in enumerate(self.order):
            a, b = self.chips[name]
            self.pair[name] = remote(
                base + number,
                part.at[square(a, b, 1 - core)],
                beside_in.at[self.slot[name]],
                send,
                recv,
                **beside,
            )

        def turn(index, name, which, place_at, where):
            return remote(
                base + index,
                summed.at[self.slot[name], pl.ds(which * half, half)],
                turn_in.at[place_at],
                send,
                recv,
                **where,
            )

        self.far_x = turn(4, "far", 0, 0, across)
        self.far_y = turn(5, "far", 1, 1, along)
        self.near_x = turn(6, "x", 0, 2, across)
        self.near_y = turn(7, "y", 1, 3, along)
        self.last_y = turn(8, "y", 0, 4, along)
        self.last_x = turn(9, "x", 1, 5, across)
        self.all = list(self.pair.values()) + [
            self.far_x,
            self.far_y,
            self.near_x,
            self.near_y,
            self.last_y,
            self.last_x,
        ]

    def send_pair(self, name):
        self.pair[name].start()

    def add_pair(self, name):
        self.pair[name].wait_recv()
        a, b = self.chips[name]
        mine = self.part[square(a, b, self.core)].astype(F32)
        slot = self.slot[name]
        self.summed[slot] = (mine + self.beside_in[slot].astype(F32)).astype(BF)
        if name == "far":
            self.far_x.start()
            self.far_y.start()
        if name == "x":
            self.near_x.start()
        if name == "y":
            self.near_y.start()

    def turn_corner(self):
        half = self.half
        low, high = pl.ds(0, half), pl.ds(half, half)
        self.far_x.wait_recv()
        slot = self.slot["y"]
        kept = self.summed[slot, low].astype(F32) + self.turn_in[0].astype(F32)
        self.summed[slot, low] = kept.astype(BF)
        self.last_y.start()
        self.far_y.wait_recv()
        slot = self.slot["x"]
        kept = self.summed[slot, high].astype(F32) + self.turn_in[1].astype(F32)
        self.summed[slot, high] = kept.astype(BF)
        self.last_x.start()

    def total(self):
        half = self.half
        slot = self.slot["own"]
        for copy in (self.near_x, self.near_y, self.last_y, self.last_x):
            copy.wait_recv()
        low = (
            self.summed[slot, pl.ds(0, half)].astype(F32)
            + self.turn_in[2].astype(F32)
            + self.turn_in[4].astype(F32)
        )
        high = (
            self.summed[slot, pl.ds(half, half)].astype(F32)
            + self.turn_in[3].astype(F32)
            + self.turn_in[5].astype(F32)
        )
        return jnp.concatenate([low, high], 0)

    def finish(self):
        for copy in self.all:
            copy.wait_send()


class LineGather:
    def __init__(self, ways, src, buf, local_sem, send, recv, base):
        self.ways, self.at = ways, lax.axis_index("shard")
        at = self.at
        rows = src.shape[0]
        self.own = pltpu.make_async_copy(src, buf.at[pl.ds(at * rows, rows)], local_sem)

        def hop(index, block, first, to):
            target = buf.at[pl.ds(block * rows, rows)]
            return remote(index, src if first else target, target, send, recv, shard=to)

        def clip(v):
            return jnp.clip(v, 0, ways - 1)

        steps = ways - 1
        self.right = [
            hop(base + k - 1, clip(at - k + 1), k == 1, clip(at + 1)) for k in range(1, ways)
        ]
        self.left = [
            hop(base + steps + k - 1, clip(at + k - 1), k == 1, clip(at - 1))
            for k in range(1, ways)
        ]

    def start(self):
        self.own.start()
        self.step(1)

    def step(self, k):
        at, ways = self.at, self.ways
        if k > 1:
            pl.when(at >= k - 1)(self.right[k - 2].wait_recv)
        pl.when((at < ways - 1) & (at >= k - 1))(self.right[k - 1].start)
        if k > 1:
            pl.when(at <= ways - k)(self.left[k - 2].wait_recv)
        pl.when((at > 0) & (at <= ways - k))(self.left[k - 1].start)

    def finish(self):
        at, ways = self.at, self.ways
        last = ways - 1
        pl.when(at >= last)(self.right[last - 1].wait_recv)
        pl.when(at <= 0)(self.left[last - 1].wait_recv)
        for k in range(1, ways):
            pl.when((at < ways - 1) & (at >= k - 1))(self.right[k - 1].wait_send)
            pl.when((at > 0) & (at <= ways - k))(self.left[k - 1].wait_send)
        self.own.wait()


def norm_rows(values):
    centre = values - jnp.mean(values, -1, keepdims=True)
    spread = jnp.mean(centre * centre, -1, keepdims=True)
    return centre, lax.rsqrt(spread + norm_eps)


def dot(left, right):
    return lax.dot_general(left, right, (((1,), (0,)), ((), ())), preferred_element_type=F32)


def dot_wide(left, right):
    return lax.dot_general(left, right, (((1,), (1,)), ((), ())), preferred_element_type=F32)


def dot_tall(left, right):
    return lax.dot_general(left, right, (((0,), (0,)), ((), ())), preferred_element_type=F32)


def gelu_parts(values):
    inner = math.sqrt(2.0 / math.pi) * (values + 0.044715 * (values * values * values))
    return jnp.tanh(inner)


def feed_forward_kernel(
    ways,
    gate,
    ready,
    hidden_ref,
    mods_ref,
    weights_hbm,
    *rest,
):
    if ways > 1:
        next_src, *rest = rest
    hidden_out, branch_out, normed_hbm, pre_hbm, *rest = rest
    if ways > 1:
        next_hbm, *rest = rest
    weights, gathered, pre, part, beside_in, summed, turn_in, *rest = rest
    if ways > 1:
        next_buf, *rest = rest
    local, send, recv = rest
    rows = hidden_ref.shape[0]
    if gate is not None:
        greet_signal(gate)
    if not ready:
        load = pltpu.make_async_copy(weights_hbm, weights, local.at[0])
        load.start()
    centre, scale_by = norm_rows(hidden_ref[...])
    normed = centre * scale_by * (1.0 + mods_ref[4:5, :]) + mods_ref[3:4, :]
    ctx, row, core = place()
    gathered[square(ctx, row, core)] = normed.astype(BF)
    gather = GroupGather(gathered, send, recv)
    scatter = GroupScatter(part, beside_in, summed, turn_in, send, recv, GATHER_COPIES)
    if gate is not None:
        greet_wait(gate)
    gather.start()
    if ways > 1:
        line = LineGather(
            ways, next_src, next_buf, local.at[3], send, recv, GATHER_COPIES + SCATTER_COPIES
        )
        line.start()
    if not ready:
        load.wait()
    width = pre.shape[-1]

    def up(name):
        a, b = scatter.chips[name]
        first = square(a, b, 0)
        rows_here = gathered[pl.ds(first, 2)].reshape(2 * rows, gathered.shape[2])
        value = dot(rows_here, weights[:, :width])
        pre[pl.ds(first, 2)] = value.reshape(2, rows, width)

    def down(name):
        a, b = scatter.chips[name]
        first = square(a, b, 0)
        value = pre[pl.ds(first, 2)].reshape(2 * rows, width)
        act = (0.5 * value * (1.0 + gelu_parts(value))).astype(BF)
        out = dot_wide(act, weights[:, width:]).astype(BF)
        part[pl.ds(first, 2)] = out.reshape(2, rows, out.shape[1])

    gather.wait_chip("own")
    up("own")
    gather.relay()
    gather.wait_chip("x")
    up("x")
    gather.wait_chip("y")
    up("y")
    if ways > 1:
        line.step(2)
    gather.relay_far()
    gather.wait_chip("far")
    keep_normed = pltpu.make_async_copy(gathered, normed_hbm, local.at[1])
    keep_normed.start()
    up("far")
    keep_pre = pltpu.make_async_copy(pre, pre_hbm, local.at[2])
    keep_pre.start()
    down("far")
    scatter.send_pair("far")
    down("x")
    scatter.send_pair("x")
    scatter.add_pair("far")
    down("y")
    scatter.send_pair("y")
    scatter.add_pair("x")
    down("own")
    scatter.send_pair("own")
    scatter.add_pair("y")
    scatter.add_pair("own")
    if ways > 1:
        for k in range(3, ways):
            line.step(k)
    scatter.turn_corner()
    branch = scatter.total()
    branch_out[...] = branch
    hidden_out[...] = hidden_ref[...] + mods_ref[5:6, :] * branch
    gather.finish()
    scatter.finish()
    keep_normed.wait()
    keep_pre.wait()
    if ways > 1:
        line.finish()
        keep_next = pltpu.make_async_copy(next_buf, next_hbm, local.at[0])
        keep_next.start()
        keep_next.wait()


ANY = pl.BlockSpec(memory_space=pl.ANY)
VMEM = pl.BlockSpec(memory_space=pltpu.VMEM)


def line_copies(ways):
    return 2 * (ways - 1) if ways > 1 else 0


def sds(shape, dtype):
    return jax.ShapeDtypeStruct(shape, dtype)


PAIR_COPIES = 3


class RowScatter:
    def __init__(self, part, beside_in, summed, turn_in, send, recv, base):
        ctx, row, core = place()
        tp = row * 2 + core
        beside = {"tp": row * 2 + 1 - core}
        self.part, self.beside_in, self.summed, self.turn_in = part, beside_in, summed, turn_in
        self.core = core
        self.chip = {"y": 1 - row, "own": row}
        self.pair = {}
        for number, name in enumerate(("y", "own")):
            self.pair[name] = remote(
                base + number,
                part.at[self.chip[name] * 2 + 1 - core],
                beside_in.at[number],
                send,
                recv,
                **beside,
            )
        self.turn = remote(base + 2, summed, turn_in, send, recv, tp=(tp + 2) % 4)
        self.all = list(self.pair.values()) + [self.turn]

    def send_pair(self, name):
        self.pair[name].start()

    def add_pair(self, name):
        number = 0 if name == "y" else 1
        self.pair[name].wait_recv()
        mine = self.part[self.chip[name] * 2 + self.core].astype(F32)
        return mine + self.beside_in[number].astype(F32)

    def send_far(self):
        self.summed[...] = self.add_pair("y").astype(BF)
        self.turn.start()

    def total(self):
        own = self.add_pair("own")
        self.turn.wait_recv()
        return own + self.turn_in[...].astype(F32)

    def finish(self):
        for copy in self.all:
            copy.wait_send()


def attention_forward_kernel(ways, gate, hidden_ref, mods_ref, weights_hbm, *rest):
    if ways > 1:
        next_src, *rest = rest
    hidden_out, branch_out, normed_hbm, q_hbm, k_hbm, v_hbm, lse_hbm, mixed_hbm, *rest = rest
    if ways > 1:
        next_hbm, *rest = rest
    weights, gathered, q, k, v, lse, mixed, part, beside_in, summed, turn_in, *rest = rest
    if ways > 1:
        next_buf, *rest = rest
    local, send, recv = rest
    rows, model = hidden_ref.shape
    heads = q.shape[0]
    cut = heads * HEAD_DIM
    greet_signal(gate)
    load = pltpu.make_async_copy(weights_hbm, weights, local.at[0])
    load.start()
    centre, scale_by = norm_rows(hidden_ref[...])
    normed = centre * scale_by * (1.0 + mods_ref[1:2, :]) + mods_ref[0:1, :]
    ctx, row, core = place()
    gathered[square(ctx, row, core)] = normed.astype(BF)
    gather = GroupGather(gathered, send, recv)
    scatter = RowScatter(part, beside_in, summed, turn_in, send, recv, GATHER_COPIES)
    greet_wait(gate)
    gather.start()
    if ways > 1:
        line = LineGather(
            ways, next_src, next_buf, local.at[8], send, recv, GATHER_COPIES + PAIR_COPIES
        )
        line.start()
    load.wait()
    chips = {
        "own": (ctx, row),
        "x": (1 - ctx, row),
        "y": (ctx, 1 - row),
        "far": (1 - ctx, 1 - row),
    }

    def project(name):
        a, b = chips[name]
        first = square(a, b, 0)
        here = gathered[pl.ds(first, 2)].reshape(2 * rows, model)
        span = pl.ds(pl.multiple_of(first * rows, 2 * rows), 2 * rows)
        pair = dot(here, weights[:, 2 * cut :]).astype(BF)
        for head in range(heads):
            k[head, span] = pair[:, head * HEAD_DIM : (head + 1) * HEAD_DIM]
            v[head, span] = pair[:, cut + head * HEAD_DIM : cut + (head + 1) * HEAD_DIM]
        if name in ("own", "y"):
            query = (dot(here, weights[:, :cut]) * SCORE_SCALE).astype(BF)
            span = pl.ds(pl.multiple_of(b * 2 * rows, 2 * rows), 2 * rows)
            for head in range(heads):
                q[head, span] = query[:, head * HEAD_DIM : (head + 1) * HEAD_DIM]

    gather.wait_chip("own")
    project("own")
    gather.relay()
    gather.wait_chip("x")
    project("x")
    gather.wait_chip("y")
    project("y")
    if ways > 1:
        line.step(2)
    gather.relay_far()
    gather.wait_chip("far")
    keep = [pltpu.make_async_copy(gathered, normed_hbm, local.at[1])]
    keep[0].start()
    project("far")
    for number, (src, dst) in enumerate(((q, q_hbm), (k, k_hbm), (v, v_hbm))):
        keep.append(pltpu.make_async_copy(src, dst, local.at[2 + number]))
        keep[-1].start()

    def attend(name):
        b = chips[name][1]
        for head in range(heads):
            @pl.loop(0, 2)
            def _(step):
                at = b * 2 + step
                span = pl.ds(pl.multiple_of(at * rows, rows), rows)
                scores = dot_wide(q[head, span], k[head])
                top = jnp.max(scores, -1, keepdims=True)
                exponent = jnp.exp(scores - top)
                total = jnp.sum(exponent, -1, keepdims=True)
                out = dot(exponent.astype(BF), v[head]) / total
                mixed[span, head * HEAD_DIM : (head + 1) * HEAD_DIM] = out.astype(BF)
                wide = jnp.broadcast_to(top + jnp.log(total), (rows, rows))
                lse[head, pl.ds(at, 1)] = wide.T[0:1]

        @pl.loop(0, 2)
        def _(step):
            at = b * 2 + step
            span = pl.ds(pl.multiple_of(at * rows, rows), rows)
            part[at] = dot_wide(mixed[span, :], weights[:, cut : 2 * cut]).astype(BF)

    attend("y")
    scatter.send_pair("y")
    if ways > 1:
        line.step(3)
    attend("own")
    scatter.send_pair("own")
    scatter.send_far()
    for number, (src, dst) in enumerate(((lse, lse_hbm), (mixed, mixed_hbm))):
        keep.append(pltpu.make_async_copy(src, dst, local.at[5 + number]))
        keep[-1].start()
    branch = scatter.total()
    branch_out[...] = branch
    hidden_out[...] = hidden_ref[...] + mods_ref[2:3, :] * branch
    gather.finish()
    scatter.finish()
    for copy in keep:
        copy.wait()
    if ways > 1:
        line.finish()
        keep_next = pltpu.make_async_copy(next_buf, next_hbm, local.at[0])
        keep_next.start()
        keep_next.wait()


def layer_forward_kernel(ways, last, *refs):
    hop, more = int(ways > 1), int(ways > 1 and not last)
    (
        (hidden, mods, weights),
        feed_weights,
        feed_own,
        ahead,
        outs,
        feed_block,
        feed_outs,
        ahead_block,
        scratch,
        feed_buf,
        sems,
        feed_scratch,
        ahead_buf,
        feed_sems,
    ) = split_refs(refs, 3, 1 - hop, hop, more, 8, hop, 4, more, 11, 1, 3, 6, more, 3)
    attention_forward_kernel(
        ways,
        ways,
        hidden,
        mods,
        weights,
        *feed_own,
        *outs,
        *feed_block,
        *scratch,
        *(feed_buf if hop else ()),
        *sems,
    )
    feed_forward_kernel(
        ways if more else 1,
        None,
        hop == 1,
        outs[0],
        mods,
        *(feed_weights or (None,)),
        *ahead,
        *feed_outs,
        *ahead_block,
        *feed_buf,
        *feed_scratch,
        *ahead_buf,
        *feed_sems,
    )


def layer_forward(hidden, mods, weights, feed_weights, feed_own, ahead, number):
    rows, model = hidden.shape
    cut = weights.shape[1] // 4
    heads = cut // HEAD_DIM
    ways = 1 if feed_own is None else lax.axis_size("shard")
    hop, last = ways > 1, ahead is None
    kept = [
        sds((8, rows, model), BF),
        sds((heads, 4 * rows, HEAD_DIM), BF),
        sds((heads, 8 * rows, HEAD_DIM), BF),
        sds((heads, 8 * rows, HEAD_DIM), BF),
        sds((heads, 4, rows), F32),
        sds((4 * rows, cut), BF),
    ]
    wide = sds(weights.shape, BF)
    width = weights.shape[1] // 2
    row_pair = [sds((rows, model), F32), sds((rows, model), F32)]
    feed_kept = [sds((8, rows, model), BF), sds((8, rows, width), F32)]
    outs = row_pair + kept + [wide] * hop + row_pair + feed_kept + [wide] * (hop and not last)
    out_specs = [VMEM, VMEM] + [ANY] * (len(kept) + hop)
    out_specs += [VMEM, VMEM] + [ANY] * (2 + (hop and not last))

    def buffers(copies, locals_used):
        return [
            pltpu.SemaphoreType.DMA((locals_used,)),
            pltpu.SemaphoreType.DMA((copies,)),
            pltpu.SemaphoreType.DMA((copies,)),
        ]

    scratch = [pltpu.VMEM(weights.shape, BF)]
    scratch += [pltpu.VMEM(leaf.shape, leaf.dtype) for leaf in kept]
    scratch += [
        pltpu.VMEM((4, rows, model), BF),
        pltpu.VMEM((2, rows, model), BF),
        pltpu.VMEM((rows, model), BF),
        pltpu.VMEM((rows, model), BF),
        pltpu.VMEM(weights.shape, BF),
    ]
    scratch += buffers(GATHER_COPIES + PAIR_COPIES + line_copies(ways), 9)
    scratch += [
        pltpu.VMEM((8, rows, model), BF),
        pltpu.VMEM((8, rows, width), F32),
        pltpu.VMEM((8, rows, model), BF),
        pltpu.VMEM((4, rows, model), BF),
        pltpu.VMEM((4, rows, model), BF),
        pltpu.VMEM((6, rows // 2, model), BF),
    ]
    if hop and not last:
        scratch.append(pltpu.VMEM(weights.shape, BF))
    scratch += buffers(GATHER_COPIES + SCATTER_COPIES + line_copies(ways), 4)
    given = [weights] + ([feed_own] if hop else [feed_weights]) + [ahead] * (hop and not last)
    result = pl.pallas_call(
        functools.partial(layer_forward_kernel, ways, last),
        out_shape=outs,
        in_specs=[VMEM, VMEM] + [ANY] * len(given),
        out_specs=out_specs,
        scratch_shapes=scratch,
        compiler_params=pltpu.CompilerParams(collective_id=number, has_side_effects=True),
        name="layer_forward",
    )(hidden, mods, *given)
    middle, branch, *rest = result
    saved, rest = rest[:6], rest[6:]
    if hop:
        feed_weights, rest = rest[0], rest[1:]
    hidden_new, feed_branch, normed, pre, *rest = rest
    kept_attention = (hidden, branch, *saved)
    kept_feed = (middle, normed, pre, feed_branch)
    return hidden_new, kept_attention, kept_feed, feed_weights, rest[0] if rest else None


class LineScatter:
    def __init__(self, ways, src, arrived, sums, total, send, recv, base):
        self.ways, self.at, self.src = ways, lax.axis_index("shard"), src
        self.arrived, self.sums, self.total = arrived, sums, total
        self.rows = total.shape[0]
        self.sem = send, recv, base
        at, steps = self.at, ways - 1
        self.sides = []
        for side in range(2):
            place_at = at if side == 0 else ways - 1 - at
            to = jnp.clip(at + 1 if side == 0 else at - 1, 0, ways - 1)
            first, summed = [], []
            for k in range(1, ways):
                index = side * steps + k - 1
                block = ways - k if side == 0 else k - 1
                first.append(self.hop(index, self.block(block), to))
                summed.append(self.hop(index, sums.at[index], to) if k > 1 else None)
            self.sides.append((place_at, first, summed))

    def block(self, number):
        return self.src.at[pl.ds(number * self.rows, self.rows)]

    def hop(self, index, src, to):
        send, recv, base = self.sem
        return pltpu.make_async_remote_copy(
            src_ref=src,
            dst_ref=self.arrived.at[index],
            send_sem=send.at[base + index],
            recv_sem=recv.at[base + index],
            device_id={"shard": to},
            device_id_type=MESH,
        )

    def step(self, k):
        ways, at = self.ways, self.at
        for side, (place_at, first, summed) in enumerate(self.sides):
            pl.when(place_at == 0)(first[k - 1].start)
            if k == 1:
                continue
            index = side * (ways - 1) + k - 1
            block = at + ways - k if side == 0 else at - ways + k

            @pl.when((place_at >= 1) & (place_at <= k - 1) & (place_at < ways - 1))
            def _():
                first[k - 2].wait_recv()
                mine = self.block(jnp.clip(block, 0, ways - 1))[...].astype(F32)
                self.sums[index] = (mine + self.arrived[index - 1].astype(F32)).astype(BF)
                summed[k - 1].start()

    def finish(self):
        ways, at = self.ways, self.at
        self.total[...] = self.block(at)[...].astype(F32)
        for side, (place_at, first, summed) in enumerate(self.sides):
            @pl.when(place_at >= 1)
            def _():
                first[ways - 2].wait_recv()
                index = side * (ways - 1) + ways - 2
                self.total[...] = self.total[...] + self.arrived[index].astype(F32)

            for k in range(1, ways):
                pl.when((place_at <= k - 1) & (place_at < ways - 1))(first[k - 1].wait_send)


class Extra:
    def __init__(self, ways, sums_src, swap_src, refs, local, first_local, send, recv, base):
        self.ways = ways
        self.sums_hbm, self.swap_hbm = sums_src, swap_src
        self.refs, self.local, self.at = refs, local, first_local
        self.ready = sums_src is not None and sums_src is refs["src"]
        if sums_src is not None and not self.ready:
            self.load = pltpu.make_async_copy(sums_src, refs["src"], local.at[first_local])
        if sums_src is not None:
            self.line = LineScatter(
                ways, refs["src"], refs["arrived"], refs["sums"], refs["total"], send, recv, base
            )
            base = base + 2 * (ways - 1)
        if swap_src is not None:
            ctx = lax.axis_index("ctx")
            self.swaps = [
                remote(base + number, src, refs["swap"].at[number], send, recv, ctx=1 - ctx)
                for number, src in enumerate(swap_src)
            ]

    def begin(self):
        if self.sums_hbm is not None and not self.ready:
            self.load.start()

    def start(self):
        if self.sums_hbm is not None:
            if not self.ready:
                self.load.wait()
            self.line.step(1)

    def start_swap(self):
        if self.swap_hbm is not None:
            for copy in self.swaps:
                copy.start()

    def step(self, k):
        if self.sums_hbm is not None and k < self.ways:
            self.line.step(k)

    def finish(self):
        keep = []
        if self.swap_hbm is not None:
            for number, copy in enumerate(self.swaps):
                copy.wait_recv()
                copy.wait_send()
            keep.append(
                pltpu.make_async_copy(
                    self.refs["swap"], self.refs["swap_out"], self.local.at[self.at + 1]
                )
            )
            keep[-1].start()
        if self.sums_hbm is not None:
            self.line.finish()
            self.refs["shard_out"][...] = self.refs["total"][...].astype(BF)
        for copy in keep:
            copy.wait()


def extra_shapes(ways, grads, swaps):
    given, outs, specs, scratch, copies = [], [], [], [], 0
    if grads is not None:
        rows, width = grads.shape[0] // ways, grads.shape[1]
        given.append(grads)
        outs.append(sds((rows, width), BF))
        specs.append(VMEM)
        scratch += [
            pltpu.VMEM(grads.shape, BF),
            pltpu.VMEM((2 * (ways - 1), rows, width), BF),
            pltpu.VMEM((2 * (ways - 1), rows, width), BF),
            pltpu.VMEM((rows, width), F32),
        ]
        copies += 2 * (ways - 1)
    if swaps:
        given += list(swaps)
        shape = (len(swaps), *swaps[0].shape)
        outs.append(sds(shape, BF))
        specs.append(ANY)
        scratch.append(pltpu.VMEM(shape, BF))
        copies += len(swaps)
    return given, outs, specs, scratch, copies


def take_extra(has_sums, swaps, ins, outs, scratch):
    refs = {}
    ins, outs, scratch = list(ins), list(outs), list(scratch)
    sums_src = swap_src = None
    if has_sums:
        sums_src = ins.pop(0)
        refs["shard_out"] = outs.pop(0)
        for name in ("src", "arrived", "sums", "total"):
            refs[name] = scratch.pop(0)
    if swaps:
        swap_src = [ins.pop(0) for _ in range(swaps)]
        refs["swap_out"] = outs.pop(0)
        refs["swap"] = scratch.pop(0)
    return sums_src, swap_src, refs


def modulate_backward(grad, hidden, scale, step_ref, small_ref):
    centre, scale_by = norm_rows(hidden)
    normed = centre * scale_by
    both = grad * normed
    small_ref[0:1, :] = jnp.sum(grad, 0, keepdims=True)
    small_ref[1:2, :] = jnp.sum(both, 0, keepdims=True)
    inner = grad * (1.0 + scale)
    mean = jnp.mean(inner, -1, keepdims=True)
    along = jnp.mean(inner * normed, -1, keepdims=True)
    step_ref[...] = step_ref[...] + (inner - mean - normed * along) * scale_by


def split_refs(refs, *counts):
    out, at = [], 0
    for count in counts:
        out.append(refs[at : at + count])
        at += count
    return out


def feed_backward_kernel(ways, gate, has_sums, swaps, *refs):
    extra_in, extra_out = int(has_sums) + swaps, int(has_sums) + int(swaps > 0)
    extra_scratch = 4 * int(has_sums) + int(swaps > 0)
    ins, ex_in, outs, ex_out, scratch, ex_scratch, sems = split_refs(
        refs, 7, extra_in, 3, extra_out, 11, extra_scratch, 3
    )
    grad_ref, hidden_ref, branch_ref, mods_ref, weights_hbm, normed_hbm, pre_hbm = ins
    grad_out, small_out, dw_hbm = outs
    weights, gathered, normed, pre, act, dpre, dw, part, beside_in, summed, turn_in = scratch
    local, send, recv = sems
    rows, model = grad_ref.shape
    width = pre.shape[-1]
    greet_signal(gate)
    loads = [
        pltpu.make_async_copy(src, dst, local.at[number])
        for number, (src, dst) in enumerate(
            ((weights_hbm, weights), (pre_hbm, pre), (normed_hbm, normed))
        )
    ]
    for copy in loads:
        copy.start()
    sums_src, swap_src, ex = take_extra(has_sums, swaps, ex_in, ex_out, ex_scratch)
    extra = Extra(
        ways, sums_src, swap_src, ex, local, 4, send, recv, GATHER_COPIES + SCATTER_COPIES
    )
    extra.begin()
    ctx, row, core = place()
    grad = grad_ref[...]
    gathered[square(ctx, row, core)] = (mods_ref[5:6, :] * grad).astype(BF)
    gather = GroupGather(gathered, send, recv)
    scatter = GroupScatter(part, beside_in, summed, turn_in, send, recv, GATHER_COPIES)
    greet_wait(gate)
    gather.start()
    extra.start()
    extra.start_swap()
    small_out[2:3, :] = jnp.sum(grad * branch_ref[...], 0, keepdims=True)
    loads[0].wait()
    loads[1].wait()

    def span_of(name):
        a, b = scatter.chips[name]
        return pl.ds(pl.multiple_of(square(a, b, 0) * rows, 2 * rows), 2 * rows)

    def back(name):
        a, b = scatter.chips[name]
        here = gathered[pl.ds(square(a, b, 0), 2)].reshape(2 * rows, model)
        value = pre[pl.ds(square(a, b, 0), 2)].reshape(2 * rows, width)
        grad_act = dot(here, weights[:, width:])
        root = math.sqrt(2.0 / math.pi)
        bend = gelu_parts(value)
        act[span_of(name), :] = (0.5 * value * (1.0 + bend)).astype(BF)
        slope = 0.5 * (1.0 + bend) + 0.5 * value * (1.0 - bend * bend) * root * (
            1.0 + 3.0 * 0.044715 * value * value
        )
        dpre[span_of(name), :] = (grad_act * slope).astype(BF)

    def down(name):
        a, b = scatter.chips[name]
        out = dot_wide(dpre[span_of(name), :], weights[:, :width]).astype(BF)
        part[pl.ds(square(a, b, 0), 2)] = out.reshape(2, rows, model)

    gather.wait_chip("own")
    back("own")
    gather.relay()
    gather.wait_chip("x")
    back("x")
    gather.wait_chip("y")
    back("y")
    extra.step(2)
    gather.relay_far()
    gather.wait_chip("far")
    back("far")
    down("far")
    scatter.send_pair("far")
    down("x")
    scatter.send_pair("x")
    scatter.add_pair("far")
    down("y")
    scatter.send_pair("y")
    scatter.add_pair("x")
    down("own")
    scatter.send_pair("own")
    scatter.add_pair("y")
    scatter.add_pair("own")
    loads[2].wait()
    tile = 256

    def wide_rows(ref, at):
        return ref[:, :, pl.ds(pl.multiple_of(at * tile, tile), tile)].reshape(8 * rows, tile)

    def out_rows(at):
        return pl.ds(pl.multiple_of(at * tile, tile), tile)

    @pl.loop(0, model // tile)
    def _(at):
        dw[out_rows(at), :width] = dot_tall(wide_rows(normed, at), dpre[...]).astype(BF)

    for k in range(3, ways):
        extra.step(k)
    scatter.turn_corner()

    @pl.loop(0, model // tile)
    def _(at):
        dw[out_rows(at), width:] = dot_tall(wide_rows(gathered, at), act[...]).astype(BF)

    keep = pltpu.make_async_copy(dw, dw_hbm, local.at[3])
    keep.start()
    grad_out[...] = grad
    modulate_backward(scatter.total(), hidden_ref[...], mods_ref[4:5, :], grad_out, small_out)
    gather.finish()
    scatter.finish()
    extra.finish()
    keep.wait()


class RowGather:
    def __init__(self, buf, send, recv):
        ctx, row, core = place()
        tp = row * 2 + core
        along, beside = {"tp": (tp + 2) % 4}, {"tp": row * 2 + 1 - core}
        other = (1 - row) * 2 + core
        self.to_y = remote(0, buf.at[tp], buf.at[tp], send, recv, **along)
        self.to_core = remote(1, buf.at[tp], buf.at[tp], send, recv, **beside)
        self.passed = remote(2, buf.at[other], buf.at[other], send, recv, **beside)

    def start(self):
        self.to_y.start()
        self.to_core.start()

    def relay(self):
        self.to_y.wait_recv()
        self.passed.start()

    def finish(self):
        for copy in (self.to_y, self.to_core, self.passed):
            copy.wait_send()


def attention_backward_kernel(ways, has_sums, swaps, *refs):
    extra_in, extra_out = int(has_sums) + swaps, int(has_sums) + int(swaps > 0)
    extra_scratch = 4 * int(has_sums) + int(swaps > 0)
    ins, ex_in, outs, ex_out, scratch, ex_scratch, sems = split_refs(
        refs, 11, extra_in, 3, extra_out, 18, extra_scratch, 3
    )
    grad_ref, hidden_ref, branch_ref, mods_ref = ins[:4]
    grad_out, small_out, dw_hbm = outs
    weights, normed, q, k, v, lse, mixed = scratch[:7]
    gathered, dmixed, dqh, dq, dkv, dk, dw, part, beside_in, summed, turn_in = scratch[7:]
    local, send, recv = sems
    rows, model = grad_ref.shape
    heads = q.shape[0]
    cut = heads * HEAD_DIM
    loads = [
        pltpu.make_async_copy(src, dst, local.at[number])
        for number, (src, dst) in enumerate(zip(ins[4:], scratch[:7]))
    ]
    for copy in loads:
        copy.start()
    sums_src, swap_src, ex = take_extra(has_sums, swaps, ex_in, ex_out, ex_scratch)
    extra = Extra(
        ways, sums_src, swap_src, ex, local, 8, send, recv, PAIR_COPIES + SCATTER_COPIES
    )
    extra.begin()
    ctx, row, core = place()
    grad = grad_ref[...]
    gathered[row * 2 + core] = (mods_ref[2:3, :] * grad).astype(BF)
    gather = RowGather(gathered, send, recv)
    scatter = GroupScatter(part, beside_in, summed, turn_in, send, recv, PAIR_COPIES)
    gather.start()
    extra.start()
    extra.start_swap()
    small_out[2:3, :] = jnp.sum(grad * branch_ref[...], 0, keepdims=True)
    for copy in loads:
        copy.wait()

    def attend(name, first):
        b = scatter.chips[name][1]
        span = pl.ds(pl.multiple_of(b * 2 * rows, 2 * rows), 2 * rows)
        here = gathered[pl.ds(b * 2, 2)].reshape(2 * rows, model)
        out = dot(here, weights[:, cut : 2 * cut]).astype(BF)
        for head in range(heads):
            dmixed[head, span] = out[:, head * HEAD_DIM : (head + 1) * HEAD_DIM]

        @pl.loop(0, heads)
        def _(head):
            query, upper = q[head, span], dmixed[head, span]
            scores = dot_wide(k[head], query)
            top = jnp.concatenate(
                [lse[head, pl.ds(b * 2, 1)], lse[head, pl.ds(b * 2 + 1, 1)]], 1
            )
            weight = jnp.exp(scores - top)
            grad_prob = dot_wide(v[head], upper)
            inner = jnp.sum(weight * grad_prob, 0, keepdims=True)
            grad_score = (weight * (grad_prob - inner)).astype(BF)
            grad_value = dot(weight.astype(BF), upper)
            grad_key = dot(grad_score, query)
            grad_query = dot_tall(grad_score, k[head])
            dqh[head, span] = (grad_query * SCORE_SCALE).astype(BF)
            if first:
                dk[head] = grad_key
                dk[heads + head] = grad_value
            else:
                dk[head] = dk[head] + grad_key
                dk[heads + head] = dk[heads + head] + grad_value

    gather.to_core.wait_recv()
    attend("own", True)
    gather.relay()
    extra.step(2)
    gather.passed.wait_recv()
    attend("y", False)
    for head in range(heads):
        dq[:, head * HEAD_DIM : (head + 1) * HEAD_DIM] = dqh[head]
    for head in range(2 * heads):
        dkv[:, head * HEAD_DIM : (head + 1) * HEAD_DIM] = dk[head].astype(BF)
    for step in range(3, ways):
        extra.step(step)

    def span_of(name):
        a, b = scatter.chips[name]
        return pl.ds(pl.multiple_of(square(a, b, 0) * rows, 2 * rows), 2 * rows)

    def down(name):
        a, b = scatter.chips[name]
        out = dot_wide(dkv[span_of(name), :], weights[:, 2 * cut :])
        if name in ("own", "y"):
            span = pl.ds(pl.multiple_of(b * 2 * rows, 2 * rows), 2 * rows)
            out = out + dot_wide(dq[span, :], weights[:, :cut])
        part[pl.ds(square(a, b, 0), 2)] = out.astype(BF).reshape(2, rows, model)

    down("far")
    scatter.send_pair("far")
    down("x")
    scatter.send_pair("x")
    scatter.add_pair("far")
    down("y")
    scatter.send_pair("y")
    scatter.add_pair("x")
    down("own")
    scatter.send_pair("own")
    scatter.add_pair("y")
    scatter.add_pair("own")
    tile = 256

    def out_rows(at):
        return pl.ds(pl.multiple_of(at * tile, tile), tile)

    @pl.loop(0, model // tile)
    def _(at):
        lanes = out_rows(at)
        all_rows = normed[:, :, lanes].reshape(8 * rows, tile)
        dw[out_rows(at), 2 * cut :] = dot_tall(all_rows, dkv[...]).astype(BF)

    scatter.turn_corner()

    @pl.loop(0, model // tile)
    def _(at):
        lanes = out_rows(at)
        mine = normed[pl.ds(ctx * 4, 4), :, lanes].reshape(4 * rows, tile)
        dw[out_rows(at), :cut] = dot_tall(mine, dq[...]).astype(BF)
        upper = gathered[:, :, lanes].reshape(4 * rows, tile)
        dw[out_rows(at), cut : 2 * cut] = dot_tall(upper, mixed[...]).astype(BF)

    keep = pltpu.make_async_copy(dw, dw_hbm, local.at[7])
    keep.start()
    grad_out[...] = grad
    modulate_backward(scatter.total(), hidden_ref[...], mods_ref[1:2, :], grad_out, small_out)
    gather.finish()
    scatter.finish()
    extra.finish()
    keep.wait()


def layer_backward_kernel(ways, prior, *refs):
    hop, before = int(ways > 1), int(ways > 1 and prior)
    (
        (grad, mods),
        feed_in,
        attention_in,
        prior_grads,
        prior_shard,
        (grad_out, small_feed, small_attention, dw_feed, dw_attention),
        shard_before,
        shard_feed,
        swap_out,
        (middle,),
        feed_scratch,
        feed_extra,
        feed_sems,
        scratch,
        hops,
        swap_buf,
        sems,
    ) = split_refs(
        refs, 2, 5, 9, before, before, 5, before, hop, before, 1, 11, 4 * before, 3, 18, 3 * hop,
        before, 3,
    )
    hidden, branch, *rest = feed_in
    feed_backward_kernel(
        ways,
        ways,
        before == 1,
        0,
        grad,
        hidden,
        branch,
        mods,
        *rest,
        *prior_grads,
        middle,
        small_feed,
        dw_feed,
        *shard_before,
        *feed_scratch,
        *feed_extra,
        *feed_sems,
    )
    hidden, branch, *rest = attention_in
    dw = feed_scratch[6]
    sources = ((dw,) if hop else ()) + tuple(prior_shard) + tuple(shard_before)
    attention_backward_kernel(
        ways,
        hop == 1,
        2 * before,
        middle,
        hidden,
        branch,
        mods,
        *rest,
        *sources,
        grad_out,
        small_attention,
        dw_attention,
        *shard_feed,
        *swap_out,
        *scratch,
        *((dw,) if hop else ()),
        *hops,
        *swap_buf,
        *sems,
    )


def layer_backward(grad, mods, blocks, kept_attention, kept_feed, prior, number):
    rows, model = grad.shape
    attention_weights, feed_weights = blocks
    shape = attention_weights.shape
    cut, width = shape[1] // 4, shape[1] // 2
    heads = cut // HEAD_DIM
    ways = lax.axis_size("shard")
    if ways > HOP_WAYS:
        ways = 1
    hop, before = ways > 1, prior is not None
    shard = (shape[0] // ways, shape[1])
    hidden, normed, pre, branch = kept_feed
    feed_in = [hidden, branch, feed_weights, normed, pre]
    hidden, branch, *saved = kept_attention
    attention_in = [hidden, branch, attention_weights, *saved]
    outs = [sds((rows, model), F32), sds((3, model), F32), sds((3, model), F32)]
    outs += [sds(shape, BF)] * 2
    specs = [VMEM, VMEM, VMEM, ANY, ANY]
    outs += [sds(shard, BF)] * (before + hop) + [sds((2, *shard), BF)] * before
    specs += [VMEM] * (before + hop) + [ANY] * before
    hops = pltpu.VMEM((line_copies(ways), *shard), BF)
    line = [hops, hops, pltpu.VMEM(shard, F32)]

    def buffers(copies, locals_used):
        return [
            pltpu.SemaphoreType.DMA((locals_used,)),
            pltpu.SemaphoreType.DMA((copies,)),
            pltpu.SemaphoreType.DMA((copies,)),
        ]

    group = [
        pltpu.VMEM((8, rows, model), BF),
        pltpu.VMEM((4, rows, model), BF),
        pltpu.VMEM((4, rows, model), BF),
        pltpu.VMEM((6, rows // 2, model), BF),
    ]
    scratch = [pltpu.VMEM((rows, model), F32)]
    scratch += [
        pltpu.VMEM(shape, BF),
        pltpu.VMEM((8, rows, model), BF),
        pltpu.VMEM((8, rows, model), BF),
        pltpu.VMEM((8, rows, width), F32),
        pltpu.VMEM((8 * rows, width), BF),
        pltpu.VMEM((8 * rows, width), BF),
        pltpu.VMEM(shape, BF),
    ] + group
    if before:
        scratch += [pltpu.VMEM(shape, BF)] + line
    scratch += buffers(GATHER_COPIES + SCATTER_COPIES + line_copies(ways), 6)
    scratch += [pltpu.VMEM(leaf.shape, leaf.dtype) for leaf in [attention_weights, *saved]]
    scratch += [
        pltpu.VMEM((4, rows, model), BF),
        pltpu.VMEM((heads, 4 * rows, HEAD_DIM), BF),
        pltpu.VMEM((heads, 4 * rows, HEAD_DIM), BF),
        pltpu.VMEM((4 * rows, cut), BF),
        pltpu.VMEM((8 * rows, 2 * cut), BF),
        pltpu.VMEM((2 * heads, 8 * rows, HEAD_DIM), F32),
        pltpu.VMEM(shape, BF),
    ] + group
    if hop:
        scratch += line
    if before:
        scratch.append(pltpu.VMEM((2, *shard), BF))
    scratch += buffers(PAIR_COPIES + SCATTER_COPIES + line_copies(ways) + 2, 10)
    result = pl.pallas_call(
        functools.partial(layer_backward_kernel, ways, before),
        out_shape=outs,
        in_specs=[VMEM] * 4 + [ANY] * 3 + [VMEM] * 2 + [ANY] * (7 + 2 * before),
        out_specs=specs,
        scratch_shapes=scratch,
        compiler_params=pltpu.CompilerParams(collective_id=number, has_side_effects=True),
        name="layer_backward",
    )(grad, mods, *feed_in, *attention_in, *(prior if before else ()))
    grad, small_feed, small_attention, dw_feed, dw_attention, *rest = result
    shard_before = rest.pop(0) if before else None
    shard_feed = rest.pop(0) if hop else None
    swapped = rest.pop(0) if before else None
    return grad, small_feed, small_attention, dw_feed, dw_attention, shard_before, shard_feed, swapped


def exchange_kernel(ways, modes, pieces, by_tp, by_x, has_block, has_sums, swaps, *refs):
    count = len(modes)
    stacked = [number for number in range(count) if pieces[number] > 1]
    extra_in, extra_out = int(has_sums) + swaps, int(has_sums) + int(swaps > 0)
    extra_scratch = 4 * int(has_sums) + int(swaps > 0)
    block = int(has_block)
    parts, block_in, ex_in, outs, block_out, ex_out, scratch, stack_buf, block_buf, ex_scratch, sems = (
        split_refs(
            refs,
            sum(pieces),
            block,
            extra_in,
            count,
            block,
            extra_out,
            3 * count,
            len(stacked),
            block,
            extra_scratch,
            3,
        )
    )
    held, arrived, far = scratch[:count], scratch[count : 2 * count], scratch[2 * count :]
    local, send, recv = sems
    sums_src, swap_src, ex = take_extra(has_sums, swaps, ex_in, ex_out, ex_scratch)
    stages = 2 * int(by_tp) + int(by_x)
    used = count * (stages + ways - 1)
    extra = Extra(ways, sums_src, swap_src, ex, local, 1, send, recv, used)
    if has_sums:
        used += line_copies(ways)
    used += swaps
    extra.begin()
    ctx, row, core = place()
    tp = row * 2 + core
    at = lax.axis_index("shard")
    barrier = pltpu.get_barrier_semaphore()
    sides = [{"tp": row * 2 + 1 - core}, {"tp": (tp + 2) % 4}] if by_tp else []
    if by_x:
        sides.append({"ctx": 1 - ctx})
    greeted = sides if by_x or not swaps else sides + [{"ctx": 1 - ctx}]
    for where in greeted:
        pl.semaphore_signal(barrier, inc=1, device_id=where, device_id_type=MESH)
    for away in range(1, ways):
        pl.semaphore_signal(
            barrier, inc=1, device_id={"shard": (at + away) % ways}, device_id_type=MESH
        )
    pl.semaphore_wait(barrier, len(greeted) + ways - 1)
    copies = []
    now, taken = [], 0
    for number in range(count):
        given = parts[taken : taken + pieces[number]]
        taken += pieces[number]
        if number in stacked:
            into, first = stack_buf[stacked.index(number)], 0
            for ref in given:
                into[first : first + ref.shape[0]] = ref[...]
                first += ref.shape[0]
            given = [into]
        now.append(given[0])
    for stage, where in enumerate(sides):
        here = []
        for number in range(count):
            here.append(
                remote(
                    number * stages + stage,
                    now[number],
                    arrived[number].at[stage],
                    send,
                    recv,
                    **where,
                )
            )
            here[-1].start()
        if stage == 0:
            if has_block:
                line = LineGather(
                    ways, block_in[0], block_buf[0], local.at[0], send, recv, used
                )
                line.start()
            extra.start()
            extra.start_swap()
        for number in range(count):
            here[number].wait_recv()
            both = now[number][...].astype(F32) + arrived[number][stage].astype(F32)
            held[number][stage] = both.astype(held[number].dtype)
            now[number] = held[number].at[stage]
        copies += here
    if has_block:
        line.step(2)
    base = count * stages
    for number, mode in enumerate(modes):
        if mode == "gather":
            far[number][at] = now[number][...].astype(far[number].dtype)
            now[number] = far[number].at[at]
    waits = []
    for number, mode in enumerate(modes):
        for away in range(1, ways):
            to = (at + away) % ways
            copy = remote(
                base + number * (ways - 1) + away - 1,
                now[number].at[to] if mode == "scatter" else now[number],
                far[number].at[at],
                send,
                recv,
                shard=to,
            )
            copy.start()
            waits.append(copy)
        if mode != "gather":
            far[number][at] = now[number][at] if mode == "scatter" else now[number][...]
    extra.step(2)
    for k in range(3, ways):
        if has_block:
            line.step(k)
        extra.step(k)
    for copy in waits:
        copy.wait_recv()
    for number, mode in enumerate(modes):
        if mode == "gather":
            outs[number][...] = far[number][...].astype(F32)
            continue
        total = far[number][0].astype(F32)
        for index in range(1, ways):
            total = total + far[number][index].astype(F32)
        outs[number][...] = total
    for copy in copies + waits:
        copy.wait_send()
    extra.finish()
    if has_block:
        line.finish()
        keep = pltpu.make_async_copy(block_buf[0], block_out[0], local.at[0])
        keep.start()
        keep.wait()


def stacked_shape(arrays):
    return (sum(array.shape[0] for array in arrays), *arrays[0].shape[1:])


def exchange(parts, number, by_tp=True, by_x=False, block=None, grads=None, swaps=()):
    ways = lax.axis_size("shard")
    if ways > HOP_WAYS:
        return exchange_plain(parts, by_tp, by_x)
    stages = 2 * int(by_tp) + int(by_x)
    modes, pieces = [mode for _, mode in parts], [len(arrays) for arrays, _ in parts]
    outs, held, arrived, far, stacks, given = [], [], [], [], [], []
    for arrays, mode in parts:
        whole, dtype = stacked_shape(arrays), arrays[0].dtype
        one = whole[1:] if mode == "scatter" else whole
        full = (ways, *one)
        given += list(arrays)
        outs.append(sds(full if mode == "gather" else one, F32))
        held.append(pltpu.VMEM((max(stages, 1), *whole), dtype))
        arrived.append(pltpu.VMEM((max(stages, 1), *whole), dtype))
        far.append(pltpu.VMEM(full, BF if mode == "gather" else dtype))
        if len(arrays) > 1:
            stacks.append(pltpu.VMEM(whole, dtype))
    specs = [VMEM] * len(outs)
    block_specs, block_scratch, inputs = [], [], len(given)
    copies = len(parts) * (stages + ways - 1)
    if block is not None:
        shape = (ways * block.shape[0], block.shape[1])
        given.append(block)
        block_specs.append(ANY)
        block_scratch.append(pltpu.VMEM(shape, BF))
        outs.append(sds(shape, BF))
        copies += line_copies(ways)
    more, more_outs, more_specs, more_scratch, more_copies = extra_shapes(ways, grads, swaps)
    copies += more_copies
    return pl.pallas_call(
        functools.partial(
            exchange_kernel,
            ways,
            tuple(modes),
            tuple(pieces),
            by_tp,
            by_x,
            block is not None,
            grads is not None,
            len(swaps),
        ),
        out_shape=outs + more_outs,
        in_specs=[VMEM] * inputs + block_specs + [ANY] * len(more),
        out_specs=specs + block_specs + more_specs,
        scratch_shapes=held
        + arrived
        + far
        + stacks
        + block_scratch
        + more_scratch
        + [
            pltpu.SemaphoreType.DMA((3,)),
            pltpu.SemaphoreType.DMA((copies,)),
            pltpu.SemaphoreType.DMA((copies,)),
        ],
        compiler_params=pltpu.CompilerParams(collective_id=number, has_side_effects=True),
        name="exchange",
    )(*given, *more)


def exchange_plain(parts, by_tp, by_x):
    near = (("ctx",) if by_x else ()) + (("tp",) if by_tp else ())
    outs = []
    for arrays, mode in parts:
        wide = jnp.concatenate(arrays, 0).astype(F32)
        if mode == "gather":
            outs.append(lax.all_gather(lax.psum(wide, near), "shard", axis=0))
        elif mode == "scatter":
            total = lax.psum_scatter(wide, "shard", scatter_dimension=0, tiled=True)
            outs.append(lax.psum(total, near)[0])
        else:
            outs.append(lax.psum(wide, ("shard",) + near))
    return outs


def spread(values, at, axis_size):
    full = jnp.zeros((*values.shape[:-1], axis_size), values.dtype)
    return lax.dynamic_update_slice_in_dim(full, values, at, values.ndim - 1)


def silu_grad(values):
    gate = jax.nn.sigmoid(values)
    return gate * (1.0 + values * (1.0 - gate))


def local(
    noised,
    velocity,
    labels,
    time_ids,
    stem,
    stem_mean,
    stem_square,
    modulation,
    modulation_mean,
    modulation_square,
    attention_in,
    attention_in_mean,
    attention_in_square,
    attention_out,
    attention_out_mean,
    attention_out_square,
    feedforward,
    feedforward_mean,
    feedforward_square,
):
    tensor_ways = lax.axis_size("tp")
    shard_ways = lax.axis_size("shard")
    own_latent = lax.axis_index("shard")
    own_ctx = lax.axis_index("ctx")
    own_tp = lax.axis_index("tp")
    owned = stem.shape[1]
    first_owned = (own_latent * tensor_ways + lax.axis_index("tp")) * owned

    def own_columns(values):
        return lax.dynamic_slice_in_dim(values, first_owned, owned, values.ndim - 1)

    stem_low = stem.astype(jnp.bfloat16)
    class_own, time_in_own, time_out_own, shift_own, scale_own, patch_own, head_own = split_stem(
        stem_low
    )
    modulation_low = modulation.astype(jnp.bfloat16)
    mine = (jnp.arange(shard_ways) == own_latent).astype(jnp.float32)[:, None]
    packed_ids = mine * jnp.concatenate([labels, time_ids]).astype(jnp.float32)[None, :]
    ids_wide = jnp.pad(packed_ids, ((0, 0), (0, 126)))
    (ids_all,) = exchange([([ids_wide], "sum")], 10, by_tp=False)
    all_labels, all_times = ids_all[:, 0].astype(jnp.int32), ids_all[:, 1].astype(jnp.int32)
    latents = all_labels.shape[0]
    features = time_features(all_times).astype(jnp.bfloat16)
    time_pre = jnp.dot(features, time_in_own, preferred_element_type=jnp.float32)
    time_hidden_own = jax.nn.silu(time_pre).astype(jnp.bfloat16)
    hidden_half = feedforward.shape[3] // lax.axis_size("ctx")
    feed_low = lax.dynamic_slice_in_dim(feedforward, own_ctx * hidden_half, hidden_half, 3).astype(
        jnp.bfloat16
    )
    in_low, out_low = attention_in.astype(jnp.bfloat16), attention_out.astype(jnp.bfloat16)
    hops = shard_ways <= HOP_WAYS
    own_blocks, blocks = [], []
    for layer_at in range(LAYERS):
        parts = [in_low[layer_at, 0], out_low[layer_at], in_low[layer_at, 1], in_low[layer_at, 2]]
        own_blocks.append(jnp.concatenate(parts, 1))
        own_blocks.append(jnp.concatenate([feed_low[layer_at, 0], feed_low[layer_at, 1]], 1))
    to_send = jnp.concatenate([time_hidden_own, patch_own, head_own], 0)
    half_rows = own_blocks[0].shape[0] // 2
    exchanged = exchange(
        [([spread(to_send, first_owned, D)], "sum")], 11, block=own_blocks[0][:half_rows]
    )
    packed = exchanged[0].astype(jnp.bfloat16)
    time_hidden = packed[:latents]
    patch_in, head_rows = packed[latents : latents + PDIM], packed[latents + PDIM :]
    onehot = (all_labels[:, None] == jnp.arange(CLASSES)[None, :]).astype(jnp.bfloat16)
    condition = jnp.dot(time_hidden, time_out_own, preferred_element_type=jnp.float32) + jnp.dot(
        onehot, class_own, preferred_element_type=jnp.float32
    )
    gated_own = jax.nn.silu(condition).astype(jnp.bfloat16)
    mod_part = jnp.einsum(
        "bd,lde->ble", gated_own, modulation_low, preferred_element_type=jnp.float32
    )
    first_half = exchanged[1:]
    mod_part = mod_part.reshape(latents, LAYERS * 6, D)
    exchanged = exchange(
        [([mod_part], "scatter"), ([spread(gated_own, first_owned, D)], "sum")],
        12,
        block=own_blocks[0][half_rows:],
    )
    layer_mods = exchanged[0].reshape(LAYERS, 6, D)
    gated = exchanged[1].astype(jnp.bfloat16)
    if hops:
        both = [part.reshape(shard_ways, half_rows, -1) for part in (first_half[0], exchanged[2])]
        blocks.append(jnp.concatenate(both, 1).reshape(shard_ways * 2 * half_rows, -1))
    else:
        for block in own_blocks:
            blocks.append(lax.all_gather(block, "shard", axis=0, tiled=True))
    end_own = jnp.stack(
        [
            jnp.dot(gated, shift_own, preferred_element_type=jnp.float32),
            jnp.dot(gated, scale_own, preferred_element_type=jnp.float32),
        ],
        1,
    )
    (end_mods,) = exchange([([spread(end_own, first_owned, D)], "scatter")], 13)
    end_shift, end_scale = end_mods[0:1], end_mods[1:2]

    pieces = patchify(noised)[0]
    rows_here = noised.shape[2] // PATCH
    first_row = (own_ctx * tensor_ways + lax.axis_index("tp")) * rows_here
    embedded = jnp.dot(pieces, patch_in, preferred_element_type=jnp.float32)
    hidden = embedded + positions(first_row, rows_here, noised.shape[3] // PATCH, D)
    saved, weights = [], blocks[0]
    for layer_at in range(LAYERS):
        final = layer_at + 1 == LAYERS
        feed_own, ahead, feed_weights = None, None, None
        if hops:
            feed_own = own_blocks[2 * layer_at + 1]
            ahead = None if final else own_blocks[2 * layer_at + 2]
        else:
            weights, feed_weights = blocks[2 * layer_at : 2 * layer_at + 2]
        hidden, kept_attention, kept_feed, feed_weights, following = layer_forward(
            hidden, layer_mods[layer_at], weights, feed_weights, feed_own, ahead, 2 + int(final)
        )
        saved.append((kept_attention, kept_feed, (weights, feed_weights)))
        weights = following

    final_normed = modulate(hidden, end_shift, end_scale).astype(jnp.bfloat16)
    predicted = jnp.einsum(
        "pd,cd->pc", final_normed, head_rows, preferred_element_type=jnp.float32
    )
    target_rows = patchify(velocity)[0].astype(jnp.float32)
    weighting = 0.5 + time_ids.astype(jnp.float32)[0] / STEPS
    misfit = predicted - target_rows
    loss_scale = 1.0 / (shard_ways * PATCHES * PDIM)
    loss_local = jnp.sum(weighting * misfit * misfit) * loss_scale
    grad_pred = (2.0 * loss_scale * weighting * misfit).astype(jnp.bfloat16)
    grad_head = jnp.einsum("pc,pd->cd", grad_pred, final_normed, preferred_element_type=jnp.float32)
    grad_normed = jnp.dot(grad_pred, head_rows, preferred_element_type=jnp.float32)
    grad_hidden, grad_end_shift, grad_end_scale = jax.vjp(modulate, hidden, end_shift, end_scale)[
        1
    ](grad_normed)

    small = [None] * (2 * LAYERS)
    shards, others = [None] * (2 * LAYERS), [None] * (2 * LAYERS)
    prior = None
    for layer_at in reversed(range(LAYERS)):
        kept_attention, kept_feed, pair = saved[layer_at]
        one, two = 2 * layer_at, 2 * layer_at + 1
        (
            grad_hidden,
            small[two],
            small[one],
            feed_grads,
            grads,
            shard_before,
            shards[two],
            swapped,
        ) = layer_backward(
            grad_hidden,
            layer_mods[layer_at],
            pair,
            kept_attention,
            kept_feed,
            prior,
            5 + int(prior is None),
        )
        if prior is not None:
            shards[one + 2] = shard_before
            others[two + 2], others[one + 2] = swapped[0], swapped[1]
        if hops:
            prior = (grads, shards[two])
        else:
            for half, local_grads in ((one, grads), (two, feed_grads)):
                shards[half] = lax.psum_scatter(
                    local_grads, "shard", scatter_dimension=0, tiled=True
                )
                others[half] = lax.ppermute(shards[half], "ctx", [(0, 1), (1, 0)])
    grad_embed = grad_hidden.astype(jnp.bfloat16)
    grad_patch = jnp.einsum("pf,pd->fd", pieces, grad_embed, preferred_element_type=jnp.float32)

    pixel = jnp.concatenate([grad_patch, grad_head], 0).astype(jnp.bfloat16)
    pixel = pixel.reshape(2 * PDIM, shard_ways, -1).transpose(1, 0, 2)
    result = exchange(
        [(small + [grad_end_shift, grad_end_scale], "gather"), ([pixel], "scatter")],
        14,
        by_x=True,
        grads=grads,
        swaps=[shards[1]],
    )
    small, pixel = result[0], result[1]
    if hops:
        shards[0], others[1] = result[2], result[3][0]
    grad_mod = small[:, : 6 * LAYERS].reshape(latents, LAYERS, 6 * D)
    grad_ends = small[:, 6 * LAYERS :]
    ends_here = own_columns(grad_ends)
    gated_part = jnp.dot(
        ends_here[:, 0], shift_own.astype(jnp.float32).T, precision=highest
    ) + jnp.dot(ends_here[:, 1], scale_own.astype(jnp.float32).T, precision=highest)
    result = exchange([([gated_part], "sum")], 15, swaps=[shards[0]])
    if hops:
        others[0] = result[1][0]
    grad_gated = own_columns(result[0]) + jnp.einsum(
        "ble,lde->bd", grad_mod, modulation_low.astype(jnp.float32), precision=highest
    )
    grad_condition = grad_gated * silu_grad(condition)
    time_part = jnp.dot(grad_condition, time_out_own.astype(jnp.float32).T, precision=highest)
    (grad_time_hidden,) = exchange([([time_part], "sum")], 16)
    grad_time_hidden = own_columns(grad_time_hidden)
    grad_time_pre = grad_time_hidden * silu_grad(time_pre)
    gated_wide = gated.astype(jnp.float32)
    grad_ends_own = lax.dynamic_slice_in_dim(pixel, own_tp * owned, owned, 1)
    shard_stem = jnp.concatenate(
        [
            jnp.dot(onehot.astype(jnp.float32).T, grad_condition, precision=highest),
            jnp.dot(features.astype(jnp.float32).T, grad_time_pre, precision=highest),
            jnp.dot(time_hidden.astype(jnp.float32).T, grad_condition, precision=highest),
            jnp.dot(gated_wide.T, ends_here[:, 0], precision=highest),
            jnp.dot(gated_wide.T, ends_here[:, 1], precision=highest),
            grad_ends_own,
        ],
        0,
    )
    shard_modulation = jnp.einsum(
        "bd,ble->lde", gated_own.astype(jnp.float32), grad_mod, precision=highest
    )
    cut = attention_in.shape[3]
    shard_in, shard_out, shard_hidden = [], [], []
    for layer_at in range(LAYERS):
        own, other = shards[2 * layer_at], others[2 * layer_at]
        both = own.astype(jnp.float32) + other.astype(jnp.float32)
        shard_out.append(both[:, cut : 2 * cut])
        shard_in.append(
            jnp.stack([both[:, number * cut : (number + 1) * cut] for number in (0, 2, 3)])
        )
        own, other = shards[2 * layer_at + 1], others[2 * layer_at + 1]
        low, high = jnp.where(own_ctx == 0, own, other), jnp.where(own_ctx == 0, other, own)
        shard_hidden.append(
            jnp.stack(
                [
                    jnp.concatenate([low[:, :hidden_half], high[:, :hidden_half]], 1),
                    jnp.concatenate([low[:, hidden_half:], high[:, hidden_half:]], 1),
                ]
            )
        )
    shard_in, shard_out = jnp.stack(shard_in), jnp.stack(shard_out)
    shard_hidden = jnp.stack(shard_hidden).astype(jnp.float32)
    squares = (
        jnp.sum(shard_stem * shard_stem)
        + jnp.sum(shard_modulation * shard_modulation)
        + jnp.sum(shard_in * shard_in)
        + jnp.sum(shard_out * shard_out)
        + jnp.sum(shard_hidden * shard_hidden)
    )
    squares = jnp.where(own_ctx == 0, squares, jnp.zeros((), jnp.float32))
    sums = jnp.stack([squares, loss_local])[:, None] * jnp.ones((1, 128), jnp.float32)
    (sums,) = exchange([([sums], "sum")], 17, by_x=True)
    square_total, train_loss = sums[0, 0], sums[1, 0]
    total_norm = jnp.sqrt(square_total)
    factor = clip_level / jnp.maximum(total_norm, clip_level)
    stem_out = adam_update(stem, stem_mean, stem_square, shard_stem, factor)
    mod_out = adam_update(modulation, modulation_mean, modulation_square, shard_modulation, factor)
    in_out = adam_update(attention_in, attention_in_mean, attention_in_square, shard_in, factor)
    proj_out = adam_update(
        attention_out, attention_out_mean, attention_out_square, shard_out, factor
    )
    feed_out = adam_update(feedforward, feedforward_mean, feedforward_square, shard_hidden, factor)
    return (
        train_loss,
        total_norm,
        stem_out[0],
        stem_out[1],
        stem_out[2],
        stem_out[3],
        mod_out[0],
        mod_out[1],
        mod_out[2],
        mod_out[3],
        in_out[0],
        in_out[1],
        in_out[2],
        in_out[3],
        proj_out[0],
        proj_out[1],
        proj_out[2],
        proj_out[3],
        feed_out[0],
        feed_out[1],
        feed_out[2],
        feed_out[3],
    )


def solution(mesh):
    placed = (
        P("shard", None, ("ctx", "tp"), None),
        P("shard", None, ("ctx", "tp"), None),
        P("shard"),
        P("shard"),
        P(None, ("shard", "tp")),
        P(None, ("shard", "tp")),
        P(None, ("shard", "tp")),
        P(None, ("shard", "tp"), None),
        P(None, ("shard", "tp"), None),
        P(None, ("shard", "tp"), None),
        P(None, None, "shard", "tp"),
        P(None, None, "shard", "tp"),
        P(None, None, "shard", "tp"),
        P(None, "shard", "tp"),
        P(None, "shard", "tp"),
        P(None, "shard", "tp"),
        P(None, None, "shard", "tp"),
        P(None, None, "shard", "tp"),
        P(None, None, "shard", "tp"),
    )
    return jax.shard_map(
        local,
        mesh=mesh,
        in_specs=placed,
        out_specs=(
            P(),
            P(),
            P(None, ("shard", "tp")),
            P(None, ("shard", "tp")),
            P(None, ("shard", "tp")),
            P(None, ("shard", "tp")),
            P(None, ("shard", "tp"), None),
            P(None, ("shard", "tp"), None),
            P(None, ("shard", "tp"), None),
            P(None, ("shard", "tp"), None),
            P(None, None, "shard", "tp"),
            P(None, None, "shard", "tp"),
            P(None, None, "shard", "tp"),
            P(None, None, "shard", "tp"),
            P(None, "shard", "tp"),
            P(None, "shard", "tp"),
            P(None, "shard", "tp"),
            P(None, "shard", "tp"),
            P(None, None, "shard", "tp"),
            P(None, None, "shard", "tp"),
            P(None, None, "shard", "tp"),
            P(None, None, "shard", "tp"),
        ),
        check_vma=False,
    )
```

time: 2190 us -> 739 us (0.34)
  waiting for transfers between devices: 1550 us -> 0 us
  Pallas kernels: 0 us -> 593 us
  blocking collectives: 174 us -> 0 us
  matrix products: 170 us -> 32.7 us
  local copies, waits for them, and re-layouts: 137 us -> 40.4 us
  other arithmetic: 112 us -> 56.6 us
    unnamed x79 -> x0, waiting for transfers between devices: 823 us -> none
    all_gather x21 -> x0, waiting for transfers between devices: 594 us -> none  [the longest x12 322 us: gather_group(): return lax.all_gather(values, GROUP, axis=0, tiled=True)]
    pallas_call x0 -> x16, Pallas kernels: none -> 593 us  [the longest x4 228 us: layer_forward(): pl.pallas_call(functools.partial(layer_forward_kernel, ways, last), out_s...]
    dot_general x84 -> x1, matrix products: 140 us -> 1.82 us  [local(): jnp.dot(grad_condition, time_out_own.astype(jnp.float32).T, precision=hig...]
    all_gather x9 -> x0, blocking collectives: 125 us -> none  [the longest x4 35.7 us: attention_backward(): lax.all_gather((gate * grad_hidden).astype(jnp.bfloat16), 'tp', axis=0, t...]
    unnamed x656 -> x144, local copies, waits for them, and re-layouts: 116 us -> 9.24 us
    psum x3 -> x0, waiting for transfers between devices: 80.4 us -> none  [the longest x1 38.6 us: local(): lax.psum(jnp.stack(shard_attention), 'ctx').astype(jnp.float32)]
    reduce_scatter x1 -> x0, waiting for transfers between devices: 56.6 us -> none  [local(): lax.psum_scatter(jnp.concatenate([grad_patch, grad_head], 0), OWNERS, sca...]
  transfers between devices with their start and end apart: 52 -> 0, of which waited for: 51 -> 0; matrix products, arithmetic and copies ran while one was open for 7% -> 0% of each run, Pallas kernels for 0% -> 0%
where the time goes in v2:
time: 739 us; the launch traced here: 732 us
  Pallas kernels  593 us (80%)
  other arithmetic  56.6 us (8%)
  local copies, waits for them, and re-layouts  40.4 us (5%)
  matrix products  32.7 us (4%)
  between operations  9.18 us (1%)
    pallas_call x4, Pallas kernels, layer_forward(): pl.pallas_call(functools.partial(layer_forward_kernel, ways, last), out_s...  228 us
    pallas_call x4, Pallas kernels, layer_backward(): pl.pallas_call(functools.partial(layer_backward_kernel, ways, before), ou...  222 us
    pallas_call x8, Pallas kernels, exchange(): pl.pallas_call(functools.partial(exchange_kernel, ways, tuple(modes), tup...  143 us
    convert_element_type x5, other arithmetic, adam_update(): return (master_new, first_new, second_new, master_new.astype(jnp.bfloat16))  28.8 us

profile of v2, /device:TPU:0, one launch (start us, length us, event | category | flops | bytes accessed | tf_op | source)
XLA Modules:
  0.0 732.0 jit_solution(6791159376502925237)
XLA Ops:
  2.9 8.6 %exchange.8 = f32[4,128]{1,0:T(4,128)} custom-call(f32[4,128]{1,0:T(4,128)} %pad.4.refs_0_), custom_call_target="tpu_custom_call" | custom-call | tf_op jit(solution)/shard_map/exchange/pallas_call | solution.py:1593
  19.7 1.8 dynamic-slice_convert_fusion
  27.1 22.3 %exchange.9 = (f32[36,768]{1,0:T(8,128)}, bf16[384,768]{1,0:T(8,128)(2,1)}) custom-call(bf16[36,768]{1,0:T(8,128)(2,1)} %copy-done.49, bf16[96,768]{1,0:T(8,128)(2,1)} %get-tuple-element.298.refs_1_), custom_call_target="tpu_custom_call" | custom-call | tf_op jit(solution)/shard_map/exchange/pallas_call | solution.py:1593
  50.3 2.0 fusion.4.refs_0_.refs_7_
  56.5 1.8 reshape.173.refs_0_
  58.3 27.0 %exchange.10 = (f32[24,768]{1,0:T(8,128)}, f32[4,768]{1,0:T(4,128)}, bf16[384,768]{1,0:T(8,128)(2,1)}) custom-call(f32[4,24,768]{2,1,0:T(8,128)} %reshape.173.refs_0_, bf16[4,768]{1,0:T(4,128)(2,1)} %copy-done.53, bf16[96,768]{1,0:T(8,128)(2,1)} %get-tuple-element.297.refs_2_), custom_call_target="tpu_custom_call" | custom-call | tf_op jit(solution)/shard_map/exchange/pallas_call | solution.py:1593
  85.3 2.3 pad_maximum_fusion.2
  91.8 11.7 %exchange.11 = f32[2,768]{1,0:T(2,128)} custom-call(f32[4,2,768]{2,1,0:T(2,128)} %dynamic_update_slice.11.refs_0_), custom_call_target="tpu_custom_call" | custom-call | tf_op jit(solution)/shard_map/exchange/pallas_call | solution.py:1593
  105.8 59.3 %layer_forward.4 = (f32[128,768]{1,0:T(8,128)}, f32[128,768]{1,0:T(8,128)}, bf16[8,128,768]{2,1,0:T(8,128)(2,1)}, bf16[3,512,64]{2,1,0:T(8,128)(2,1)}, bf16[3,10...) custom-call(f32[128,768]{1,0:T(8,128)} %fusion.4.refs_0_.refs_7_, ...), custom_call_target="tpu_custom_call" | custom-call | tf_op jit(solution)/shard_map/layer_forward/pallas_call | solution.py:801
  165.2 56.9 %layer_forward.5 = (f32[128,768]{1,0:T(8,128)}, f32[128,768]{1,0:T(8,128)}, bf16[8,128,768]{2,1,0:T(8,128)(2,1)}, bf16[3,512,64]{2,1,0:T(8,128)(2,1)}, bf16[3,10...) custom-call(f32[128,768]{1,0:T(8,128)} %get-tuple-element.118.refs_0, ...), custom_call_target="tpu_custom_call" | custom-call | tf_op jit(solution)/shard_map/layer_forward/pallas_call | solution.py:801
  222.0 59.1 %layer_forward.6 = (f32[128,768]{1,0:T(8,128)}, f32[128,768]{1,0:T(8,128)}, bf16[8,128,768]{2,1,0:T(8,128)(2,1)}, bf16[3,512,64]{2,1,0:T(8,128)(2,1)}, bf16[3,10...) custom-call(f32[128,768]{1,0:T(8,128)} %get-tuple-element.120.refs_0, ...), custom_call_target="tpu_custom_call" | custom-call | tf_op jit(solution)/shard_map/layer_forward/pallas_call | solution.py:801
  281.1 53.1 %layer_forward.7 = (f32[128,768]{1,0:T(8,128)}, f32[128,768]{1,0:T(8,128)}, bf16[8,128,768]{2,1,0:T(8,128)(2,1)}, bf16[3,512,64]{2,1,0:T(8,128)(2,1)}, bf16[3,10...) custom-call(f32[128,768]{1,0:T(8,128)} %get-tuple-element.122.refs_0, ...), custom_call_target="tpu_custom_call" | custom-call | tf_op jit(solution)/shard_map/layer_forward/pallas_call | solution.py:801
  346.8 1.9 multiply_reduce_fusion.4
  352.1 49.6 %layer_backward.4 = (f32[128,768]{1,0:T(8,128)}, f32[3,768]{1,0:T(4,128)}, f32[3,768]{1,0:T(4,128)}, bf16[768,768]{1,0:T(8,128)(2,1)}, bf16[768,768]{1,0:T(8,128)(2,1)}, /*index=5*/bf16[192,768]{1,0:T(8,128)(2,1)}) custom-call(f32[128,768]{1,0:T(8,128)} %broadcast_add_fusion.refs_0_, f32[6,768]{1,0:T(8,128)} %get-tuple-element.299.refs_1_, ...), custom_call_target="tpu_custom_call" | custom-call | tf_op jit(solution)/shard_map/layer_backward/pallas_call | solution.py:1408
  401.6 57.1 %layer_backward.5 = (f32[128,768]{1,0:T(8,128)}, f32[3,768]{1,0:T(4,128)}, f32[3,768]{1,0:T(4,128)}, bf16[768,768]{1,0:T(8,128)(2,1)}, bf16[768,768]{1,0:T(8,128...) custom-call(f32[128,768]{1,0:T(8,128)} %get-tuple-element.138.refs_0_, ...), custom_call_target="tpu_custom_call" | custom-call | tf_op jit(solution)/shard_map/layer_backward/pallas_call | solution.py:1408
  458.7 57.4 %layer_backward.6 = (f32[128,768]{1,0:T(8,128)}, f32[3,768]{1,0:T(4,128)}, f32[3,768]{1,0:T(4,128)}, bf16[768,768]{1,0:T(8,128)(2,1)}, bf16[768,768]{1,0:T(8,128...) custom-call(f32[128,768]{1,0:T(8,128)} %get-tuple-element.153.refs_0_, ...), custom_call_target="tpu_custom_call" | custom-call | tf_op jit(solution)/shard_map/layer_backward/pallas_call | solution.py:1408
  516.2 57.9 %layer_backward.7 = (f32[128,768]{1,0:T(8,128)}, f32[3,768]{1,0:T(4,128)}, f32[3,768]{1,0:T(4,128)}, bf16[768,768]{1,0:T(8,128)(2,1)}, bf16[768,768]{1,0:T(8,128...) custom-call(f32[128,768]{1,0:T(8,128)} %get-tuple-element.168.refs_0_, ...), custom_call_target="tpu_custom_call" | custom-call | tf_op jit(solution)/shard_map/layer_backward/pallas_call | solution.py:1408
  580.0 40.7 %exchange.12 = (f32[4,26,768]{2,1,0:T(8,128)}, f32[32,192]{1,0:T(8,128)}, bf16[192,768]{1,0:T(8,128)(2,1)}, bf16[1,192,768]{2,1,0:T(8,128)(2,1)}) custom-call(f32[3,768]{1,0:T(4,128)} %get-tuple-element.183.refs_0_, f32[3,768]{1,0:T(4,128)} %get-tuple-element.184.refs_1_, f32[3,768]{1,0:T(4,128)} %get-tuple-element.185.refs_2_, ...), custom_call_target="tpu_custom_call" | custom-call | tf_op jit(solution)/shard_map/exchange/pallas_call | solution.py:1593
  629.2 1.8 convolution_add_fusion.refs_0_
  632.9 11.1 %exchange.13 = (f32[4,768]{1,0:T(4,128)}, bf16[1,192,768]{2,1,0:T(8,128)(2,1)}) custom-call(f32[4,768]{1,0:T(4,128)} %convolution_add_fusion.refs_0_, bf16[192,768]{1,0:T(8,128)(2,1)} %get-tuple-element.195.refs_1_), custom_call_target="tpu_custom_call" | custom-call | tf_op jit(solution)/shard_map/exchange/pallas_call | solution.py:1593
  644.1 2.5 fusion.7
  646.6 1.8 fusion.25.refs_0_
  648.4 9.5 %exchange.14 = f32[4,768]{1,0:T(4,128)} custom-call(f32[4,768]{1,0:T(4,128)} %fusion.25.refs_0_), custom_call_target="tpu_custom_call" | custom-call | tf_op jit(solution)/shard_map/exchange/pallas_call | solution.py:1593
  662.2 2.2 concatenate.105
  664.5 2.0 multiply_reduce_fusion.3
  677.3 4.1 multiply_reduce_fusion
  685.4 11.9 %exchange.15 = f32[2,128]{1,0:T(2,128)} custom-call(f32[2,128]{1,0:T(2,128)} %mul.421.refs_0_), custom_call_target="tpu_custom_call" | custom-call | tf_op jit(solution)/shard_map/exchange/pallas_call | solution.py:1593
  699.4 3.7 fusion.67
  703.2 3.9 fusion.61
  707.1 4.9 fusion.63
  712.4 8.6 %fusion.65 = (bf16[4,48,4608]{2,1,0:T(8,128)(2,1)}, f32[4,48,4608]{2,1,0:T(8,128)}, f32[4,48,4608]{2,1,0:T(8,128)}, f32[4,48,4608]{2,1,0:T(8,128)}) fusion(f32[4,48,4608]{2,1,0:T(8,128)S(1)} %copy-done, f32[4,4608,48]{1,2,0:T(8,128)S(1)} %copy-done.1, f32[]{:T(128)S(6)} %div.108, f32[4,48,4608]{2,1,0:T(8,128)S(1)} %copy-done.21, f32[4,48,4608]{2,1,0:T(8,128)} %param.28), kind=kLoop, calls=%fused_computation.216 | loop fusion | flops 14155776 | bytes 26542084 | tf_op jit(solution)/shard_map/convert_element_type | solution.py:100
  723.0 7.7 %fusion.59 = (bf16[4,2,192,768]{3,2,1,0:T(8,128)(2,1)}, f32[4,2,192,768]{3,2,1,0:T(8,128)}, f32[4,2,192,768]{3,2,1,0:T(8,128)}, f32[4,2,192,768]{3,2,1,0:T(8,128)}) fusion(f32[4,2,192,768]{3,2,1,0:T(8,128)S(1)} %bitcast.203, f32[]{:T(128)S(6)} %div.108, bf16[1,2,192,768]{3,2,1,0:T(8,128)(2,1)S(1)} %copy-done.19, bf16[1,2,192,768]{3,2,1,0:T(8,128)(2,1)S(1)} %copy-done.17, ...), kind=kLoop, calls=%fused_computation.213 | loop fusion | flops 23592960 | bytes 33030148 | tf_op jit(solution)/shard_map/convert_element_type | solution.py:100
  (273 shorter events, 76.4 us)
Async XLA Ops:
  0.7 16.7 %copy-start.22 = (f32[4,192,192]{2,1,0:T(8,128)S(1)}, f32[4,192,192]{2,1,0:T(8,128)}, u32[]{:S(2)}) copy-start(f32[4,192,192]{2,1,0:T(8,128)} %param.32) | copy-start | bytes 1769476
  0.7 17.5 %copy-start.24 = (f32[3592,48]{0,1:T(8,128)S(1)}, f32[3592,48]{0,1:T(8,128)}, u32[]{:S(2)}) copy-start(f32[3592,48]{0,1:T(8,128)} %param.23) | copy-start | bytes 2068996
  12.2 41.2 %copy-start.60 = (s32[4]{0:T(128)}, s32[4]{0:T(128)S(1)}, u32[]{:S(2)}) copy-start(s32[4]{0:T(128)S(1)} %convert_reduce_fusion.1) | copy-start | bytes 52
  13.2 5.4 copy-start.62
  13.2 5.4 copy-start.63
  14.8 35.5 %copy-start.51 = (bf16[128,16]{0,1:T(8,128)(2,1)}, bf16[128,16]{0,1:T(8,128)(2,1)S(1)}, u32[]{:S(2)}) copy-start(bf16[128,16]{0,1:T(8,128)(2,1)S(1)} %squeeze_reshape.4) | copy-start | bytes 12292
  24.4 30.9 %copy-start = (f32[4,48,4608]{2,1,0:T(8,128)S(1)}, f32[4,48,4608]{2,1,0:T(8,128)}, u32[]{:S(2)}) copy-start(f32[4,48,4608]{2,1,0:T(8,128)} %param.26) | copy-start | bytes 10616836
  104.3 233.9 %copy-start.50 = (f32[768]{0:T(1024)}, f32[768]{0:T(1024)S(1)}, u32[]{:S(2)}) copy-start(f32[768]{0:T(1024)S(1)} %get-tuple-element.209) | copy-start | bytes 9220
  336.5 5.1 copy-start.58
  516.1 57.9 %copy-start.54 = (f32[768]{0:T(1024)S(1)}, f32[768]{0:T(1024)}, u32[]{:S(2)}) copy-start(f32[768]{0:T(1024)} %get-tuple-element.208) | copy-start | bytes 9220
  516.2 58.5 %copy-start.52 = (bf16[128,16]{0,1:T(8,128)(2,1)S(1)}, bf16[128,16]{0,1:T(8,128)(2,1)}, u32[]{:S(2)}) copy-start(bf16[128,16]{0,1:T(8,128)(2,1)} %copy-done.51) | copy-start | bytes 12292
  632.0 29.2 %copy-start.61 = (s32[4]{0:T(128)S(1)}, s32[4]{0:T(128)}, u32[]{:S(2)}) copy-start(s32[4]{0:T(128)} %copy-done.60) | copy-start | bytes 52
  667.7 5.4 copy-start.28
  667.8 6.2 copy-start.4
  669.2 6.3 copy-start.12
  669.6 4.4 copy-start.6
  671.0 4.5 copy-start.14
  675.5 6.0 copy-start.18
  699.4 7.7 %copy-start.26 = (f32[4,3,192,192]{3,2,1,0:T(8,128)S(1)}, f32[4,3,192,192]{3,2,1,0:T(8,128)}, u32[]{:S(2)}) copy-start(f32[4,3,192,192]{3,2,1,0:T(8,128)} %param.30) | copy-start | bytes 5308420
  699.4 7.7 %copy-start.27 = (f32[4,3,192,192]{3,2,1,0:T(8,128)S(1)}, f32[4,3,192,192]{3,2,1,0:T(8,128)}, u32[]{:S(2)}) copy-start(f32[4,3,192,192]{3,2,1,0:T(8,128)} %param.31) | copy-start | bytes 5308420
  707.1 4.9 copy-start.1
  707.1 5.3 copy-start.21
  712.0 9.0 %slice-start = ((s8[4718592]{0:T(1024)(128)(4,1)}), s8[4194304]{0:T(1024)(128)(4,1)S(1)}, s32[]{:S(2)}) async-start(s8[4718592]{0:T(1024)(128)(4,1)} %bitcast.202), calls=%async_computation | async-start | bytes 8388608
  712.0 9.0 %slice-start.2 = ((s8[4718592]{0:T(1024)(128)(4,1)}), s8[4194304]{0:T(1024)(128)(4,1)S(1)}, s32[]{:S(2)}) async-start(s8[4718592]{0:T(1024)(128)(4,1)} %bitcast.204), calls=%async_computation.2 | async-start | bytes 8388608
  712.0 9.7 %slice-start.4 = ((s8[4718592]{0:T(1024)(128)(4,1)}), s8[4194304]{0:T(1024)(128)(4,1)S(1)}, s32[]{:S(2)}) async-start(s8[4718592]{0:T(1024)(128)(4,1)} %bitcast.206), calls=%async_computation.4 | async-start | bytes 8388608
  712.4 9.6 %slice-start.1 = ((s8[4718592]{0:T(1024)(128)(4,1)}), s8[524288]{0:T(1024)(128)(4,1)S(1)}, s32[]{:S(2)}) async-start(s8[4718592]{0:T(1024)(128)(4,1)} %bitcast.202), calls=%async_computation.1 | async-start | bytes 1048576
  712.4 9.8 %copy-start.13 = (bf16[1,2,192,768]{3,2,1,0:T(8,128)(2,1)S(1)}, bf16[1,2,192,768]{3,2,1,0:T(8,128)(2,1)}, u32[]{:S(2)}) copy-start(bf16[1,2,192,768]{3,2,1,0:T(8,128)(2,1)} %copy-done.12) | copy-start | bytes 1769476
  712.4 10.0 %copy-start.15 = (bf16[1,2,192,768]{3,2,1,0:T(8,128)(2,1)S(1)}, bf16[1,2,192,768]{3,2,1,0:T(8,128)(2,1)}, u32[]{:S(2)}) copy-start(bf16[1,2,192,768]{3,2,1,0:T(8,128)(2,1)} %copy-done.14) | copy-start | bytes 1769476
  712.4 10.1 %copy-start.17 = (bf16[1,2,192,768]{3,2,1,0:T(8,128)(2,1)S(1)}, bf16[1,2,192,768]{3,2,1,0:T(8,128)(2,1)}, u32[]{:S(2)}) copy-start(bf16[1,2,192,768]{3,2,1,0:T(8,128)(2,1)} %copy-done.16) | copy-start | bytes 1769476
  712.4 10.3 %copy-start.19 = (bf16[1,2,192,768]{3,2,1,0:T(8,128)(2,1)S(1)}, bf16[1,2,192,768]{3,2,1,0:T(8,128)(2,1)}, u32[]{:S(2)}) copy-start(bf16[1,2,192,768]{3,2,1,0:T(8,128)(2,1)} %copy-done.18) | copy-start | bytes 1769476
  712.4 10.4 %slice-start.3 = ((s8[4718592]{0:T(1024)(128)(4,1)}), s8[524288]{0:T(1024)(128)(4,1)S(1)}, s32[]{:S(2)}) async-start(s8[4718592]{0:T(1024)(128)(4,1)} %bitcast.204), calls=%async_computation.3 | async-start | bytes 1048576
  712.4 10.6 %slice-start.5 = ((s8[4718592]{0:T(1024)(128)(4,1)}), s8[524288]{0:T(1024)(128)(4,1)S(1)}, s32[]{:S(2)}) async-start(s8[4718592]{0:T(1024)(128)(4,1)} %bitcast.206), calls=%async_computation.5 | async-start | bytes 1048576
  (39 other events, 86.7 us)

commit v3 on v2

--- a/solution.py
+++ b/solution.py
@@ -103,7 +103,7 @@
 GROUP = ("ctx", "tp")
 OWNERS = ("shard", "tp")
 EVERY = ("shard", "ctx", "tp")
-HOP_WAYS = 8
+HOP_WAYS = 4
 
 
 MESH = pl.DeviceIdType.MESH
@@ -143,17 +143,26 @@
     pl.semaphore_signal(
         barrier, inc=1, device_id={"tp": row * 2 + 1 - core}, device_id_type=MESH
     )
-    if shard_ways == 1:
-        return
+    if shard_ways > 1:
+        line_signal(shard_ways)
+
+
+def line_signal(ways):
+    barrier = pltpu.get_barrier_semaphore()
     at = lax.axis_index("shard")
-
-    @pl.when(at > 0)
-    def _():
-        pl.semaphore_signal(barrier, inc=1, device_id={"shard": at - 1}, device_id_type=MESH)
-
-    @pl.when(at < shard_ways - 1)
-    def _():
-        pl.semaphore_signal(barrier, inc=1, device_id={"shard": at + 1}, device_id_type=MESH)
+    for away in (1, 2):
+
+        @pl.when(at >= away)
+        def _():
+            pl.semaphore_signal(
+                barrier, inc=1, device_id={"shard": at - away}, device_id_type=MESH
+            )
+
+        @pl.when(at < ways - away)
+        def _():
+            pl.semaphore_signal(
+                barrier, inc=1, device_id={"shard": at + away}, device_id_type=MESH
+            )
 
 
 def greet_wait(shard_ways):
@@ -162,14 +171,12 @@
         pl.semaphore_wait(barrier, 3)
         return
     at = lax.axis_index("shard")
-
-    @pl.when((at > 0) & (at < shard_ways - 1))
-    def _():
-        pl.semaphore_wait(barrier, 5)
-
-    @pl.when((at == 0) | (at == shard_ways - 1))
-    def _():
-        pl.semaphore_wait(barrier, 4)
+    for own in range(shard_ways):
+        near = min(own, 2) + min(shard_ways - 1 - own, 2)
+
+        @pl.when(at == own)
+        def _():
+            pl.semaphore_wait(barrier, 3 + near)
 
 
 GATHER_COPIES = 13
@@ -359,42 +366,49 @@
         self.own = pltpu.make_async_copy(src, buf.at[pl.ds(at * rows, rows)], local_sem)
 
         def hop(index, block, first, to):
-            target = buf.at[pl.ds(block * rows, rows)]
-            return remote(index, src if first else target, target, send, recv, shard=to)
-
-        def clip(v):
-            return jnp.clip(v, 0, ways - 1)
-
-        steps = ways - 1
-        self.right = [
-            hop(base + k - 1, clip(at - k + 1), k == 1, clip(at + 1)) for k in range(1, ways)
-        ]
-        self.left = [
-            hop(base + steps + k - 1, clip(at + k - 1), k == 1, clip(at - 1))
-            for k in range(1, ways)
-        ]
+            target = buf.at[pl.ds(jnp.clip(block, 0, ways - 1) * rows, rows)]
+            to = jnp.clip(to, 0, ways - 1)
+            return remote(base + index, src if first else target, target, send, recv, shard=to)
+
+        self.direct, self.passed = [], []
+        for side, sign in ((0, 1), (1, -1)):
+            place_at = at if side == 0 else ways - 1 - at
+            for away in (2, 1):
+                if away < ways:
+                    copy = hop(3 * side + away - 1, at, True, at + sign * away)
+                    self.direct.append((copy, place_at < ways - away, place_at >= away))
+            if ways > 3:
+                copy = hop(3 * side + 2, at - 2 * sign, False, at + sign)
+                passes = (place_at >= 2) & (place_at < ways - 1)
+                self.passed.append((copy, passes, place_at >= 3, self.direct[2 * side]))
 
     def start(self):
         self.own.start()
-        self.step(1)
+        for number in (0, 2, 1, 3):
+            if number < len(self.direct):
+                copy, sends, _ = self.direct[number]
+                pl.when(sends)(copy.start)
 
     def step(self, k):
-        at, ways = self.at, self.ways
-        if k > 1:
-            pl.when(at >= k - 1)(self.right[k - 2].wait_recv)
-        pl.when((at < ways - 1) & (at >= k - 1))(self.right[k - 1].start)
-        if k > 1:
-            pl.when(at <= ways - k)(self.left[k - 2].wait_recv)
-        pl.when((at > 0) & (at <= ways - k))(self.left[k - 1].start)
+        if k != 2:
+            return
+        for copy, passes, _, needed in self.passed:
+
+            @pl.when(passes)
+            def _():
+                needed[0].wait_recv()
+                copy.start()
 
     def finish(self):
-        at, ways = self.at, self.ways
-        last = ways - 1
-        pl.when(at >= last)(self.right[last - 1].wait_recv)
-        pl.when(at <= 0)(self.left[last - 1].wait_recv)
-        for k in range(1, ways):
-            pl.when((at < ways - 1) & (at >= k - 1))(self.right[k - 1].wait_send)
-            pl.when((at > 0) & (at <= ways - k))(self.left[k - 1].wait_send)
+        waited = [passes for _, passes, _, _ in self.passed]
+        for number, (copy, sends, receives) in enumerate(self.direct):
+            if waited and number % 2 == 0:
+                receives = receives & jnp.logical_not(waited[number // 2])
+            pl.when(receives)(copy.wait_recv)
+            pl.when(sends)(copy.wait_send)
+        for copy, passes, receives, _ in self.passed:
+            pl.when(receives)(copy.wait_recv)
+            pl.when(passes)(copy.wait_send)
         self.own.wait()
 
 
@@ -485,13 +499,13 @@
     up("x")
     gather.wait_chip("y")
     up("y")
-    if ways > 1:
-        line.step(2)
     gather.relay_far()
     gather.wait_chip("far")
     keep_normed = pltpu.make_async_copy(gathered, normed_hbm, local.at[1])
     keep_normed.start()
     up("far")
+    if ways > 1:
+        line.step(2)
     keep_pre = pltpu.make_async_copy(pre, pre_hbm, local.at[2])
     keep_pre.start()
     down("far")
@@ -506,9 +520,6 @@
     scatter.send_pair("own")
     scatter.add_pair("y")
     scatter.add_pair("own")
-    if ways > 1:
-        for k in range(3, ways):
-            line.step(k)
     scatter.turn_corner()
     branch = scatter.total()
     branch_out[...] = branch
@@ -529,7 +540,7 @@
 
 
 def line_copies(ways):
-    return 2 * (ways - 1) if ways > 1 else 0
+    return 6 if ways > 1 else 0
 
 
 def sds(shape, dtype):
@@ -642,32 +653,31 @@
     project("x")
     gather.wait_chip("y")
     project("y")
-    if ways > 1:
-        line.step(2)
     gather.relay_far()
     gather.wait_chip("far")
     keep = [pltpu.make_async_copy(gathered, normed_hbm, local.at[1])]
     keep[0].start()
     project("far")
+    if ways > 1:
+        line.step(2)
     for number, (src, dst) in enumerate(((q, q_hbm), (k, k_hbm), (v, v_hbm))):
         keep.append(pltpu.make_async_copy(src, dst, local.at[2 + number]))
         keep[-1].start()
 
     def attend(name):
         b = chips[name][1]
+        span = pl.ds(pl.multiple_of(b * 2 * rows, 2 * rows), 2 * rows)
         for head in range(heads):
-            @pl.loop(0, 2)
-            def _(step):
-                at = b * 2 + step
-                span = pl.ds(pl.multiple_of(at * rows, rows), rows)
-                scores = dot_wide(q[head, span], k[head])
-                top = jnp.max(scores, -1, keepdims=True)
-                exponent = jnp.exp(scores - top)
-                total = jnp.sum(exponent, -1, keepdims=True)
-                out = dot(exponent.astype(BF), v[head]) / total
-                mixed[span, head * HEAD_DIM : (head + 1) * HEAD_DIM] = out.astype(BF)
-                wide = jnp.broadcast_to(top + jnp.log(total), (rows, rows))
-                lse[head, pl.ds(at, 1)] = wide.T[0:1]
+            scores = dot_wide(q[head, span], k[head])
+            top = jnp.max(scores, -1, keepdims=True)
+            exponent = jnp.exp(scores - top)
+            total = jnp.sum(exponent, -1, keepdims=True)
+            out = dot(exponent.astype(BF), v[head]) / total
+            mixed[span, head * HEAD_DIM : (head + 1) * HEAD_DIM] = out.astype(BF)
+            logs = top + jnp.log(total)
+            for half in range(2):
+                wide = jnp.broadcast_to(logs[half * rows : (half + 1) * rows], (rows, rows))
+                lse[head, pl.ds(b * 2 + half, 1)] = wide.T[0:1]
 
         @pl.loop(0, 2)
         def _(step):
@@ -677,8 +687,6 @@
 
     attend("y")
     scatter.send_pair("y")
-    if ways > 1:
-        line.step(3)
     attend("own")
     scatter.send_pair("own")
     scatter.send_far()
@@ -822,62 +830,80 @@
         self.ways, self.at, self.src = ways, lax.axis_index("shard"), src
         self.arrived, self.sums, self.total = arrived, sums, total
         self.rows = total.shape[0]
-        self.sem = send, recv, base
-        at, steps = self.at, ways - 1
-        self.sides = []
+        at = self.at
+
+        def hop(index, part, to):
+            return pltpu.make_async_remote_copy(
+                src_ref=part,
+                dst_ref=arrived.at[index],
+                send_sem=send.at[base + index],
+                recv_sem=recv.at[base + index],
+                device_id={"shard": jnp.clip(to, 0, ways - 1)},
+                device_id_type=MESH,
+            )
+
+        self.far, self.near, self.two, self.summed = [], [], [], []
+        for side, sign in ((0, 1), (1, -1)):
+            place_at = at if side == 0 else ways - 1 - at
+            first = 3 * side
+            passes = (place_at >= 1) & (place_at < ways - 2)
+            if ways > 3:
+                copy = hop(first + 2, self.block(at + 3 * sign), at + sign)
+                self.far.append((copy, place_at < ways - 3, passes))
+            copy = hop(first, self.block(at + sign), at + sign)
+            self.near.append((copy, place_at < ways - 1, place_at >= 1))
+            if ways > 2:
+                plain = place_at < ways - 2
+                if ways > 3:
+                    plain = plain & (place_at < 1)
+                    copy = hop(first + 1, sums.at[side], at + 2 * sign)
+                    self.summed.append((copy, passes, first + 2, at + 2 * sign))
+                copy = hop(first + 1, self.block(at + 2 * sign), at + 2 * sign)
+                self.two.append((copy, plain, place_at < ways - 2, place_at >= 2))
+
+    def block(self, number):
+        return self.src.at[pl.ds(jnp.clip(number, 0, self.ways - 1) * self.rows, self.rows)]
+
+    def step(self, k):
+        if k == 1:
+            for copy, sends, _ in self.far:
+                pl.when(sends)(copy.start)
+            for copy, sends, _, _ in self.two:
+                pl.when(sends)(copy.start)
+            for copy, sends, _ in self.near:
+                pl.when(sends)(copy.start)
+        if k == 2:
+            for side, (copy, sends, slot, owner) in enumerate(self.summed):
+
+                @pl.when(sends)
+                def _():
+                    self.far[side][0].wait_recv()
+                    mine = self.block(owner)[...].astype(F32)
+                    self.sums[side] = (mine + self.arrived[slot].astype(F32)).astype(BF)
+                    copy.start()
+
+    def finish(self):
+        self.total[...] = self.block(self.at)[...].astype(F32)
         for side in range(2):
-            place_at = at if side == 0 else ways - 1 - at
-            to = jnp.clip(at + 1 if side == 0 else at - 1, 0, ways - 1)
-            first, summed = [], []
-            for k in range(1, ways):
-                index = side * steps + k - 1
-                block = ways - k if side == 0 else k - 1
-                first.append(self.hop(index, self.block(block), to))
-                summed.append(self.hop(index, sums.at[index], to) if k > 1 else None)
-            self.sides.append((place_at, first, summed))
-
-    def block(self, number):
-        return self.src.at[pl.ds(number * self.rows, self.rows)]
-
-    def hop(self, index, src, to):
-        send, recv, base = self.sem
-        return pltpu.make_async_remote_copy(
-            src_ref=src,
-            dst_ref=self.arrived.at[index],
-            send_sem=send.at[base + index],
-            recv_sem=recv.at[base + index],
-            device_id={"shard": to},
-            device_id_type=MESH,
-        )
-
-    def step(self, k):
-        ways, at = self.ways, self.at
-        for side, (place_at, first, summed) in enumerate(self.sides):
-            pl.when(place_at == 0)(first[k - 1].start)
-            if k == 1:
-                continue
-            index = side * (ways - 1) + k - 1
-            block = at + ways - k if side == 0 else at - ways + k
-
-            @pl.when((place_at >= 1) & (place_at <= k - 1) & (place_at < ways - 1))
+            copy, _, receives = self.near[side]
+
+            @pl.when(receives)
             def _():
-                first[k - 2].wait_recv()
-                mine = self.block(jnp.clip(block, 0, ways - 1))[...].astype(F32)
-                self.sums[index] = (mine + self.arrived[index - 1].astype(F32)).astype(BF)
-                summed[k - 1].start()
-
-    def finish(self):
-        ways, at = self.ways, self.at
-        self.total[...] = self.block(at)[...].astype(F32)
-        for side, (place_at, first, summed) in enumerate(self.sides):
-            @pl.when(place_at >= 1)
-            def _():
-                first[ways - 2].wait_recv()
-                index = side * (ways - 1) + ways - 2
-                self.total[...] = self.total[...] + self.arrived[index].astype(F32)
-
-            for k in range(1, ways):
-                pl.when((place_at <= k - 1) & (place_at < ways - 1))(first[k - 1].wait_send)
+                copy.wait_recv()
+                self.total[...] = self.total[...] + self.arrived[3 * side].astype(F32)
+
+            if self.two:
+                pair, _, _, receives = self.two[side]
+
+                @pl.when(receives)
+                def _():
+                    pair.wait_recv()
+                    self.total[...] = self.total[...] + self.arrived[3 * side + 1].astype(F32)
+
+        for copy, sends, _ in self.far + self.near:
+            pl.when(sends)(copy.wait_send)
+        for copy, _, sends, _ in self.two:
+            pl.when(sends)(copy.wait_send)
 
 
 class Extra:
@@ -892,7 +918,7 @@
             self.line = LineScatter(
                 ways, refs["src"], refs["arrived"], refs["sums"], refs["total"], send, recv, base
             )
-            base = base + 2 * (ways - 1)
+            base = base + line_copies(ways)
         if swap_src is not None:
             ctx = lax.axis_index("ctx")
             self.swaps = [
@@ -947,11 +973,11 @@
         specs.append(VMEM)
         scratch += [
             pltpu.VMEM(grads.shape, BF),
-            pltpu.VMEM((2 * (ways - 1), rows, width), BF),
-            pltpu.VMEM((2 * (ways - 1), rows, width), BF),
+            pltpu.VMEM((line_copies(ways), rows, width), BF),
+            pltpu.VMEM((2, rows, width), BF),
             pltpu.VMEM((rows, width), F32),
         ]
-        copies += 2 * (ways - 1)
+        copies += line_copies(ways)
     if swaps:
         given += list(swaps)
         shape = (len(swaps), *swaps[0].shape)
@@ -1095,8 +1121,6 @@
     def _(at):
         dw[out_rows(at), :width] = dot_tall(wide_rows(normed, at), dpre[...]).astype(BF)
 
-    for k in range(3, ways):
-        extra.step(k)
     scatter.turn_corner()
 
     @pl.loop(0, model // tile)
@@ -1213,8 +1237,6 @@
         dq[:, head * HEAD_DIM : (head + 1) * HEAD_DIM] = dqh[head]
     for head in range(2 * heads):
         dkv[:, head * HEAD_DIM : (head + 1) * HEAD_DIM] = dk[head].astype(BF)
-    for step in range(3, ways):
-        extra.step(step)
 
     def span_of(name):
         a, b = scatter.chips[name]
@@ -1361,8 +1383,11 @@
     specs = [VMEM, VMEM, VMEM, ANY, ANY]
     outs += [sds(shard, BF)] * (before + hop) + [sds((2, *shard), BF)] * before
     specs += [VMEM] * (before + hop) + [ANY] * before
-    hops = pltpu.VMEM((line_copies(ways), *shard), BF)
-    line = [hops, hops, pltpu.VMEM(shard, F32)]
+    line = [
+        pltpu.VMEM((max(line_copies(ways), 1), *shard), BF),
+        pltpu.VMEM((2, *shard), BF),
+        pltpu.VMEM(shard, F32),
+    ]
 
     def buffers(copies, locals_used):
         return [
@@ -1508,6 +1533,8 @@
             held[number][stage] = both.astype(held[number].dtype)
             now[number] = held[number].at[stage]
         copies += here
+        if stage == 1:
+            extra.step(2)
     if has_block:
         line.step(2)
     base = count * stages
@@ -1531,7 +1558,6 @@
             waits.append(copy)
         if mode != "gather":
             far[number][at] = now[number][at] if mode == "scatter" else now[number][...]
-    extra.step(2)
     for k in range(3, ways):
         if has_block:
             line.step(k)
@@ -1636,6 +1662,48 @@
     return outs
 
 
+def loss_kernel(
+    loss_scale,
+    hidden_ref,
+    ends_ref,
+    head_ref,
+    target_ref,
+    weight_ref,
+    grad_out,
+    small_out,
+    head_out,
+    loss_out,
+):
+    hidden, head = hidden_ref[...], head_ref[...]
+    shift, scale = ends_ref[0:1, :], ends_ref[1:2, :]
+    centre, scale_by = norm_rows(hidden)
+    normed = (centre * scale_by * (1.0 + scale) + shift).astype(BF)
+    misfit = dot_wide(normed, head) - target_ref[...]
+    weighted = weight_ref[...] * misfit
+    rows = jnp.sum(weighted * misfit, 1, keepdims=True)
+    loss_out[...] = jnp.sum(rows, 0, keepdims=True) * loss_scale
+    grad_pred = (2.0 * loss_scale * weighted).astype(BF)
+    head_out[...] = dot_tall(grad_pred, normed)
+    grad_out[...] = jnp.zeros_like(grad_out)
+    modulate_backward(dot(grad_pred, head), hidden, scale, grad_out, small_out)
+
+
+def loss_and_grad(hidden, ends, head_rows, target, weight, loss_scale):
+    rows, model = hidden.shape
+    return pl.pallas_call(
+        functools.partial(loss_kernel, loss_scale),
+        out_shape=[
+            sds((rows, model), F32),
+            sds((2, model), F32),
+            sds(head_rows.shape, F32),
+            sds((1, 1), F32),
+        ],
+        in_specs=[VMEM] * 5,
+        out_specs=[VMEM] * 4,
+        name="loss_and_grad",
+    )(hidden, ends, head_rows, target, weight)
+
+
 def spread(values, at, axis_size):
     full = jnp.zeros((*values.shape[:-1], axis_size), values.dtype)
     return lax.dynamic_update_slice_in_dim(full, values, at, values.ndim - 1)
@@ -1742,7 +1810,6 @@
         1,
     )
     (end_mods,) = exchange([([spread(end_own, first_owned, D)], "scatter")], 13)
-    end_shift, end_scale = end_mods[0:1], end_mods[1:2]
 
     pieces = patchify(noised)[0]
     rows_here = noised.shape[2] // PATCH
@@ -1764,21 +1831,13 @@
         saved.append((kept_attention, kept_feed, (weights, feed_weights)))
         weights = following
 
-    final_normed = modulate(hidden, end_shift, end_scale).astype(jnp.bfloat16)
-    predicted = jnp.einsum(
-        "pd,cd->pc", final_normed, head_rows, preferred_element_type=jnp.float32
-    )
     target_rows = patchify(velocity)[0].astype(jnp.float32)
-    weighting = 0.5 + time_ids.astype(jnp.float32)[0] / STEPS
-    misfit = predicted - target_rows
+    weighting = 0.5 + time_ids.astype(jnp.float32)[:, None] / STEPS
     loss_scale = 1.0 / (shard_ways * PATCHES * PDIM)
-    loss_local = jnp.sum(weighting * misfit * misfit) * loss_scale
-    grad_pred = (2.0 * loss_scale * weighting * misfit).astype(jnp.bfloat16)
-    grad_head = jnp.einsum("pc,pd->cd", grad_pred, final_normed, preferred_element_type=jnp.float32)
-    grad_normed = jnp.dot(grad_pred, head_rows, preferred_element_type=jnp.float32)
-    grad_hidden, grad_end_shift, grad_end_scale = jax.vjp(modulate, hidden, end_shift, end_scale)[
-        1
-    ](grad_normed)
+    grad_hidden, grad_ends, grad_head, loss_local = loss_and_grad(
+        hidden, end_mods, head_rows, target_rows, weighting, loss_scale
+    )
+    loss_local = loss_local[0, 0]
 
     small = [None] * (2 * LAYERS)
     shards, others = [None] * (2 * LAYERS), [None] * (2 * LAYERS)
@@ -1821,7 +1880,7 @@
     pixel = jnp.concatenate([grad_patch, grad_head], 0).astype(jnp.bfloat16)
     pixel = pixel.reshape(2 * PDIM, shard_ways, -1).transpose(1, 0, 2)
     result = exchange(
-        [(small + [grad_end_shift, grad_end_scale], "gather"), ([pixel], "scatter")],
+        [(small + [grad_ends], "gather"), ([pixel], "scatter")],
         14,
         by_x=True,
         grads=grads,
@@ -1884,9 +1943,15 @@
         )
     shard_in, shard_out = jnp.stack(shard_in), jnp.stack(shard_out)
     shard_hidden = jnp.stack(shard_hidden).astype(jnp.float32)
+    flat_mod = grad_mod.reshape(latents, -1)
+    wide_own = gated_own.astype(jnp.float32)
+    modulation_square_sum = jnp.sum(
+        jnp.dot(wide_own, wide_own.T, precision=highest)
+        * jnp.dot(flat_mod, flat_mod.T, precision=highest)
+    )
     squares = (
         jnp.sum(shard_stem * shard_stem)
-        + jnp.sum(shard_modulation * shard_modulation)
+        + modulation_square_sum
         + jnp.sum(shard_in * shard_in)
         + jnp.sum(shard_out * shard_out)
         + jnp.sum(shard_hidden * shard_hidden)

time: 739 us -> 679 us (0.919)
  Pallas kernels: 593 us -> 534 us
  other arithmetic: 56.6 us -> 49.1 us
    pallas_call x4, Pallas kernels: 228 us -> 198 us  [layer_forward(): pl.pallas_call(functools.partial(layer_forward_kernel, ways, last), out_s...]
    pallas_call x4, Pallas kernels: 222 us -> 203 us  [layer_backward(): pl.pallas_call(functools.partial(layer_backward_kernel, ways, before), ou...]
    pallas_call x8, Pallas kernels: 143 us -> 130 us  [exchange(): pl.pallas_call(functools.partial(exchange_kernel, ways, tuple(modes), tup...]
    convert_element_type x5 -> x4, other arithmetic: 28.8 us -> 21.3 us  [adam_update(): return (master_new, first_new, second_new, master_new.astype(jnp.bfloat16))]
where the time goes in v3:
time: 679 us; the launch traced here: 672 us
  Pallas kernels  534 us (79%)
  other arithmetic  49.1 us (7%)
  local copies, waits for them, and re-layouts  47.3 us (7%)
  matrix products  33.3 us (5%)
  between operations  8.19 us (1%)
    pallas_call x4, Pallas kernels, layer_backward(): pl.pallas_call(functools.partial(layer_backward_kernel, ways, before), ou...  203 us
    pallas_call x4, Pallas kernels, layer_forward(): pl.pallas_call(functools.partial(layer_forward_kernel, ways, last), out_s...  198 us
    pallas_call x8, Pallas kernels, exchange(): pl.pallas_call(functools.partial(exchange_kernel, ways, tuple(modes), tup...  130 us
    convert_element_type x4, other arithmetic, adam_update(): return (master_new, first_new, second_new, master_new.astype(jnp.bfloat16))  21.3 us

profile of v3, /device:TPU:0, one launch (start us, length us, event | category | flops | bytes accessed | tf_op | source)
XLA Modules:
  0.0 672.2 jit_solution(9228740604397768577)
XLA Ops:
  0.7 1.9 convert_element_type.180
  5.8 2.3 copy.50
  10.2 8.6 %exchange.8 = f32[4,128]{1,0:T(4,128)} custom-call(f32[4,128]{1,0:T(4,128)} %pad.4.refs_0_), custom_call_target="tpu_custom_call" | custom-call | tf_op jit(solution)/shard_map/exchange/pallas_call | solution.py:1619
  24.0 20.7 %exchange.9 = (f32[36,768]{1,0:T(8,128)}, bf16[384,768]{1,0:T(8,128)(2,1)}) custom-call(bf16[36,768]{1,0:T(8,128)(2,1)} %dynamic_update_slice.9.refs_0_, bf16[96,768]{1,0:T(8,128)(2,1)} %get-tuple-element.299.refs_1_), custom_call_target="tpu_custom_call" | custom-call | tf_op jit(solution)/shard_map/exchange/pallas_call | solution.py:1619
  53.1 24.2 %exchange.10 = (f32[24,768]{1,0:T(8,128)}, f32[4,768]{1,0:T(4,128)}, bf16[384,768]{1,0:T(8,128)(2,1)}) custom-call(f32[4,24,768]{2,1,0:T(8,128)} %reshape.143.refs_0_, bf16[4,768]{1,0:T(4,128)(2,1)} %copy-done.50, bf16[96,768]{1,0:T(8,128)(2,1)} %get-tuple-element.298.refs_2_), custom_call_target="tpu_custom_call" | custom-call | tf_op jit(solution)/shard_map/exchange/pallas_call | solution.py:1619
  77.3 2.4 pad_maximum_fusion.2
  84.2 2.0 fusion.5.refs_0_.refs_7_
  89.8 50.3 %layer_forward.4 = (f32[128,768]{1,0:T(8,128)}, f32[128,768]{1,0:T(8,128)}, bf16[8,128,768]{2,1,0:T(8,128)(2,1)}, bf16[3,512,64]{2,1,0:T(8,128)(2,1)}, bf16[3,10...) custom-call(f32[128,768]{1,0:T(8,128)} %fusion.5.refs_0_.refs_7_, ...), custom_call_target="tpu_custom_call" | custom-call | tf_op jit(solution)/shard_map/layer_forward/pallas_call | solution.py:809
  140.1 2.3 pad_maximum_fusion.9
  142.4 49.4 %layer_forward.5 = (f32[128,768]{1,0:T(8,128)}, f32[128,768]{1,0:T(8,128)}, bf16[8,128,768]{2,1,0:T(8,128)(2,1)}, bf16[3,512,64]{2,1,0:T(8,128)(2,1)}, bf16[3,10...) custom-call(f32[128,768]{1,0:T(8,128)} %get-tuple-element.122.refs_0, ...), custom_call_target="tpu_custom_call" | custom-call | tf_op jit(solution)/shard_map/layer_forward/pallas_call | solution.py:809
  191.7 2.0 pad_maximum_fusion.10
  193.7 50.5 %layer_forward.6 = (f32[128,768]{1,0:T(8,128)}, f32[128,768]{1,0:T(8,128)}, bf16[8,128,768]{2,1,0:T(8,128)(2,1)}, bf16[3,512,64]{2,1,0:T(8,128)(2,1)}, bf16[3,10...) custom-call(f32[128,768]{1,0:T(8,128)} %get-tuple-element.124.refs_0, ...), custom_call_target="tpu_custom_call" | custom-call | tf_op jit(solution)/shard_map/layer_forward/pallas_call | solution.py:809
  244.3 47.9 %layer_forward.7 = (f32[128,768]{1,0:T(8,128)}, f32[128,768]{1,0:T(8,128)}, bf16[8,128,768]{2,1,0:T(8,128)(2,1)}, bf16[3,512,64]{2,1,0:T(8,128)(2,1)}, bf16[3,10...) custom-call(f32[128,768]{1,0:T(8,128)} %get-tuple-element.126.refs_0, ...), custom_call_target="tpu_custom_call" | custom-call | tf_op jit(solution)/shard_map/layer_forward/pallas_call | solution.py:809
  297.0 10.1 %exchange.11.ends_ref = f32[2,768]{1,0:T(2,128)} custom-call(f32[4,2,768]{2,1,0:T(2,128)} %dynamic_update_slice.11.refs_0_), custom_call_target="tpu_custom_call" | custom-call | tf_op jit(solution)/shard_map/exchange/pallas_call | solution.py:1619
  313.4 2.5 loss_and_grad.1
  315.9 47.7 %layer_backward.4 = (f32[128,768]{1,0:T(8,128)}, f32[3,768]{1,0:T(4,128)}, f32[3,768]{1,0:T(4,128)}, bf16[768,768]{1,0:T(8,128)(2,1)}, bf16[768,768]{1,0:T(8,128)(2,1)}, /*index=5*/bf16[192,768]{1,0:T(8,128)(2,1)}) custom-call(f32[128,768]{1,0:T(8,128)} %get-tuple-element.130.refs_0_, f32[6,768]{1,0:T(8,128)} %get-tuple-element.300.refs_1_, ...), custom_call_target="tpu_custom_call" | custom-call | tf_op jit(solution)/shard_map/layer_backward/pallas_call | solution.py:1433
  363.6 51.7 %layer_backward.5 = (f32[128,768]{1,0:T(8,128)}, f32[3,768]{1,0:T(4,128)}, f32[3,768]{1,0:T(4,128)}, bf16[768,768]{1,0:T(8,128)(2,1)}, bf16[768,768]{1,0:T(8,128...) custom-call(f32[128,768]{1,0:T(8,128)} %get-tuple-element.143.refs_0_, ...), custom_call_target="tpu_custom_call" | custom-call | tf_op jit(solution)/shard_map/layer_backward/pallas_call | solution.py:1433
  415.3 52.1 %layer_backward.6 = (f32[128,768]{1,0:T(8,128)}, f32[3,768]{1,0:T(4,128)}, f32[3,768]{1,0:T(4,128)}, bf16[768,768]{1,0:T(8,128)(2,1)}, bf16[768,768]{1,0:T(8,128...) custom-call(f32[128,768]{1,0:T(8,128)} %get-tuple-element.158.refs_0_, ...), custom_call_target="tpu_custom_call" | custom-call | tf_op jit(solution)/shard_map/layer_backward/pallas_call | solution.py:1433
  467.5 52.0 %layer_backward.7 = (f32[128,768]{1,0:T(8,128)}, f32[3,768]{1,0:T(4,128)}, f32[3,768]{1,0:T(4,128)}, bf16[768,768]{1,0:T(8,128)(2,1)}, bf16[768,768]{1,0:T(8,128...) custom-call(f32[128,768]{1,0:T(8,128)} %get-tuple-element.173.refs_0_, ...), custom_call_target="tpu_custom_call" | custom-call | tf_op jit(solution)/shard_map/layer_backward/pallas_call | solution.py:1433
  529.1 33.1 %exchange.12 = (f32[4,26,768]{2,1,0:T(8,128)}, f32[32,192]{1,0:T(8,128)}, bf16[192,768]{1,0:T(8,128)(2,1)}, bf16[1,192,768]{2,1,0:T(8,128)(2,1)}) custom-call(f32[3,768]{1,0:T(4,128)} %get-tuple-element.188.refs_0_, f32[3,768]{1,0:T(4,128)} %get-tuple-element.189.refs_1_, f32[3,768]{1,0:T(4,128)} %get-tuple-element.190.refs_2_, ...), custom_call_target="tpu_custom_call" | custom-call | tf_op jit(solution)/shard_map/exchange/pallas_call | solution.py:1619
  573.9 11.1 %exchange.13 = (f32[4,768]{1,0:T(4,128)}, bf16[1,192,768]{2,1,0:T(8,128)(2,1)}) custom-call(f32[4,768]{1,0:T(4,128)} %convolution_add_fusion.refs_0_, bf16[192,768]{1,0:T(8,128)(2,1)} %get-tuple-element.202.refs_1_), custom_call_target="tpu_custom_call" | custom-call | tf_op jit(solution)/shard_map/exchange/pallas_call | solution.py:1619
  591.2 2.0 fusion.15
  596.9 2.5 fusion.9
  602.9 10.6 %exchange.14 = f32[4,768]{1,0:T(4,128)} custom-call(f32[4,768]{1,0:T(4,128)} %fusion.28.refs_0_), custom_call_target="tpu_custom_call" | custom-call | tf_op jit(solution)/shard_map/exchange/pallas_call | solution.py:1619
  617.6 2.2 concatenate.105
  619.9 1.9 multiply_reduce_fusion.2
  626.2 11.9 %exchange.15 = f32[2,128]{1,0:T(2,128)} custom-call(f32[2,128]{1,0:T(2,128)} %mul.319.refs_0_), custom_call_target="tpu_custom_call" | custom-call | tf_op jit(solution)/shard_map/exchange/pallas_call | solution.py:1619
  640.2 12.4 %fusion.57 = (bf16[4,2,192,768]{3,2,1,0:T(8,128)(2,1)}, f32[4,2,192,768]{3,2,1,0:T(8,128)}, f32[4,2,192,768]{3,2,1,0:T(8,128)}, f32[4,2,192,768]{3,2,1,0:T(8,128)}) fusion(f32[4,2,192,768]{3,2,1,0:T(8,128)} %param.35, f32[]{:T(128)S(6)} %div.83, bf16[1,2,192,768]{3,2,1,0:T(8,128)(2,1)} %copy-done.14, bf16[1,2,192,768]{3,2,1,0:T(8,128)(2,1)} %copy-done.13, ...), kind=kLoop, calls=%fused_computation.196 | loop fusion | flops 23592960 | bytes 33030148 | tf_op jit(solution)/shard_map/convert_element_type | solution.py:100
  652.7 2.0 fusion.59
  655.9 5.0 fusion.61
  662.0 7.0 %fusion.63 = (bf16[4,48,4608]{2,1,0:T(8,128)(2,1)}, f32[4,48,4608]{2,1,0:T(8,128)}, f32[4,48,4608]{2,1,0:T(8,128)}, f32[4,48,4608]{2,1,0:T(8,128)}) fusion(f32[4,48,4608]{2,1,0:T(8,128)S(1)} %copy-done, f32[4,48,4608]{2,1,0:T(8,128)S(1)} %copy-done.61, f32[4,48,4608]{2,1,0:T(8,128)S(1)} %copy-done.62, f32[]{:T(128)S(6)} %div.83, ...), kind=kOutput, calls=%fused_computation.199 | convolution fusion | flops 56623104 | bytes 23298436 | tf_op jit(solution)/shard_map/bd,ble->lde/dot_general | solution.py:1922
  669.0 1.9 fusion.65
  (244 shorter events, 79.7 us)
Async XLA Ops:
  0.7 2.7 copy-start.15
  4.1 45.9 %copy-start = (f32[4,48,4608]{2,1,0:T(8,128)S(1)}, f32[4,48,4608]{2,1,0:T(8,128)}, u32[]{:S(2)}) copy-start(f32[4,48,4608]{2,1,0:T(8,128)} %param.26) | copy-start | bytes 10616836
  49.9 3.2 copy-start.51
  50.1 3.0 copy-start.50
  53.1 28.5 %copy-start.54 = (bf16[1,4,8,64]{3,2,1,0:T(8,128)(2,1)S(1)}, bf16[1,4,8,64]{3,2,1,0:T(8,128)(2,1)}, u32[]{:S(2)}) copy-start(bf16[1,4,8,64]{3,2,1,0:T(8,128)(2,1)} %param.19) | copy-start | bytes 12292
  467.4 52.0 %copy-start.49 = (bf16[128,16]{0,1:T(8,128)(2,1)S(1)}, bf16[128,16]{0,1:T(8,128)(2,1)}, u32[]{:S(2)}) copy-start(bf16[128,16]{0,1:T(8,128)(2,1)} %squeeze_reshape.4) | copy-start | bytes 12292
  563.6 3.0 copy-start.11
  589.1 6.0 copy-start.7
  595.1 18.4 %copy-start.58 = (bf16[4,128]{1,0:T(4,128)(2,1)S(1)}, bf16[4,128]{1,0:T(4,128)(2,1)}, u32[]{:S(2)}) copy-start(bf16[4,128]{1,0:T(4,128)(2,1)} %copy-done.57) | copy-start | bytes 3076
  595.1 18.4 %copy-start.60 = (bf16[4,128]{1,0:T(4,128)(2,1)S(1)}, bf16[4,128]{1,0:T(4,128)(2,1)}, u32[]{:S(2)}) copy-start(bf16[4,128]{1,0:T(4,128)(2,1)} %copy-done.59) | copy-start | bytes 3076
  595.1 20.1 %copy-start.56 = (s32[4]{0:T(128)S(1)}, s32[4]{0:T(128)}, u32[]{:S(2)}) copy-start(s32[4]{0:T(128)} %copy-done.55) | copy-start | bytes 52
  640.1 12.5 %copy-start.16 = (f32[4,192,192]{2,1,0:T(8,128)S(1)}, f32[4,192,192]{2,1,0:T(8,128)}, u32[]{:S(2)}) copy-start(f32[4,192,192]{2,1,0:T(8,128)} %param.32) | copy-start | bytes 1769476
  640.1 12.5 %copy-start.22 = (f32[1,192,192]{2,1,0:T(8,128)S(1)}, f32[1,192,192]{2,1,0:T(8,128)}, u32[]{:S(2)}) copy-start(f32[1,192,192]{2,1,0:T(8,128)} %copy-done.21) | copy-start | bytes 442372
  640.1 12.5 %copy-start.24 = (f32[1,192,192]{2,1,0:T(8,128)S(1)}, f32[1,192,192]{2,1,0:T(8,128)}, u32[]{:S(2)}) copy-start(f32[1,192,192]{2,1,0:T(8,128)} %copy-done.23) | copy-start | bytes 442372
  640.1 12.5 %copy-start.26 = (f32[1,192,192]{2,1,0:T(8,128)S(1)}, f32[1,192,192]{2,1,0:T(8,128)}, u32[]{:S(2)}) copy-start(f32[1,192,192]{2,1,0:T(8,128)} %copy-done.25) | copy-start | bytes 442372
  640.1 12.5 %copy-start.28 = (f32[1,192,192]{2,1,0:T(8,128)S(1)}, f32[1,192,192]{2,1,0:T(8,128)}, u32[]{:S(2)}) copy-start(f32[1,192,192]{2,1,0:T(8,128)} %copy-done.27) | copy-start | bytes 442372
  640.1 12.5 %copy-start.33 = (f32[4,192,192]{2,1,0:T(8,128)S(1)}, f32[4,192,192]{2,1,0:T(8,128)}, u32[]{:S(2)}) copy-start(f32[4,192,192]{2,1,0:T(8,128)} %param.33) | copy-start | bytes 1769476
  640.2 12.5 %copy-start.34 = (f32[4,192,192]{2,1,0:T(8,128)S(1)}, f32[4,192,192]{2,1,0:T(8,128)}, u32[]{:S(2)}) copy-start(f32[4,192,192]{2,1,0:T(8,128)} %param.34) | copy-start | bytes 1769476
  640.2 14.5 %copy-start.19 = (f32[4,3,192,192]{3,2,1,0:T(8,128)S(1)}, f32[4,3,192,192]{3,2,1,0:T(8,128)}, u32[]{:S(2)}) copy-start(f32[4,3,192,192]{3,2,1,0:T(8,128)} %param.30) | copy-start | bytes 5308420
  640.2 14.5 %copy-start.20 = (f32[4,3,192,192]{3,2,1,0:T(8,128)S(1)}, f32[4,3,192,192]{3,2,1,0:T(8,128)}, u32[]{:S(2)}) copy-start(f32[4,3,192,192]{3,2,1,0:T(8,128)} %param.31) | copy-start | bytes 5308420
  652.6 2.8 copy-start.4
  652.6 2.9 copy-start.6
  652.6 3.1 copy-start.8
  652.7 3.3 copy-start.10
  655.9 5.1 copy-start.29
  655.9 5.1 copy-start.53
  655.9 5.1 copy-start.61
  655.9 6.0 copy-start.62
  661.9 7.0 %copy-start.2 = (f32[3592,48]{0,1:T(8,128)S(1)}, f32[3592,48]{0,1:T(8,128)}, u32[]{:S(2)}) copy-start(f32[3592,48]{0,1:T(8,128)} %concatenate.105) | copy-start | bytes 2068996
  661.9 7.0 %copy-start.17 = (f32[3592,48]{0,1:T(8,128)S(1)}, f32[3592,48]{0,1:T(8,128)}, u32[]{:S(2)}) copy-start(f32[3592,48]{0,1:T(8,128)} %param.23) | copy-start | bytes 2068996
  661.9 7.0 %copy-start.35 = (f32[3592,48]{0,1:T(8,128)S(1)}, f32[3592,48]{0,1:T(8,128)}, u32[]{:S(2)}) copy-start(f32[3592,48]{0,1:T(8,128)} %param.24) | copy-start | bytes 2068996
  661.9 7.0 %copy-start.36 = (f32[3592,48]{0,1:T(8,128)S(1)}, f32[3592,48]{0,1:T(8,128)}, u32[]{:S(2)}) copy-start(f32[3592,48]{0,1:T(8,128)} %param.25) | copy-start | bytes 2068996
  (31 other events, 45.0 us)

commit v4 on v3

--- a/solution.py
+++ b/solution.py
@@ -1664,9 +1664,10 @@
 
 def loss_kernel(
     loss_scale,
+    first_head,
     hidden_ref,
     ends_ref,
-    head_ref,
+    packed_ref,
     target_ref,
     weight_ref,
     grad_out,
@@ -1674,7 +1675,7 @@
     head_out,
     loss_out,
 ):
-    hidden, head = hidden_ref[...], head_ref[...]
+    hidden, head = hidden_ref[...], packed_ref[first_head : first_head + PDIM, :].astype(BF)
     shift, scale = ends_ref[0:1, :], ends_ref[1:2, :]
     centre, scale_by = norm_rows(hidden)
     normed = (centre * scale_by * (1.0 + scale) + shift).astype(BF)
@@ -1688,20 +1689,20 @@
     modulate_backward(dot(grad_pred, head), hidden, scale, grad_out, small_out)
 
 
-def loss_and_grad(hidden, ends, head_rows, target, weight, loss_scale):
+def loss_and_grad(hidden, ends, packed, first_head, target, weight, loss_scale):
     rows, model = hidden.shape
     return pl.pallas_call(
-        functools.partial(loss_kernel, loss_scale),
+        functools.partial(loss_kernel, loss_scale, first_head),
         out_shape=[
             sds((rows, model), F32),
             sds((2, model), F32),
-            sds(head_rows.shape, F32),
+            sds((PDIM, model), F32),
             sds((1, 1), F32),
         ],
         in_specs=[VMEM] * 5,
         out_specs=[VMEM] * 4,
         name="loss_and_grad",
-    )(hidden, ends, head_rows, target, weight)
+    )(hidden, ends, packed, target, weight)
 
 
 def spread(values, at, axis_size):
@@ -1776,9 +1777,10 @@
     exchanged = exchange(
         [([spread(to_send, first_owned, D)], "sum")], 11, block=own_blocks[0][:half_rows]
     )
-    packed = exchanged[0].astype(jnp.bfloat16)
+    packed_wide = exchanged[0]
+    packed = packed_wide.astype(jnp.bfloat16)
     time_hidden = packed[:latents]
-    patch_in, head_rows = packed[latents : latents + PDIM], packed[latents + PDIM :]
+    patch_in = packed[latents : latents + PDIM]
     onehot = (all_labels[:, None] == jnp.arange(CLASSES)[None, :]).astype(jnp.bfloat16)
     condition = jnp.dot(time_hidden, time_out_own, preferred_element_type=jnp.float32) + jnp.dot(
         onehot, class_own, preferred_element_type=jnp.float32
@@ -1835,9 +1837,8 @@
     weighting = 0.5 + time_ids.astype(jnp.float32)[:, None] / STEPS
     loss_scale = 1.0 / (shard_ways * PATCHES * PDIM)
     grad_hidden, grad_ends, grad_head, loss_local = loss_and_grad(
-        hidden, end_mods, head_rows, target_rows, weighting, loss_scale
-    )
-    loss_local = loss_local[0, 0]
+        hidden, end_mods, packed_wide, latents + PDIM, target_rows, weighting, loss_scale
+    )
 
     small = [None] * (2 * LAYERS)
     shards, others = [None] * (2 * LAYERS), [None] * (2 * LAYERS)
@@ -1877,18 +1878,18 @@
     grad_embed = grad_hidden.astype(jnp.bfloat16)
     grad_patch = jnp.einsum("pf,pd->fd", pieces, grad_embed, preferred_element_type=jnp.float32)
 
-    pixel = jnp.concatenate([grad_patch, grad_head], 0).astype(jnp.bfloat16)
-    pixel = pixel.reshape(2 * PDIM, shard_ways, -1).transpose(1, 0, 2)
+    pixel = [grad_patch.astype(jnp.bfloat16), grad_head.astype(jnp.bfloat16)]
+    loss_row = loss_local[0, 0] * jnp.ones((1, 128), jnp.float32)
     result = exchange(
-        [(small + [grad_ends], "gather"), ([pixel], "scatter")],
+        [(small + [grad_ends], "gather"), (pixel, "sum"), ([loss_row], "sum")],
         14,
         by_x=True,
         grads=grads,
         swaps=[shards[1]],
     )
-    small, pixel = result[0], result[1]
+    small, pixel, train_loss = result[0], result[1], result[2][0, 0]
     if hops:
-        shards[0], others[1] = result[2], result[3][0]
+        shards[0], others[1] = result[3], result[4][0]
     grad_mod = small[:, : 6 * LAYERS].reshape(latents, LAYERS, 6 * D)
     grad_ends = small[:, 6 * LAYERS :]
     ends_here = own_columns(grad_ends)
@@ -1907,7 +1908,7 @@
     grad_time_hidden = own_columns(grad_time_hidden)
     grad_time_pre = grad_time_hidden * silu_grad(time_pre)
     gated_wide = gated.astype(jnp.float32)
-    grad_ends_own = lax.dynamic_slice_in_dim(pixel, own_tp * owned, owned, 1)
+    grad_ends_own = own_columns(pixel)
     shard_stem = jnp.concatenate(
         [
             jnp.dot(onehot.astype(jnp.float32).T, grad_condition, precision=highest),
@@ -1956,10 +1957,8 @@
         + jnp.sum(shard_out * shard_out)
         + jnp.sum(shard_hidden * shard_hidden)
     )
-    squares = jnp.where(own_ctx == 0, squares, jnp.zeros((), jnp.float32))
-    sums = jnp.stack([squares, loss_local])[:, None] * jnp.ones((1, 128), jnp.float32)
-    (sums,) = exchange([([sums], "sum")], 17, by_x=True)
-    square_total, train_loss = sums[0, 0], sums[1, 0]
+    (sums,) = exchange([([squares * jnp.ones((1, 128), jnp.float32)], "sum")], 17)
+    square_total = sums[0, 0]
     total_norm = jnp.sqrt(square_total)
     factor = clip_level / jnp.maximum(total_norm, clip_level)
     stem_out = adam_update(stem, stem_mean, stem_square, shard_stem, factor)

time: 679 us -> 670 us (0.987)
  no operation moved by 1% of the time
where the time goes in v4:
time: 670 us; the launch traced here: 664 us
  Pallas kernels  534 us (80%)
  other arithmetic  47 us (7%)
  local copies, waits for them, and re-layouts  40.6 us (6%)
  matrix products  33.3 us (5%)
  between operations  9.62 us (1%)
    pallas_call x4, Pallas kernels, layer_backward(): pl.pallas_call(functools.partial(layer_backward_kernel, ways, before), ou...  203 us
    pallas_call x4, Pallas kernels, layer_forward(): pl.pallas_call(functools.partial(layer_forward_kernel, ways, last), out_s...  198 us
    pallas_call x8, Pallas kernels, exchange(): pl.pallas_call(functools.partial(exchange_kernel, ways, tuple(modes), tup...  130 us
    convert_element_type x4, other arithmetic, adam_update(): return (master_new, first_new, second_new, master_new.astype(jnp.bfloat16))  21.3 us

profile of v4, /device:TPU:0, one launch (start us, length us, event | category | flops | bytes accessed | tf_op | source)
XLA Modules:
  0.0 664.3 jit_solution(1359778205210386900)
XLA Ops:
  5.8 2.3 copy.50
  10.2 8.6 %exchange.8 = f32[4,128]{1,0:T(4,128)} custom-call(f32[4,128]{1,0:T(4,128)} %pad.4.refs_0_), custom_call_target="tpu_custom_call" | custom-call | tf_op jit(solution)/shard_map/exchange/pallas_call | solution.py:1619
  24.0 20.7 %exchange.9 = (f32[36,768]{1,0:T(8,128)}, bf16[384,768]{1,0:T(8,128)(2,1)}) custom-call(bf16[36,768]{1,0:T(8,128)(2,1)} %dynamic_update_slice.9.refs_0_, bf16[96,768]{1,0:T(8,128)(2,1)} %get-tuple-element.301.refs_1_), custom_call_target="tpu_custom_call" | custom-call | tf_op jit(solution)/shard_map/exchange/pallas_call | solution.py:1619
  53.1 24.2 %exchange.10 = (f32[24,768]{1,0:T(8,128)}, f32[4,768]{1,0:T(4,128)}, bf16[384,768]{1,0:T(8,128)(2,1)}) custom-call(f32[4,24,768]{2,1,0:T(8,128)} %reshape.137.refs_0_, bf16[4,768]{1,0:T(4,128)(2,1)} %copy-done.50, bf16[96,768]{1,0:T(8,128)(2,1)} %get-tuple-element.300.refs_2_), custom_call_target="tpu_custom_call" | custom-call | tf_op jit(solution)/shard_map/exchange/pallas_call | solution.py:1619
  77.3 2.4 pad_maximum_fusion.2
  84.2 2.0 fusion.5.refs_0_.refs_7_
  89.8 50.3 %layer_forward.4 = (f32[128,768]{1,0:T(8,128)}, f32[128,768]{1,0:T(8,128)}, bf16[8,128,768]{2,1,0:T(8,128)(2,1)}, bf16[3,512,64]{2,1,0:T(8,128)(2,1)}, bf16[3,10...) custom-call(f32[128,768]{1,0:T(8,128)} %fusion.5.refs_0_.refs_7_, ...), custom_call_target="tpu_custom_call" | custom-call | tf_op jit(solution)/shard_map/layer_forward/pallas_call | solution.py:809
  140.1 2.3 pad_maximum_fusion.9
  142.3 49.4 %layer_forward.5 = (f32[128,768]{1,0:T(8,128)}, f32[128,768]{1,0:T(8,128)}, bf16[8,128,768]{2,1,0:T(8,128)(2,1)}, bf16[3,512,64]{2,1,0:T(8,128)(2,1)}, bf16[3,10...) custom-call(f32[128,768]{1,0:T(8,128)} %get-tuple-element.123.refs_0, ...), custom_call_target="tpu_custom_call" | custom-call | tf_op jit(solution)/shard_map/layer_forward/pallas_call | solution.py:809
  191.7 2.0 pad_maximum_fusion.10
  193.7 50.3 %layer_forward.6 = (f32[128,768]{1,0:T(8,128)}, f32[128,768]{1,0:T(8,128)}, bf16[8,128,768]{2,1,0:T(8,128)(2,1)}, bf16[3,512,64]{2,1,0:T(8,128)(2,1)}, bf16[3,10...) custom-call(f32[128,768]{1,0:T(8,128)} %get-tuple-element.125.refs_0, ...), custom_call_target="tpu_custom_call" | custom-call | tf_op jit(solution)/shard_map/layer_forward/pallas_call | solution.py:809
  244.0 47.9 %layer_forward.7 = (f32[128,768]{1,0:T(8,128)}, f32[128,768]{1,0:T(8,128)}, bf16[8,128,768]{2,1,0:T(8,128)(2,1)}, bf16[3,512,64]{2,1,0:T(8,128)(2,1)}, bf16[3,10...) custom-call(f32[128,768]{1,0:T(8,128)} %get-tuple-element.127.refs_0, ...), custom_call_target="tpu_custom_call" | custom-call | tf_op jit(solution)/shard_map/layer_forward/pallas_call | solution.py:809
  296.8 10.1 %exchange.11.ends_ref = f32[2,768]{1,0:T(2,128)} custom-call(f32[4,2,768]{2,1,0:T(2,128)} %dynamic_update_slice.11.refs_0_), custom_call_target="tpu_custom_call" | custom-call | tf_op jit(solution)/shard_map/exchange/pallas_call | solution.py:1619
  311.7 2.6 loss_and_grad.1
  314.3 48.0 %layer_backward.4 = (f32[128,768]{1,0:T(8,128)}, f32[3,768]{1,0:T(4,128)}, f32[3,768]{1,0:T(4,128)}, bf16[768,768]{1,0:T(8,128)(2,1)}, bf16[768,768]{1,0:T(8,128)(2,1)}, /*index=5*/bf16[192,768]{1,0:T(8,128)(2,1)}) custom-call(f32[128,768]{1,0:T(8,128)} %get-tuple-element.131.refs_0_, f32[6,768]{1,0:T(8,128)} %get-tuple-element.302.refs_1_, ...), custom_call_target="tpu_custom_call" | custom-call | tf_op jit(solution)/shard_map/layer_backward/pallas_call | solution.py:1433
  362.3 51.5 %layer_backward.5 = (f32[128,768]{1,0:T(8,128)}, f32[3,768]{1,0:T(4,128)}, f32[3,768]{1,0:T(4,128)}, bf16[768,768]{1,0:T(8,128)(2,1)}, bf16[768,768]{1,0:T(8,128...) custom-call(f32[128,768]{1,0:T(8,128)} %get-tuple-element.144.refs_0_, ...), custom_call_target="tpu_custom_call" | custom-call | tf_op jit(solution)/shard_map/layer_backward/pallas_call | solution.py:1433
  413.8 52.2 %layer_backward.6 = (f32[128,768]{1,0:T(8,128)}, f32[3,768]{1,0:T(4,128)}, f32[3,768]{1,0:T(4,128)}, bf16[768,768]{1,0:T(8,128)(2,1)}, bf16[768,768]{1,0:T(8,128...) custom-call(f32[128,768]{1,0:T(8,128)} %get-tuple-element.159.refs_0_, ...), custom_call_target="tpu_custom_call" | custom-call | tf_op jit(solution)/shard_map/layer_backward/pallas_call | solution.py:1433
  466.0 51.8 %layer_backward.7 = (f32[128,768]{1,0:T(8,128)}, f32[3,768]{1,0:T(4,128)}, f32[3,768]{1,0:T(4,128)}, bf16[768,768]{1,0:T(8,128)(2,1)}, bf16[768,768]{1,0:T(8,128...) custom-call(f32[128,768]{1,0:T(8,128)} %get-tuple-element.174.refs_0_, ...), custom_call_target="tpu_custom_call" | custom-call | tf_op jit(solution)/shard_map/layer_backward/pallas_call | solution.py:1433
  522.1 36.2 %exchange.12 = (f32[4,26,768]{2,1,0:T(8,128)}, f32[32,768]{1,0:T(8,128)}, f32[1,128]{1,0:T(1,128)}, bf16[192,768]{1,0:T(8,128)(2,1)}, bf16[1,192,768]{2,1,0:T(8,128)(2,1)}) custom-call(f32[3,768]{1,0:T(4,128)} %get-tuple-element.189.refs_0_, f32[3,768]{1,0:T(4,128)} %get-tuple-element.190.refs_1_, f32[3,768]{1,0:T(4,128)} %get-tuple-element.191.refs_2_, ...), custom_call_target="tpu_custom_call" | custom-call | tf_op jit(solution)/shard_map/exchange/pallas_call | solution.py:1619
  562.8 1.9 fusion.1
  570.1 10.9 %exchange.13 = (f32[4,768]{1,0:T(4,128)}, bf16[1,192,768]{2,1,0:T(8,128)(2,1)}) custom-call(f32[4,768]{1,0:T(4,128)} %convolution_add_fusion.refs_0_, bf16[192,768]{1,0:T(8,128)(2,1)} %get-tuple-element.205.refs_1_), custom_call_target="tpu_custom_call" | custom-call | tf_op jit(solution)/shard_map/exchange/pallas_call | solution.py:1619
  587.2 2.1 fusion.15
  593.0 2.5 fusion.9
  599.0 10.8 %exchange.14 = f32[4,768]{1,0:T(4,128)} custom-call(f32[4,768]{1,0:T(4,128)} %fusion.28.refs_0_), custom_call_target="tpu_custom_call" | custom-call | tf_op jit(solution)/shard_map/exchange/pallas_call | solution.py:1619
  614.0 2.2 concatenate.93
  616.2 1.9 multiply_reduce_fusion.2
  621.9 8.3 %exchange.15 = f32[1,128]{1,0:T(1,128)} custom-call(f32[1,128]{1,0:T(1,128)} %mul.317.refs_0_), custom_call_target="tpu_custom_call" | custom-call | tf_op jit(solution)/shard_map/exchange/pallas_call | solution.py:1619
  631.1 12.4 %fusion.57 = (bf16[4,2,192,768]{3,2,1,0:T(8,128)(2,1)}, f32[4,2,192,768]{3,2,1,0:T(8,128)}, f32[4,2,192,768]{3,2,1,0:T(8,128)}, f32[4,2,192,768]{3,2,1,0:T(8,128)}) fusion(f32[4,2,192,768]{3,2,1,0:T(8,128)} %param.35, f32[]{:T(128)S(6)} %div.83, bf16[1,2,192,768]{3,2,1,0:T(8,128)(2,1)} %copy-done.14, bf16[1,2,192,768]{3,2,1,0:T(8,128)(2,1)} %copy-done.13, ...), kind=kLoop, calls=%fused_computation.194 | loop fusion | flops 23592960 | bytes 33030148 | tf_op jit(solution)/shard_map/convert_element_type | solution.py:100
  643.6 2.0 fusion.59
  646.8 5.0 fusion.61
  652.8 7.0 %fusion.63 = (bf16[4,48,4608]{2,1,0:T(8,128)(2,1)}, f32[4,48,4608]{2,1,0:T(8,128)}, f32[4,48,4608]{2,1,0:T(8,128)}, f32[4,48,4608]{2,1,0:T(8,128)}) fusion(f32[4,48,4608]{2,1,0:T(8,128)S(1)} %copy-done, f32[4,48,4608]{2,1,0:T(8,128)S(1)} %copy-done.61, f32[4,48,4608]{2,1,0:T(8,128)S(1)} %copy-done.62, f32[]{:T(128)S(6)} %div.83, ...), kind=kOutput, calls=%fused_computation.197 | convolution fusion | flops 56623104 | bytes 23298436 | tf_op jit(solution)/shard_map/bd,ble->lde/dot_general | solution.py:1923
  659.9 1.9 fusion.65
  (239 shorter events, 71.0 us)
Async XLA Ops:
  0.7 2.7 copy-start.15
  4.1 45.9 %copy-start = (f32[4,48,4608]{2,1,0:T(8,128)S(1)}, f32[4,48,4608]{2,1,0:T(8,128)}, u32[]{:S(2)}) copy-start(f32[4,48,4608]{2,1,0:T(8,128)} %param.26) | copy-start | bytes 10616836
  49.9 3.2 copy-start.51
  50.1 3.0 copy-start.50
  53.1 28.5 %copy-start.54 = (bf16[1,4,8,64]{3,2,1,0:T(8,128)(2,1)S(1)}, bf16[1,4,8,64]{3,2,1,0:T(8,128)(2,1)}, u32[]{:S(2)}) copy-start(bf16[1,4,8,64]{3,2,1,0:T(8,128)(2,1)} %param.19) | copy-start | bytes 12292
  466.0 51.8 %copy-start.49 = (bf16[128,16]{0,1:T(8,128)(2,1)S(1)}, bf16[128,16]{0,1:T(8,128)(2,1)}, u32[]{:S(2)}) copy-start(bf16[128,16]{0,1:T(8,128)(2,1)} %squeeze_reshape.4) | copy-start | bytes 12292
  559.8 3.0 copy-start.11
  585.2 6.0 copy-start.7
  591.2 18.7 %copy-start.58 = (bf16[4,128]{1,0:T(4,128)(2,1)S(1)}, bf16[4,128]{1,0:T(4,128)(2,1)}, u32[]{:S(2)}) copy-start(bf16[4,128]{1,0:T(4,128)(2,1)} %copy-done.57) | copy-start | bytes 3076
  591.2 18.7 %copy-start.60 = (bf16[4,128]{1,0:T(4,128)(2,1)S(1)}, bf16[4,128]{1,0:T(4,128)(2,1)}, u32[]{:S(2)}) copy-start(bf16[4,128]{1,0:T(4,128)(2,1)} %copy-done.59) | copy-start | bytes 3076
  591.2 20.3 %copy-start.56 = (s32[4]{0:T(128)S(1)}, s32[4]{0:T(128)}, u32[]{:S(2)}) copy-start(s32[4]{0:T(128)} %copy-done.55) | copy-start | bytes 52
  631.0 12.5 %copy-start.16 = (f32[4,192,192]{2,1,0:T(8,128)S(1)}, f32[4,192,192]{2,1,0:T(8,128)}, u32[]{:S(2)}) copy-start(f32[4,192,192]{2,1,0:T(8,128)} %param.32) | copy-start | bytes 1769476
  631.0 12.5 %copy-start.22 = (f32[1,192,192]{2,1,0:T(8,128)S(1)}, f32[1,192,192]{2,1,0:T(8,128)}, u32[]{:S(2)}) copy-start(f32[1,192,192]{2,1,0:T(8,128)} %copy-done.21) | copy-start | bytes 442372
  631.0 12.5 %copy-start.24 = (f32[1,192,192]{2,1,0:T(8,128)S(1)}, f32[1,192,192]{2,1,0:T(8,128)}, u32[]{:S(2)}) copy-start(f32[1,192,192]{2,1,0:T(8,128)} %copy-done.23) | copy-start | bytes 442372
  631.0 12.5 %copy-start.26 = (f32[1,192,192]{2,1,0:T(8,128)S(1)}, f32[1,192,192]{2,1,0:T(8,128)}, u32[]{:S(2)}) copy-start(f32[1,192,192]{2,1,0:T(8,128)} %copy-done.25) | copy-start | bytes 442372
  631.0 12.5 %copy-start.28 = (f32[1,192,192]{2,1,0:T(8,128)S(1)}, f32[1,192,192]{2,1,0:T(8,128)}, u32[]{:S(2)}) copy-start(f32[1,192,192]{2,1,0:T(8,128)} %copy-done.27) | copy-start | bytes 442372
  631.0 12.5 %copy-start.33 = (f32[4,192,192]{2,1,0:T(8,128)S(1)}, f32[4,192,192]{2,1,0:T(8,128)}, u32[]{:S(2)}) copy-start(f32[4,192,192]{2,1,0:T(8,128)} %param.33) | copy-start | bytes 1769476
  631.0 12.5 %copy-start.34 = (f32[4,192,192]{2,1,0:T(8,128)S(1)}, f32[4,192,192]{2,1,0:T(8,128)}, u32[]{:S(2)}) copy-start(f32[4,192,192]{2,1,0:T(8,128)} %param.34) | copy-start | bytes 1769476
  631.1 14.5 %copy-start.19 = (f32[4,3,192,192]{3,2,1,0:T(8,128)S(1)}, f32[4,3,192,192]{3,2,1,0:T(8,128)}, u32[]{:S(2)}) copy-start(f32[4,3,192,192]{3,2,1,0:T(8,128)} %param.30) | copy-start | bytes 5308420
  631.1 14.5 %copy-start.20 = (f32[4,3,192,192]{3,2,1,0:T(8,128)S(1)}, f32[4,3,192,192]{3,2,1,0:T(8,128)}, u32[]{:S(2)}) copy-start(f32[4,3,192,192]{3,2,1,0:T(8,128)} %param.31) | copy-start | bytes 5308420
  643.5 2.8 copy-start.4
  643.5 2.9 copy-start.6
  643.5 3.1 copy-start.8
  643.6 3.3 copy-start.10
  646.8 5.1 copy-start.29
  646.8 5.1 copy-start.53
  646.8 5.1 copy-start.61
  646.8 6.0 copy-start.62
  652.8 7.0 %copy-start.2 = (f32[3592,48]{0,1:T(8,128)S(1)}, f32[3592,48]{0,1:T(8,128)}, u32[]{:S(2)}) copy-start(f32[3592,48]{0,1:T(8,128)} %concatenate.93) | copy-start | bytes 2068996
  652.8 7.0 %copy-start.17 = (f32[3592,48]{0,1:T(8,128)S(1)}, f32[3592,48]{0,1:T(8,128)}, u32[]{:S(2)}) copy-start(f32[3592,48]{0,1:T(8,128)} %param.23) | copy-start | bytes 2068996
  652.8 7.0 %copy-start.35 = (f32[3592,48]{0,1:T(8,128)S(1)}, f32[3592,48]{0,1:T(8,128)}, u32[]{:S(2)}) copy-start(f32[3592,48]{0,1:T(8,128)} %param.24) | copy-start | bytes 2068996
  652.8 7.0 %copy-start.36 = (f32[3592,48]{0,1:T(8,128)S(1)}, f32[3592,48]{0,1:T(8,128)}, u32[]{:S(2)}) copy-start(f32[3592,48]{0,1:T(8,128)} %param.25) | copy-start | bytes 2068996
  (32 other events, 46.3 us)
